TPU v7x, 32 devices: a whole 2x2x4 slice. The times are simulated.
32 devices in a mesh: gr: 8 (over y, x, core), gc: 4 (over z).
Axes of the slice: x: 2, y: 2, z: 4, core: 2. Of those that a mesh axis runs over, the one named last changes fastest.
Arguments:
- returns: bfloat16 [4096, 8192], P(('gr', 'gc')), may hold values from -6 to 6
- start_seed: int32 [8192, 64], replicated, may hold values from -1000 to 999
Outputs:
- loadings: float32 [8192, 64], P('gr')
- strengths: float32 [3, 64], replicated
All inputs are finite; a program needn't handle non-finite values.
Results may differ from a plain program's by a relative error of at most 0.0003.
Values may be sent and summed in bfloat16 or wider, within the bound.
No kernel may reach another device: no remote copies, remote signals or barrier semaphores. Data moves between devices by JAX's collectives and lax.ppermute only.
A program may use at most 128 MiB of HBM per device.

v0:
```python
import functools
import math

import jax
import jax.numpy as jnp
from jax import lax
from jax.experimental import pallas as pl
from jax.experimental.pallas import tpu as pltpu
from jax.sharding import PartitionSpec as P

ITERS = 3
LANES = 128
GROUP = 8
CUT = 4
HIGH = lax.Precision.HIGHEST
F32 = jnp.float32
BF16 = jnp.bfloat16


def vmem(count):
    return [pl.BlockSpec(memory_space=pltpu.VMEM)] * count


def smem():
    return [pl.BlockSpec(memory_space=pltpu.SMEM)]


def call(body, outs, scalars, arrays, flops, scratch=()):
    in_specs = smem() * len(scalars) + vmem(len(arrays))
    moved = sum(math.prod(o[0]) * 4 for o in outs)
    return pl.pallas_call(
        body,
        out_shape=[jax.ShapeDtypeStruct(shape, dtype) for shape, dtype in outs],
        in_specs=in_specs,
        out_specs=vmem(len(outs)),
        scratch_shapes=list(scratch),
        cost_estimate=pl.CostEstimate(flops=flops, bytes_accessed=moved, transcendentals=0),
        compiler_params=pltpu.CompilerParams(vmem_limit_bytes=40 * 1024 * 1024),
    )(*scalars, *arrays)


def thirds(x):
    top = x.astype(BF16)
    rest = x - top.astype(F32)
    mid = rest.astype(BF16)
    low = (rest - mid.astype(F32)).astype(BF16)
    return top, mid, low


def fold(tall, rows):
    return tall[2 * rows :] + tall[rows : 2 * rows] + tall[:rows]


def deal_body(returns_ref, out_ref, sems):
    blocks, _, width = out_ref.shape
    span = returns_ref.shape[1] // blocks
    copies = [
        pltpu.make_async_copy(returns_ref.at[:, b * span : b * span + width], out_ref.at[b], sems.at[b])
        for b in range(blocks)
    ]
    for copy in copies:
        copy.start()
    for copy in copies:
        copy.wait()


def deal(returns, blocks, width):
    return pl.pallas_call(
        deal_body,
        out_shape=jax.ShapeDtypeStruct((blocks, returns.shape[0], width), returns.dtype),
        in_specs=[pl.BlockSpec(memory_space=pl.ANY)],
        out_specs=pl.BlockSpec(memory_space=pltpu.VMEM),
        scratch_shapes=[pltpu.SemaphoreType.DMA((blocks,))],
    )(returns)


def project_first_body(span, me_ref, returns_ref, seed_ref, out_ref, *pieces):
    factors = out_ref.shape[0]
    for mask, piece in enumerate(pieces):
        width = piece.shape[1]
        at = pl.multiple_of((me_ref[0] ^ mask) * span + span - width, LANES)
        piece[...] = returns_ref[:, pl.ds(at, width)]
    seed = seed_ref[...]
    coarse = (seed >> 3) << 3
    fine = seed - coarse
    both = jnp.concatenate([coarse.astype(F32).astype(BF16), fine.astype(F32).astype(BF16)], axis=0)
    tall = lax.dot_general(both, returns_ref[...], (((1,), (1,)), ((), ())), preferred_element_type=F32)
    out_ref[...] = (tall[:factors] + tall[factors:]) / 1000.0


def halves(par_ref, full_ref, keep_ref, send_ref):
    rows = keep_ref.shape[0]
    at = pl.multiple_of(par_ref[0] * rows, 8)
    other = pl.multiple_of((1 - par_ref[0]) * rows, 8)
    keep_ref[...] = full_ref[pl.ds(at, rows), :]
    send_ref[...] = full_ref[pl.ds(other, rows), :]


def joined(par_ref, mine_ref, theirs_ref, full_ref):
    rows = mine_ref.shape[0]
    at = pl.multiple_of(par_ref[0] * rows, 8)
    other = pl.multiple_of((1 - par_ref[0]) * rows, 8)
    full_ref[pl.ds(at, rows), :] = mine_ref[...]
    full_ref[pl.ds(other, rows), :] = theirs_ref[...]


def lane_halves(par_ref, full_ref, keep_ref, send_ref):
    lanes = keep_ref.shape[1]
    at = pl.multiple_of(par_ref[0] * lanes, LANES)
    other = pl.multiple_of((1 - par_ref[0]) * lanes, LANES)
    keep_ref[...] = full_ref[:, pl.ds(at, lanes)]
    send_ref[...] = full_ref[:, pl.ds(other, lanes)]


def lane_joined(par_ref, mine_ref, theirs_ref, full_ref, start=0):
    lanes = mine_ref.shape[1]
    at = pl.multiple_of(start + par_ref[0] * lanes, LANES)
    other = pl.multiple_of(start + (1 - par_ref[0]) * lanes, LANES)
    full_ref[:, pl.ds(at, lanes)] = mine_ref[...]
    full_ref[:, pl.ds(other, lanes)] = theirs_ref[...]


def spans(block_refs):
    start, found = 0, []
    for ref in block_refs:
        found.append((start, ref))
        start += ref.shape[1]
    return found


def back_project(projected, block_refs, full_ref):
    parts = jnp.concatenate(thirds(projected), axis=0)
    for start, ref in spans(block_refs):
        tall = jnp.dot(parts, ref[...], preferred_element_type=F32)
        full_ref[:, start : start + ref.shape[1]] = fold(tall, projected.shape[0])


def forward_project(applied, block_refs):
    total = 0.0
    for start, ref in spans(block_refs):
        parts = jnp.concatenate(thirds(applied[:, start : start + ref.shape[1]]), axis=0)
        tall = lax.dot_general(parts, ref[...], (((1,), (1,)), ((), ())), preferred_element_type=F32)
        total = total + fold(tall, applied.shape[0])
    return total


def apply_first_body(masks, gathered, me_ref, par_ref, own_ref, twin_ref, *rest):
    pairs = rest[: len(masks)]
    rest = rest[len(masks) :]
    me = me_ref[0]
    days = own_ref.shape[1]
    if gathered:
        *pieces, block_ref, keep_ref, send_ref, proj_ref, full_ref = rest
        for mask, piece in enumerate(pieces):
            block_ref[pl.ds(pl.multiple_of((me ^ mask) * days, LANES), days), :] = piece[...]
    else:
        block_ref, keep_ref, send_ref, proj_ref, full_ref = rest

    def place(source, value):
        proj_ref[:, pl.ds(pl.multiple_of(source * days, LANES), days)] = value

    place(me, own_ref[...])
    place(me ^ 1, twin_ref[...])
    for mask, pair_ref in zip(masks, pairs):
        place(me ^ mask, pair_ref[0])
        place(me ^ mask ^ 1, pair_ref[1])
    back_project(proj_ref[...], [block_ref], full_ref)
    lane_halves(par_ref, full_ref, keep_ref, send_ref)


def apply_body(core_ref, par_ref, mine_ref, theirs_ref, *rest):
    *block_refs, keep_ref, send_ref, proj_ref, full_ref = rest
    joined(core_ref, mine_ref, theirs_ref, proj_ref)
    back_project(proj_ref[:, : block_refs[0].shape[0]], block_refs, full_ref)
    lane_halves(par_ref, full_ref, keep_ref, send_ref)


def gram_of(applied):
    return lax.dot_general(applied, applied, (((1,), (1,)), ((), ())), precision=HIGH, preferred_element_type=F32)


def project_body(days_all, scaled, pieces, chunks, par_ref, core_ref, *rest):
    halves_refs = rest[: 2 * pieces]
    block_refs = rest[2 * pieces : 2 * pieces + chunks]
    rest = rest[2 * pieces + chunks :]
    inv_ref, rest = (rest[0], rest[1:]) if scaled else (None, rest)
    keep_ref, send_ref, full_ref, out_ref = rest
    start = 0
    for k in range(pieces):
        mine_ref, theirs_ref = halves_refs[2 * k : 2 * k + 2]
        lane_joined(par_ref, mine_ref, theirs_ref, full_ref, start)
        start += 2 * mine_ref.shape[1]
    factors = full_ref.shape[0]
    applied = full_ref[...] / days_all
    if scaled:
        applied = jnp.dot(inv_ref[...], applied, precision=HIGH, preferred_element_type=F32)
    days = block_refs[0].shape[0]
    out_ref[:, :days] = forward_project(applied, block_refs)
    out_ref[:, days:] = jnp.concatenate(
        [gram_of(applied), jnp.zeros((factors, out_ref.shape[1] - days - factors), F32)], axis=1
    )
    halves(core_ref, out_ref, keep_ref, send_ref)


def eliminate(gram):
    size = gram.shape[0]
    rows = lax.broadcasted_iota(jnp.int32, (size, 2 * size), 0)
    lanes = lax.broadcasted_iota(jnp.int32, (size, 2 * size), 1)
    work = jnp.concatenate([gram, jnp.zeros_like(gram)], axis=1)
    work = jnp.where(lanes == rows + size, 1.0, work)
    for first in range(0, size, GROUP):
        columns = [jnp.broadcast_to(work[:, first + j : first + j + 1], work.shape) for j in range(GROUP)]
        for j in range(GROUP):
            k = first + j
            inverse = 1.0 / columns[j][k : k + 1, :]
            below = jnp.where(rows > k, columns[j], 0.0)
            for later in range(j + 1, GROUP):
                columns[later] = columns[later] - below * (columns[later][k : k + 1, :] * inverse)
            work = work - below * (work[k : k + 1, :] * inverse)
    on_diag = jnp.where(lanes == rows, work, 0.0)
    pivots = jnp.sqrt(jnp.sum(on_diag, axis=1, keepdims=True))
    diag_row = jnp.sqrt(jnp.sum(on_diag, axis=0, keepdims=True))[:, :size]
    return work[:, size:] / pivots, diag_row


def factor_body(days, core_ref, mine_ref, theirs_ref, inv_ref, diag_ref, full_ref):
    joined(core_ref, mine_ref, theirs_ref, full_ref)
    size = inv_ref.shape[0]
    inverse, diag_row = eliminate(full_ref[:, days : days + size])
    inv_ref[...] = inverse
    diag_ref[...] = diag_row


def last_gram_body(days_all, mine_ref, inv_ref, applied_ref, gram_ref):
    applied = jnp.dot(inv_ref[...], mine_ref[...] / days_all, precision=HIGH, preferred_element_type=F32)
    applied_ref[...] = applied
    gram = gram_of(applied)
    half = gram_ref.shape[0]
    gram_ref[...] = jnp.concatenate([gram[:half], gram[half:]], axis=1)


def last_body(scale, par_ref, mine_ref, theirs_ref, gram_ref, *rest):
    diag_refs = rest[: ITERS - 1]
    out_ref, strengths_ref, full_ref = rest[ITERS - 1 :]
    lane_joined(par_ref, mine_ref, theirs_ref, full_ref)
    factors = full_ref.shape[0]
    gram = jnp.concatenate([gram_ref[:, :factors], gram_ref[:, factors:]], axis=0)
    inverse, diag_row = eliminate(gram)
    out_ref[...] = jnp.dot(inverse, full_ref[...], precision=HIGH, preferred_element_type=F32) * scale
    for k, ref in enumerate(diag_refs):
        strengths_ref[k : k + 1, :] = ref[...]
    strengths_ref[ITERS - 1 : ITERS, :] = diag_row


def swap(x, axis, mask):
    size = lax.axis_size(axis)
    return lax.ppermute(x, axis, [(s, s ^ mask) for s in range(size)])


def tree(parts):
    while len(parts) > 1:
        parts = [parts[i] + parts[i + 1] for i in range(0, len(parts), 2)]
    return parts[0]


def sum_chips(x):
    size = lax.axis_size("gr")
    return tree([x if m == 0 else swap(x, "gr", m) for m in range(0, size, 2)])


def sum_days(keep, send):
    size = lax.axis_size("gc")
    mine = keep + swap(send, "gc", 1)
    mask = 2
    while mask < size:
        mine = mine + swap(mine, "gc", mask)
        mask *= 2
    return mine


def sum_assets(keep, send):
    mine = sum_chips(keep + swap(send, "gr", 1))
    return mine, swap(mine, "gr", 1)


def local(returns, start_seed):
    days, assets = returns.shape
    factors = start_seed.shape[1]
    blocks, slabs = lax.axis_size("gr"), lax.axis_size("gc")
    span = assets // blocks
    slab_days = days * blocks
    days_all = slab_days * slabs
    core = (lax.axis_index("gr") % 2).astype(jnp.int32).reshape(1)
    par = (lax.axis_index("gc") % 2).astype(jnp.int32).reshape(1)
    me = lax.axis_index("gr").astype(jnp.int32).reshape(1)
    half = factors // 2
    packed_width = slab_days + LANES
    dots = 6 * factors * slab_days * span

    unit = 2 * LANES
    cut = span * CUT // 8 // unit * unit
    rest = span - cut
    masks = tuple(range(2, blocks, 2))

    dealt = deal(returns, blocks, cut)
    block = lax.all_to_all(dealt, "gr", 0, 0).reshape(slab_days, cut)
    own, *pieces = call(
        functools.partial(project_first_body, span),
        [((factors, days), F32)] + [((days, rest), BF16)] * blocks,
        [me], [returns, start_seed.T], 4 * days * assets * factors,
    )
    twin = swap(own, "gr", 1)
    both = jnp.stack([own, twin])
    pairs = [swap(both, "gr", m) for m in masks]
    pieces = [p if m == 0 else swap(p, "gr", m) for m, p in enumerate(pieces)]

    asset_half = ((factors, span // 2), F32)
    day_half = ((half, packed_width), F32)
    full_assets = pltpu.VMEM((factors, span), F32)
    slab = pltpu.VMEM((factors, slab_days), F32)
    full_days = pltpu.VMEM((factors, packed_width), F32)

    shared = [own, twin, *pairs]
    keep, send = call(
        functools.partial(apply_first_body, masks, False), [((factors, cut // 2), F32)] * 2, [me, par],
        shared + [block], dots, [slab, pltpu.VMEM((factors, cut), F32)],
    )
    mine = sum_days(keep, send)
    theirs = swap(mine, "gc", 1)
    last, keep, send = call(
        functools.partial(apply_first_body, masks, True),
        [((slab_days, rest), BF16)] + [((factors, rest // 2), F32)] * 2, [me, par],
        shared + pieces, dots, [slab, pltpu.VMEM((factors, rest), F32)],
    )
    mine_late = sum_days(keep, send)
    pieces = [mine, theirs, mine_late, swap(mine_late, "gc", 1)]
    block_list = [block, last]
    inverse = None
    diagonals = []
    for sweep in range(ITERS - 1):
        if sweep:
            mine = sum_days(keep, send)
            pieces = [mine, swap(mine, "gc", 1)]
        arrays = pieces + block_list + ([] if inverse is None else [inverse])
        keep, send = call(
            functools.partial(
                project_body, days_all, inverse is not None, len(pieces) // 2, len(block_list)
            ),
            [day_half] * 2, [par, core], arrays, dots, [full_assets, full_days],
        )
        mine, theirs = sum_assets(keep, send)
        keep, send = call(
            apply_body, [asset_half] * 2, [core, par], [mine, theirs, *block_list], dots,
            [full_days, full_assets],
        )
        inverse, diag_row = call(
            functools.partial(factor_body, slab_days),
            [((factors, factors), F32), ((1, factors), F32)], [core], [mine, theirs],
            dots, [full_days],
        )
        diagonals.append(diag_row)
    mine = sum_days(keep, send)
    applied, gram = call(
        functools.partial(last_gram_body, days_all),
        [asset_half, ((half, 2 * factors), F32)], [], [mine, inverse], dots,
    )
    theirs = swap(applied, "gc", 1)
    gram = gram + swap(gram, "gr", 1)
    mask = 2
    while mask < blocks:
        gram = gram + swap(gram, "gr", mask)
        mask *= 2
    gram = gram + swap(gram, "gc", 1)
    loadings, strengths = call(
        functools.partial(last_body, math.sqrt(assets)),
        [((factors, span), F32), ((ITERS, factors), F32)], [par],
        [applied, theirs, gram, *diagonals], dots, [full_assets],
    )
    return loadings.T, strengths


def solution(mesh):
    placed = (P(("gr", "gc"), None), P())
    return jax.shard_map(local, mesh=mesh, in_specs=placed, out_specs=(P("gr", None), P()), check_vma=False)
```

profile of v0, /device:TPU:0, one launch (start us, length us, event | category | flops | bytes accessed | tf_op | source)
XLA Modules:
  0.0 145.6 jit_solution(16131552819148899918)
XLA Ops:
  0.6 2.5 %shard_map.42 = bf16[8,128,512]{2,1,0:T(8,128)(2,1)} custom-call(bf16[128,8192]{1,0:T(8,128)(2,1)} %returns_ref.3), custom_call_target="tpu_custom_call" | custom-call | tf_op jit(solution)/shard_map/pallas_call | solution.py:68
  3.1 5.2 %all-to-all-start = ((bf16[8,128,512]{2,1,0:T(8,128)(2,1)}), bf16[8,128,512]{2,1,0:T(8,128)(2,1)S(1)}, u32[]{:S(2)}, u32[]{:S(2)}) async-start(bf16[8,128,512]{2,1,0:T(8,128)(2,1)} %shard_map.42), calls=%async_computation | async-start | bytes 2097152 | tf_op jit(solution)/shard_map/all_to_all | solution.py:306
  13.5 1.8 %collective-permute-start.1 = (f32[2,64,128]{2,1,0:T(8,128)S(1)}, f32[2,64,128]{2,1,0:T(8,128)S(1)}, u32[]{:S(2)}, u32[]{:S(2)}) collective-permute-start(f32[2,64,128]{2,1,0:T(8,128)S(1)} %pad_maximum_fusion), channel_id=1, source_target_pairs={{0,8},{4,12},{8,0},{12,4},{16,24},{20,28},{24,16},{28,20},{1,9},{5... | collective-permute-start | bytes 196616 | tf_op jit(solution)/shard_map/ppermute | solution.py:257
  17.1 7.8 %collective-permute-done.1.rest_0_ = f32[2,64,128]{2,1,0:T(8,128)S(1)} collective-permute-done((f32[2,64,128]{2,1,0:T(8,128)S(1)}, f32[2,64,128]{2,1,0:T(8,128)S(1)}, u32[]{:S(2)}, u32[]{:S(2)}) %collective-permute-start.1) | collective-permute-done | bytes 65568 | tf_op jit(solution)/shard_map/ppermute | solution.py:257
  26.3 7.7 %collective-permute-done.2.rest_1_ = f32[2,64,128]{2,1,0:T(8,128)S(1)} collective-permute-done((f32[2,64,128]{2,1,0:T(8,128)S(1)}, f32[2,64,128]{2,1,0:T(8,128)S(1)}, u32[]{:S(2)}, u32[]{:S(2)}) %collective-permute-start.2) | collective-permute-done | bytes 65568 | tf_op jit(solution)/shard_map/ppermute | solution.py:257
  38.1 3.2 %collective-permute-done.13.rest_10_ = bf16[128,512]{1,0:T(8,128)(2,1)S(1)} collective-permute-done((bf16[128,512]{1,0:T(8,128)(2,1)}, bf16[128,512]{1,0:T(8,128)(2,1)S(1)}, u32[]{:S(2)}, u32[]{:S(2)}) %collective-permute-start.13) | collective-permute-done | bytes 131104 | tf_op jit(solution)/shard_map/ppermute | solution.py:257
  41.3 2.2 %collective-permute-done.8.rest_5_ = bf16[128,512]{1,0:T(8,128)(2,1)S(1)} collective-permute-done((bf16[128,512]{1,0:T(8,128)(2,1)}, bf16[128,512]{1,0:T(8,128)(2,1)S(1)}, u32[]{:S(2)}, u32[]{:S(2)}) %collective-permute-start.8) | collective-permute-done | bytes 131104 | tf_op jit(solution)/shard_map/ppermute | solution.py:257
  43.5 2.4 %collective-permute-done.9.rest_6_ = bf16[128,512]{1,0:T(8,128)(2,1)S(1)} collective-permute-done((bf16[128,512]{1,0:T(8,128)(2,1)S(1)}, bf16[128,512]{1,0:T(8,128)(2,1)S(1)}, u32[]{:S(2)}, u32[]{:S(2)}) %collective-permute-start.9) | collective-permute-done | bytes 131104 | tf_op jit(solution)/shard_map/ppermute | solution.py:257
  51.2 2.0 %collective-permute-done.14 = f32[64,256]{1,0:T(8,128)S(1)} collective-permute-done((f32[64,256]{1,0:T(8,128)}, f32[64,256]{1,0:T(8,128)S(1)}, u32[]{:S(2)}, u32[]{:S(2)}) %collective-permute-start.14) | collective-permute-done | bytes 65568 | tf_op jit(solution)/shard_map/ppermute | solution.py:257
  53.2 2.7 %collective-permute-start.15 = (f32[64,256]{1,0:T(8,128)S(1)}, f32[64,256]{1,0:T(8,128)S(1)}, u32[]{:S(2)}, u32[]{:S(2)}) collective-permute-start(f32[64,256]{1,0:T(8,128)S(1)} %add.71), channel_id=1, source_target_pairs={{0,2},{1,3},{2,0},{3,1},{4,6},{5,7},{6,4},{7,5},{8,10},{9,11},{10,... | collective-permute-start | bytes 196616 | tf_op jit(solution)/shard_map/ppermute | solution.py:257
  55.8 2.1 %collective-permute-start.5 = (f32[64,256]{1,0:T(8,128)S(1)}, f32[64,256]{1,0:T(8,128)S(1)}, u32[]{:S(2)}, u32[]{:S(2)}) collective-permute-start(f32[64,256]{1,0:T(8,128)S(1)} %add.69), channel_id=1, source_target_pairs={{0,2},{1,3},{2,0},{3,1},{4,6},{5,7},{6,4},{7,5},{8,10},{9,11},{10,... | collective-permute-start | bytes 196616 | tf_op jit(solution)/shard_map/ppermute | solution.py:257
  58.7 2.4 %collective-permute-start.16 = (f32[64,256]{1,0:T(8,128)S(1)}, f32[64,256]{1,0:T(8,128)S(1)}, u32[]{:S(2)}, u32[]{:S(2)}) collective-permute-start(f32[64,256]{1,0:T(8,128)S(1)} %add.72.rest_2_), channel_id=1, source_target_pairs={{0,1},{1,0},{2,3},{3,2},{4,5},{5,4},{6,7},{7,6},{8,9},{9,8},{10,11... | collective-permute-start | bytes 196616 | tf_op jit(solution)/shard_map/ppermute | solution.py:257
  61.2 2.2 %collective-permute-start.6 = (f32[64,256]{1,0:T(8,128)S(1)}, f32[64,256]{1,0:T(8,128)S(1)}, u32[]{:S(2)}, u32[]{:S(2)}) collective-permute-start(f32[64,256]{1,0:T(8,128)S(1)} %add.70.rest_0_), channel_id=1, source_target_pairs={{0,1},{1,0},{2,3},{3,2},{4,5},{5,4},{6,7},{7,6},{8,9},{9,8},{10,11... | collective-permute-start | bytes 196616 | tf_op jit(solution)/shard_map/ppermute | solution.py:257
  63.4 2.2 %collective-permute-done.6.rest_1_ = f32[64,256]{1,0:T(8,128)S(1)} collective-permute-done((f32[64,256]{1,0:T(8,128)S(1)}, f32[64,256]{1,0:T(8,128)S(1)}, u32[]{:S(2)}, u32[]{:S(2)}) %collective-permute-start.6) | collective-permute-done | bytes 65568 | tf_op jit(solution)/shard_map/ppermute | solution.py:257
  71.7 3.2 %collective-permute-done.18 = f32[32,1152]{1,0:T(8,128)S(1)} collective-permute-done((f32[32,1152]{1,0:T(8,128)S(1)}, f32[32,1152]{1,0:T(8,128)S(1)}, u32[]{:S(2)}, u32[]{:S(2)}) %collective-permute-start.18) | collective-permute-done | bytes 147488 | tf_op jit(solution)/shard_map/ppermute | solution.py:257
  74.9 3.5 %collective-permute-done.19 = f32[32,1152]{1,0:T(8,128)S(1)} collective-permute-done((f32[32,1152]{1,0:T(8,128)S(1)}, f32[32,1152]{1,0:T(8,128)S(1)}, u32[]{:S(2)}, u32[]{:S(2)}) %collective-permute-start.19) | collective-permute-done | bytes 147488 | tf_op jit(solution)/shard_map/ppermute | solution.py:257
  80.5 2.1 %collective-permute-start.22 = (f32[64,512]{1,0:T(8,128)S(1)}, f32[64,512]{1,0:T(8,128)S(1)}, u32[]{:S(2)}, u32[]{:S(2)}) collective-permute-start(f32[64,512]{1,0:T(8,128)S(1)} %get-tuple-element.49), channel_id=1, source_target_pairs={{0,1},{1,0},{2,3},{3,2},{4,5},{5,4},{6,7},{7,6},{8,9},{9,8},{10,11... | collective-permute-start | bytes 393224 | tf_op jit(solution)/shard_map/ppermute | solution.py:257
  82.6 3.8 %collective-permute-done.22 = f32[64,512]{1,0:T(8,128)S(1)} collective-permute-done((f32[64,512]{1,0:T(8,128)S(1)}, f32[64,512]{1,0:T(8,128)S(1)}, u32[]{:S(2)}, u32[]{:S(2)}) %collective-permute-start.22) | collective-permute-done | bytes 131104 | tf_op jit(solution)/shard_map/ppermute | solution.py:257
  86.4 3.4 %collective-permute-start.23 = (f32[64,512]{1,0:T(8,128)S(1)}, f32[64,512]{1,0:T(8,128)S(1)}, u32[]{:S(2)}, u32[]{:S(2)}) collective-permute-start(f32[64,512]{1,0:T(8,128)S(1)} %add.77), channel_id=1, source_target_pairs={{0,2},{1,3},{2,0},{3,1},{4,6},{5,7},{6,4},{7,5},{8,10},{9,11},{10,... | collective-permute-start | bytes 393224 | tf_op jit(solution)/shard_map/ppermute | solution.py:257
  89.8 5.8 %collective-permute-done.23 = f32[64,512]{1,0:T(8,128)S(1)} collective-permute-done((f32[64,512]{1,0:T(8,128)S(1)}, f32[64,512]{1,0:T(8,128)S(1)}, u32[]{:S(2)}, u32[]{:S(2)}) %collective-permute-start.23) | collective-permute-done | bytes 131104 | tf_op jit(solution)/shard_map/ppermute | solution.py:257
  95.7 1.7 %shard_map.47 = (f32[64,64]{1,0:T(8,128)S(1)}, f32[1,64]{1,0:T(1,128)S(1)}) custom-call(s32[1]{0:T(128)} %bitcast.1.core_ref, f32[32,1152]{1,0:T(8,128)S(1)} %add_add_fusion.1.mine_ref, f32[32,1152]{1,0:T(8,128)S(1)} %collective-permute-done.21.theirs_ref), custom_call_target="tpu_custom_call" | custom-call | flops 402653184 | bytes 16640 | tf_op jit(solution)/shard_map/pallas_call | solution.py:31
  97.3 3.3 %collective-permute-done.24.rest_1_ = f32[64,512]{1,0:T(8,128)S(1)} collective-permute-done((f32[64,512]{1,0:T(8,128)S(1)}, f32[64,512]{1,0:T(8,128)S(1)}, u32[]{:S(2)}, u32[]{:S(2)}) %collective-permute-start.24) | collective-permute-done | bytes 131104 | tf_op jit(solution)/shard_map/ppermute | solution.py:257
  106.9 3.2 %collective-permute-done.26 = f32[32,1152]{1,0:T(8,128)S(1)} collective-permute-done((f32[32,1152]{1,0:T(8,128)S(1)}, f32[32,1152]{1,0:T(8,128)S(1)}, u32[]{:S(2)}, u32[]{:S(2)}) %collective-permute-start.26) | collective-permute-done | bytes 147488 | tf_op jit(solution)/shard_map/ppermute | solution.py:257
  111.2 2.4 %collective-permute-done.28 = f32[32,1152]{1,0:T(8,128)S(1)} collective-permute-done((f32[32,1152]{1,0:T(8,128)S(1)}, f32[32,1152]{1,0:T(8,128)S(1)}, u32[]{:S(2)}, u32[]{:S(2)}) %collective-permute-start.28) | collective-permute-done | bytes 147488 | tf_op jit(solution)/shard_map/ppermute | solution.py:257
  116.0 5.3 %collective-permute-done.30 = f32[64,512]{1,0:T(8,128)S(1)} collective-permute-done((f32[64,512]{1,0:T(8,128)S(1)}, f32[64,512]{1,0:T(8,128)S(1)}, u32[]{:S(2)}, u32[]{:S(2)}) %collective-permute-start.30) | collective-permute-done | bytes 131104 | tf_op jit(solution)/shard_map/ppermute | solution.py:257
  122.9 1.7 %shard_map.50 = (f32[64,64]{1,0:T(8,128)S(1)}, f32[1,64]{1,0:T(1,128)S(1)}) custom-call(s32[1]{0:T(128)} %bitcast.1.core_ref, f32[32,1152]{1,0:T(8,128)S(1)} %add_add_fusion.mine_ref, f32[32,1152]{1,0:T(8,128)S(1)} %collective-permute-done.29.theirs_ref), custom_call_target="tpu_custom_call" | custom-call | flops 402653184 | bytes 16640 | tf_op jit(solution)/shard_map/pallas_call | solution.py:31
  124.5 5.2 %collective-permute-done.31 = f32[64,512]{1,0:T(8,128)S(1)} collective-permute-done((f32[64,512]{1,0:T(8,128)S(1)}, f32[64,512]{1,0:T(8,128)S(1)}, u32[]{:S(2)}, u32[]{:S(2)}) %collective-permute-start.31) | collective-permute-done | bytes 131104 | tf_op jit(solution)/shard_map/ppermute | solution.py:257
  132.3 3.1 %collective-permute-done.34 = f32[32,128]{1,0:T(8,128)S(1)} collective-permute-done((f32[32,128]{1,0:T(8,128)S(1)}, f32[32,128]{1,0:T(8,128)S(1)}, u32[]{:S(2)}, u32[]{:S(2)}) %collective-permute-start.34) | collective-permute-done | bytes 16416 | tf_op jit(solution)/shard_map/ppermute | solution.py:257
  136.0 3.1 %collective-permute-done.35 = f32[32,128]{1,0:T(8,128)S(1)} collective-permute-done((f32[32,128]{1,0:T(8,128)S(1)}, f32[32,128]{1,0:T(8,128)S(1)}, u32[]{:S(2)}, u32[]{:S(2)}) %collective-permute-start.35) | collective-permute-done | bytes 16416 | tf_op jit(solution)/shard_map/ppermute | solution.py:257
  139.2 1.9 %collective-permute-start.36 = (f32[32,128]{1,0:T(8,128)S(1)}, f32[32,128]{1,0:T(8,128)S(1)}, u32[]{:S(2)}, u32[]{:S(2)}) collective-permute-start(f32[32,128]{1,0:T(8,128)S(1)} %add.87), channel_id=1, source_target_pairs={{0,1},{1,0},{2,3},{3,2},{4,5},{5,4},{6,7},{7,6},{8,9},{9,8},{10,11... | collective-permute-start | bytes 49160 | tf_op jit(solution)/shard_map/ppermute | solution.py:257
  141.1 1.8 %collective-permute-done.36 = f32[32,128]{1,0:T(8,128)S(1)} collective-permute-done((f32[32,128]{1,0:T(8,128)S(1)}, f32[32,128]{1,0:T(8,128)S(1)}, u32[]{:S(2)}, u32[]{:S(2)}) %collective-permute-start.36) | collective-permute-done | bytes 16416 | tf_op jit(solution)/shard_map/ppermute | solution.py:257
  142.9 2.7 %shard_map.52 = (f32[64,1024]{1,0:T(8,128)}, f32[3,64]{1,0:T(4,128)}) custom-call(s32[1]{0:T(128)} %bitcast.par_ref, f32[64,512]{1,0:T(8,128)S(1)} %get-tuple-element.56.mine_ref, f32[64,512]{1,0:T(8,128)S(1)} %collective-permute-done.32.theirs_ref, f32[32,128]{1,0:T(8,128)S(1)} %add.88.gram_ref, f32[1,64]{1,0:T(1,128)S(1)} %get-tuple-element.58.rest_0_, ...), custom_call_target="tpu_custom_call" | custom-call | flops 402653184 | bytes 262912 | tf_op jit(solution)/shard_map/pallas_call | solution.py:31
  (85 shorter events, 41.3 us)
Async XLA Ops:
  3.1 47.1 %all-to-all-start = ((bf16[8,128,512]{2,1,0:T(8,128)(2,1)}), bf16[8,128,512]{2,1,0:T(8,128)(2,1)S(1)}, u32[]{:S(2)}, u32[]{:S(2)}) async-start(bf16[8,128,512]{2,1,0:T(8,128)(2,1)} %shard_map.42), calls=%async_computation | async-start | bytes 2097152 | tf_op jit(solution)/shard_map/all_to_all | solution.py:306
  11.9 24.8 %collective-permute-start.10 = (bf16[128,512]{1,0:T(8,128)(2,1)S(1)}, bf16[128,512]{1,0:T(8,128)(2,1)S(1)}, u32[]{:S(2)}, u32[]{:S(2)}) collective-permute-start(bf16[128,512]{1,0:T(8,128)(2,1)S(1)} %get-tuple-element.39), channel_id=1, source_target_pairs={{0,16},{4,20},{8,24},{12,28},{16,0},{20,4},{24,8},{28,12},{1,17},{... | collective-permute-start | bytes 393224 | tf_op jit(solution)/shard_map/ppermute | solution.py:257
  13.5 23.7 %collective-permute-start.11 = (bf16[128,512]{1,0:T(8,128)(2,1)S(1)}, bf16[128,512]{1,0:T(8,128)(2,1)S(1)}, u32[]{:S(2)}, u32[]{:S(2)}) collective-permute-start(bf16[128,512]{1,0:T(8,128)(2,1)S(1)} %get-tuple-element.40), channel_id=1, source_target_pairs={{0,20},{4,16},{8,28},{12,24},{16,4},{20,0},{24,12},{28,8},{1,21},{... | collective-permute-start | bytes 393224 | tf_op jit(solution)/shard_map/ppermute | solution.py:257
  13.5 11.3 %collective-permute-start.1 = (f32[2,64,128]{2,1,0:T(8,128)S(1)}, f32[2,64,128]{2,1,0:T(8,128)S(1)}, u32[]{:S(2)}, u32[]{:S(2)}) collective-permute-start(f32[2,64,128]{2,1,0:T(8,128)S(1)} %pad_maximum_fusion), channel_id=1, source_target_pairs={{0,8},{4,12},{8,0},{12,4},{16,24},{20,28},{24,16},{28,20},{1,9},{5... | collective-permute-start | bytes 196616 | tf_op jit(solution)/shard_map/ppermute | solution.py:257
  15.3 18.7 %collective-permute-start.2 = (f32[2,64,128]{2,1,0:T(8,128)S(1)}, f32[2,64,128]{2,1,0:T(8,128)S(1)}, u32[]{:S(2)}, u32[]{:S(2)}) collective-permute-start(f32[2,64,128]{2,1,0:T(8,128)S(1)} %pad_maximum_fusion), channel_id=1, source_target_pairs={{0,16},{4,20},{8,24},{12,28},{16,0},{20,4},{24,8},{28,12},{1,17},{... | collective-permute-start | bytes 196616 | tf_op jit(solution)/shard_map/ppermute | solution.py:257
  16.8 18.8 %collective-permute-start.3 = (f32[2,64,128]{2,1,0:T(8,128)S(1)}, f32[2,64,128]{2,1,0:T(8,128)S(1)}, u32[]{:S(2)}, u32[]{:S(2)}) collective-permute-start(f32[2,64,128]{2,1,0:T(8,128)S(1)} %pad_maximum_fusion), channel_id=1, source_target_pairs={{0,24},{4,28},{8,16},{12,20},{16,8},{20,12},{24,0},{28,4},{1,25},{... | collective-permute-start | bytes 196616 | tf_op jit(solution)/shard_map/ppermute | solution.py:257
  24.9 13.2 %collective-permute-start.12 = (bf16[128,512]{1,0:T(8,128)(2,1)}, bf16[128,512]{1,0:T(8,128)(2,1)S(1)}, u32[]{:S(2)}, u32[]{:S(2)}) collective-permute-start(bf16[128,512]{1,0:T(8,128)(2,1)} %get-tuple-element.41), channel_id=1, source_target_pairs={{0,24},{4,28},{8,16},{12,20},{16,8},{20,12},{24,0},{28,4},{1,25},{... | collective-permute-start | bytes 393224 | tf_op jit(solution)/shard_map/ppermute | solution.py:257
  34.6 6.6 %collective-permute-start.13 = (bf16[128,512]{1,0:T(8,128)(2,1)}, bf16[128,512]{1,0:T(8,128)(2,1)S(1)}, u32[]{:S(2)}, u32[]{:S(2)}) collective-permute-start(bf16[128,512]{1,0:T(8,128)(2,1)} %get-tuple-element.42), channel_id=1, source_target_pairs={{0,28},{4,24},{8,20},{12,16},{16,12},{20,8},{24,4},{28,0},{1,29},{... | collective-permute-start | bytes 393224 | tf_op jit(solution)/shard_map/ppermute | solution.py:257
  36.2 5.0 %collective-permute-start.7 = (bf16[128,512]{1,0:T(8,128)(2,1)}, bf16[128,512]{1,0:T(8,128)(2,1)S(1)}, u32[]{:S(2)}, u32[]{:S(2)}) collective-permute-start(bf16[128,512]{1,0:T(8,128)(2,1)} %get-tuple-element.36), channel_id=1, source_target_pairs={{0,4},{4,0},{8,12},{12,8},{16,20},{20,16},{24,28},{28,24},{1,5},{5... | collective-permute-start | bytes 393224 | tf_op jit(solution)/shard_map/ppermute | solution.py:257
  36.7 6.8 %collective-permute-start.8 = (bf16[128,512]{1,0:T(8,128)(2,1)}, bf16[128,512]{1,0:T(8,128)(2,1)S(1)}, u32[]{:S(2)}, u32[]{:S(2)}) collective-permute-start(bf16[128,512]{1,0:T(8,128)(2,1)} %get-tuple-element.37), channel_id=1, source_target_pairs={{0,8},{4,12},{8,0},{12,4},{16,24},{20,28},{24,16},{28,20},{1,9},{5... | collective-permute-start | bytes 393224 | tf_op jit(solution)/shard_map/ppermute | solution.py:257
  37.2 8.7 %collective-permute-start.9 = (bf16[128,512]{1,0:T(8,128)(2,1)S(1)}, bf16[128,512]{1,0:T(8,128)(2,1)S(1)}, u32[]{:S(2)}, u32[]{:S(2)}) collective-permute-start(bf16[128,512]{1,0:T(8,128)(2,1)S(1)} %get-tuple-element.38), channel_id=1, source_target_pairs={{0,12},{4,8},{8,4},{12,0},{16,28},{20,24},{24,20},{28,16},{1,13},{... | collective-permute-start | bytes 393224 | tf_op jit(solution)/shard_map/ppermute | solution.py:257
  48.7 4.5 %collective-permute-start.14 = (f32[64,256]{1,0:T(8,128)}, f32[64,256]{1,0:T(8,128)S(1)}, u32[]{:S(2)}, u32[]{:S(2)}) collective-permute-start(f32[64,256]{1,0:T(8,128)} %get-tuple-element.44), channel_id=1, source_target_pairs={{0,1},{1,0},{2,3},{3,2},{4,5},{5,4},{6,7},{7,6},{8,9},{9,8},{10,11... | collective-permute-start | bytes 196616 | tf_op jit(solution)/shard_map/ppermute | solution.py:257
  50.7 5.2 %collective-permute-start.4 = (f32[64,256]{1,0:T(8,128)S(1)}, f32[64,256]{1,0:T(8,128)S(1)}, u32[]{:S(2)}, u32[]{:S(2)}) collective-permute-start(f32[64,256]{1,0:T(8,128)S(1)} %get-tuple-element.34), channel_id=1, source_target_pairs={{0,1},{1,0},{2,3},{3,2},{4,5},{5,4},{6,7},{7,6},{8,9},{9,8},{10,11... | collective-permute-start | bytes 196616 | tf_op jit(solution)/shard_map/ppermute | solution.py:257
  53.2 5.6 %collective-permute-start.15 = (f32[64,256]{1,0:T(8,128)S(1)}, f32[64,256]{1,0:T(8,128)S(1)}, u32[]{:S(2)}, u32[]{:S(2)}) collective-permute-start(f32[64,256]{1,0:T(8,128)S(1)} %add.71), channel_id=1, source_target_pairs={{0,2},{1,3},{2,0},{3,1},{4,6},{5,7},{6,4},{7,5},{8,10},{9,11},{10,... | collective-permute-start | bytes 196616 | tf_op jit(solution)/shard_map/ppermute | solution.py:257
  55.8 5.4 %collective-permute-start.5 = (f32[64,256]{1,0:T(8,128)S(1)}, f32[64,256]{1,0:T(8,128)S(1)}, u32[]{:S(2)}, u32[]{:S(2)}) collective-permute-start(f32[64,256]{1,0:T(8,128)S(1)} %add.69), channel_id=1, source_target_pairs={{0,2},{1,3},{2,0},{3,1},{4,6},{5,7},{6,4},{7,5},{8,10},{9,11},{10,... | collective-permute-start | bytes 196616 | tf_op jit(solution)/shard_map/ppermute | solution.py:257
  58.7 4.7 %collective-permute-start.16 = (f32[64,256]{1,0:T(8,128)S(1)}, f32[64,256]{1,0:T(8,128)S(1)}, u32[]{:S(2)}, u32[]{:S(2)}) collective-permute-start(f32[64,256]{1,0:T(8,128)S(1)} %add.72.rest_2_), channel_id=1, source_target_pairs={{0,1},{1,0},{2,3},{3,2},{4,5},{5,4},{6,7},{7,6},{8,9},{9,8},{10,11... | collective-permute-start | bytes 196616 | tf_op jit(solution)/shard_map/ppermute | solution.py:257
  61.2 4.4 %collective-permute-start.6 = (f32[64,256]{1,0:T(8,128)S(1)}, f32[64,256]{1,0:T(8,128)S(1)}, u32[]{:S(2)}, u32[]{:S(2)}) collective-permute-start(f32[64,256]{1,0:T(8,128)S(1)} %add.70.rest_0_), channel_id=1, source_target_pairs={{0,1},{1,0},{2,3},{3,2},{4,5},{5,4},{6,7},{7,6},{8,9},{9,8},{10,11... | collective-permute-start | bytes 196616 | tf_op jit(solution)/shard_map/ppermute | solution.py:257
  68.1 6.8 %collective-permute-start.18 = (f32[32,1152]{1,0:T(8,128)S(1)}, f32[32,1152]{1,0:T(8,128)S(1)}, u32[]{:S(2)}, u32[]{:S(2)}) collective-permute-start(f32[32,1152]{1,0:T(8,128)S(1)} %add.73), channel_id=1, source_target_pairs={{0,8},{4,12},{8,0},{12,4},{16,24},{20,28},{24,16},{28,20},{1,9},{5... | collective-permute-start | bytes 442376 | tf_op jit(solution)/shard_map/ppermute | solution.py:257
  69.6 8.8 %collective-permute-start.19 = (f32[32,1152]{1,0:T(8,128)S(1)}, f32[32,1152]{1,0:T(8,128)S(1)}, u32[]{:S(2)}, u32[]{:S(2)}) collective-permute-start(f32[32,1152]{1,0:T(8,128)S(1)} %add.73), channel_id=1, source_target_pairs={{0,16},{4,20},{8,24},{12,28},{16,0},{20,4},{24,8},{28,12},{1,17},{... | collective-permute-start | bytes 442376 | tf_op jit(solution)/shard_map/ppermute | solution.py:257
  71.2 7.1 %collective-permute-start.20 = (f32[32,1152]{1,0:T(8,128)S(1)}, f32[32,1152]{1,0:T(8,128)S(1)}, u32[]{:S(2)}, u32[]{:S(2)}) collective-permute-start(f32[32,1152]{1,0:T(8,128)S(1)} %add.73), channel_id=1, source_target_pairs={{0,24},{4,28},{8,16},{12,20},{16,8},{20,12},{24,0},{28,4},{1,25},{... | collective-permute-start | bytes 442376 | tf_op jit(solution)/shard_map/ppermute | solution.py:257
  80.5 5.9 %collective-permute-start.22 = (f32[64,512]{1,0:T(8,128)S(1)}, f32[64,512]{1,0:T(8,128)S(1)}, u32[]{:S(2)}, u32[]{:S(2)}) collective-permute-start(f32[64,512]{1,0:T(8,128)S(1)} %get-tuple-element.49), channel_id=1, source_target_pairs={{0,1},{1,0},{2,3},{3,2},{4,5},{5,4},{6,7},{7,6},{8,9},{9,8},{10,11... | collective-permute-start | bytes 393224 | tf_op jit(solution)/shard_map/ppermute | solution.py:257
  86.4 9.2 %collective-permute-start.23 = (f32[64,512]{1,0:T(8,128)S(1)}, f32[64,512]{1,0:T(8,128)S(1)}, u32[]{:S(2)}, u32[]{:S(2)}) collective-permute-start(f32[64,512]{1,0:T(8,128)S(1)} %add.77), channel_id=1, source_target_pairs={{0,2},{1,3},{2,0},{3,1},{4,6},{5,7},{6,4},{7,5},{8,10},{9,11},{10,... | collective-permute-start | bytes 393224 | tf_op jit(solution)/shard_map/ppermute | solution.py:257
  95.6 5.0 %collective-permute-start.24 = (f32[64,512]{1,0:T(8,128)S(1)}, f32[64,512]{1,0:T(8,128)S(1)}, u32[]{:S(2)}, u32[]{:S(2)}) collective-permute-start(f32[64,512]{1,0:T(8,128)S(1)} %add.78.rest_0_), channel_id=1, source_target_pairs={{0,1},{1,0},{2,3},{3,2},{4,5},{5,4},{6,7},{7,6},{8,9},{9,8},{10,11... | collective-permute-start | bytes 393224 | tf_op jit(solution)/shard_map/ppermute | solution.py:257
  103.4 6.8 %collective-permute-start.26 = (f32[32,1152]{1,0:T(8,128)S(1)}, f32[32,1152]{1,0:T(8,128)S(1)}, u32[]{:S(2)}, u32[]{:S(2)}) collective-permute-start(f32[32,1152]{1,0:T(8,128)S(1)} %add.79), channel_id=1, source_target_pairs={{0,8},{4,12},{8,0},{12,4},{16,24},{20,28},{24,16},{28,20},{1,9},{5... | collective-permute-start | bytes 442376 | tf_op jit(solution)/shard_map/ppermute | solution.py:257
  104.8 6.4 %collective-permute-start.27 = (f32[32,1152]{1,0:T(8,128)S(1)}, f32[32,1152]{1,0:T(8,128)S(1)}, u32[]{:S(2)}, u32[]{:S(2)}) collective-permute-start(f32[32,1152]{1,0:T(8,128)S(1)} %add.79), channel_id=1, source_target_pairs={{0,16},{4,20},{8,24},{12,28},{16,0},{20,4},{24,8},{28,12},{1,17},{... | collective-permute-start | bytes 442376 | tf_op jit(solution)/shard_map/ppermute | solution.py:257
  105.4 8.1 %collective-permute-start.28 = (f32[32,1152]{1,0:T(8,128)S(1)}, f32[32,1152]{1,0:T(8,128)S(1)}, u32[]{:S(2)}, u32[]{:S(2)}) collective-permute-start(f32[32,1152]{1,0:T(8,128)S(1)} %add.79), channel_id=1, source_target_pairs={{0,24},{4,28},{8,16},{12,20},{16,8},{20,12},{24,0},{28,4},{1,25},{... | collective-permute-start | bytes 442376 | tf_op jit(solution)/shard_map/ppermute | solution.py:257
  115.6 5.6 %collective-permute-start.30 = (f32[64,512]{1,0:T(8,128)S(1)}, f32[64,512]{1,0:T(8,128)S(1)}, u32[]{:S(2)}, u32[]{:S(2)}) collective-permute-start(f32[64,512]{1,0:T(8,128)S(1)} %get-tuple-element.54), channel_id=1, source_target_pairs={{0,1},{1,0},{2,3},{3,2},{4,5},{5,4},{6,7},{7,6},{8,9},{9,8},{10,11... | collective-permute-start | bytes 393224 | tf_op jit(solution)/shard_map/ppermute | solution.py:257
  121.3 8.5 %collective-permute-start.31 = (f32[64,512]{1,0:T(8,128)S(1)}, f32[64,512]{1,0:T(8,128)S(1)}, u32[]{:S(2)}, u32[]{:S(2)}) collective-permute-start(f32[64,512]{1,0:T(8,128)S(1)} %add.83), channel_id=1, source_target_pairs={{0,2},{1,3},{2,0},{3,1},{4,6},{5,7},{6,4},{7,5},{8,10},{9,11},{10,... | collective-permute-start | bytes 393224 | tf_op jit(solution)/shard_map/ppermute | solution.py:257
  130.4 12.5 %collective-permute-start.32 = (f32[64,512]{1,0:T(8,128)S(1)}, f32[64,512]{1,0:T(8,128)S(1)}, u32[]{:S(2)}, u32[]{:S(2)}) collective-permute-start(f32[64,512]{1,0:T(8,128)S(1)} %get-tuple-element.56.mine_ref), channel_id=1, source_target_pairs={{0,1},{1,0},{2,3},{3,2},{4,5},{5,4},{6,7},{7,6},{8,9},{9,8},{10,11... | collective-permute-start | bytes 393224 | tf_op jit(solution)/shard_map/ppermute | solution.py:257
  131.7 3.7 %collective-permute-start.34 = (f32[32,128]{1,0:T(8,128)S(1)}, f32[32,128]{1,0:T(8,128)S(1)}, u32[]{:S(2)}, u32[]{:S(2)}) collective-permute-start(f32[32,128]{1,0:T(8,128)S(1)} %add.85), channel_id=1, source_target_pairs={{0,8},{4,12},{8,0},{12,4},{16,24},{20,28},{24,16},{28,20},{1,9},{5... | collective-permute-start | bytes 49160 | tf_op jit(solution)/shard_map/ppermute | solution.py:257
  135.4 3.7 %collective-permute-start.35 = (f32[32,128]{1,0:T(8,128)S(1)}, f32[32,128]{1,0:T(8,128)S(1)}, u32[]{:S(2)}, u32[]{:S(2)}) collective-permute-start(f32[32,128]{1,0:T(8,128)S(1)} %add.86), channel_id=1, source_target_pairs={{0,16},{4,20},{8,24},{12,28},{16,0},{20,4},{24,8},{28,12},{1,17},{... | collective-permute-start | bytes 49160 | tf_op jit(solution)/shard_map/ppermute | solution.py:257
  139.2 3.7 %collective-permute-start.36 = (f32[32,128]{1,0:T(8,128)S(1)}, f32[32,128]{1,0:T(8,128)S(1)}, u32[]{:S(2)}, u32[]{:S(2)}) collective-permute-start(f32[32,128]{1,0:T(8,128)S(1)} %add.87), channel_id=1, source_target_pairs={{0,1},{1,0},{2,3},{3,2},{4,5},{5,4},{6,7},{7,6},{8,9},{9,8},{10,11... | collective-permute-start | bytes 49160 | tf_op jit(solution)/shard_map/ppermute | solution.py:257
  (12 other events, 21.4 us)
where the time goes:
time: 146 us
  waiting for transfers between devices  79.7 us (55%)
  starting transfers between devices  44.8 us (31%)
  Pallas kernels  15.5 us (11%)
  local copies, waits for them, and re-layouts  4.5 us (3%)
    ppermute x37, waiting for transfers between devices, swap(): return lax.ppermute(x, axis, [(s, s ^ mask) for s in range(size)])  79.7 us
    ppermute x37, starting transfers between devices, swap(): return lax.ppermute(x, axis, [(s, s ^ mask) for s in range(size)])  39.6 us
    pallas_call x11, Pallas kernels, call(): pl.pallas_call(body, out_shape=[jax.ShapeDtypeStruct(shape, dtype) for sh...  13 us
    all_to_all x1, starting transfers between devices, local(): block = lax.all_to_all(dealt, 'gr', 0, 0).reshape(slab_days, cut)  5.21 us
    unnamed x12, local copies, waits for them, and re-layouts  4.5 us
  transfers between devices with their start and end apart: 38, of which 26 were waited for; matrix products, arithmetic and copies ran while one was open for 0% of the time, Pallas kernels for 4%

commit v1 on v0

--- a/solution.py
+++ b/solution.py
@@ -35,7 +35,7 @@
         out_specs=vmem(len(outs)),
         scratch_shapes=list(scratch),
         cost_estimate=pl.CostEstimate(flops=flops, bytes_accessed=moved, transcendentals=0),
-        compiler_params=pltpu.CompilerParams(vmem_limit_bytes=40 * 1024 * 1024),
+        compiler_params=pltpu.CompilerParams(vmem_limit_bytes=16 * 1024 * 1024),
     )(*scalars, *arrays)
 
 
@@ -175,30 +175,65 @@
     lane_halves(par_ref, full_ref, keep_ref, send_ref)
 
 
-def gram_of(applied):
-    return lax.dot_general(applied, applied, (((1,), (1,)), ((), ())), precision=HIGH, preferred_element_type=F32)
-
-
-def project_body(days_all, scaled, pieces, chunks, par_ref, core_ref, *rest):
+def gram_of(left, right):
+    tall = lax.dot_general(
+        jnp.concatenate(thirds(left), axis=0), jnp.concatenate(thirds(right), axis=0),
+        (((1,), (1,)), ((), ())), preferred_element_type=F32,
+    )
+    rows, cols = left.shape[0], right.shape[0]
+    part = [[tall[i * rows : (i + 1) * rows, k * cols : (k + 1) * cols] for k in range(3)] for i in range(3)]
+    small = (part[0][2] + part[2][0]) + part[1][1]
+    return ((part[2][2] + (part[1][2] + part[2][1])) + small) + (part[0][1] + part[1][0]) + part[0][0]
+
+
+def widen(gram, lanes):
+    return jnp.concatenate([gram, jnp.zeros((gram.shape[0], lanes - gram.shape[1]), F32)], axis=1)
+
+
+def project_both_body(days_all, pieces, chunks, par_ref, core_ref, *rest):
     halves_refs = rest[: 2 * pieces]
     block_refs = rest[2 * pieces : 2 * pieces + chunks]
-    rest = rest[2 * pieces + chunks :]
-    inv_ref, rest = (rest[0], rest[1:]) if scaled else (None, rest)
-    keep_ref, send_ref, full_ref, out_ref = rest
+    *out_refs, full_ref, out_ref = rest[2 * pieces + chunks :]
     start = 0
     for k in range(pieces):
         mine_ref, theirs_ref = halves_refs[2 * k : 2 * k + 2]
         lane_joined(par_ref, mine_ref, theirs_ref, full_ref, start)
         start += 2 * mine_ref.shape[1]
-    factors = full_ref.shape[0]
     applied = full_ref[...] / days_all
-    if scaled:
-        applied = jnp.dot(inv_ref[...], applied, precision=HIGH, preferred_element_type=F32)
+    days = block_refs[0].shape[0]
+    projected = forward_project(applied, block_refs)
+    gram = gram_of(applied, applied)
+    half = out_ref.shape[0]
+    for k in range(2):
+        out_ref[:, :days] = projected[k * half : (k + 1) * half]
+        out_ref[:, days:] = widen(gram[k * half : (k + 1) * half], LANES)
+        halves(core_ref, out_ref, *out_refs[2 * k : 2 * k + 2])
+
+
+def project_lead_body(days_all, par_ref, core_ref, mine_ref, theirs_ref, *rest):
+    *block_refs, inv_ref, keep_ref, send_ref, raw_ref, applied_ref, full_ref, out_ref = rest
+    lane_joined(par_ref, mine_ref, theirs_ref, full_ref)
+    raw = full_ref[...] / days_all
+    half = full_ref.shape[0]
+    applied = jnp.dot(inv_ref[:half, :half], raw, precision=HIGH, preferred_element_type=F32)
+    raw_ref[...] = raw
+    applied_ref[...] = applied
     days = block_refs[0].shape[0]
     out_ref[:, :days] = forward_project(applied, block_refs)
-    out_ref[:, days:] = jnp.concatenate(
-        [gram_of(applied), jnp.zeros((factors, out_ref.shape[1] - days - factors), F32)], axis=1
-    )
+    out_ref[:, days:] = widen(gram_of(applied, applied), LANES)
+    halves(core_ref, out_ref, keep_ref, send_ref)
+
+
+def project_trail_body(days_all, par_ref, core_ref, mine_ref, theirs_ref, raw_ref, lead_ref, *rest):
+    *block_refs, inv_ref, keep_ref, send_ref, full_ref, out_ref = rest
+    lane_joined(par_ref, mine_ref, theirs_ref, full_ref)
+    half = full_ref.shape[0]
+    raw = jnp.concatenate([raw_ref[...], full_ref[...] / days_all], axis=0)
+    applied = jnp.dot(inv_ref[half:, :], raw, precision=HIGH, preferred_element_type=F32)
+    days = block_refs[0].shape[0]
+    out_ref[:, :days] = forward_project(applied, block_refs)
+    both = jnp.concatenate([lead_ref[...], applied], axis=0)
+    out_ref[:, days:] = widen(gram_of(applied, both), LANES)
     halves(core_ref, out_ref, keep_ref, send_ref)
 
 
@@ -223,18 +258,24 @@
     return work[:, size:] / pivots, diag_row
 
 
-def factor_body(days, core_ref, mine_ref, theirs_ref, inv_ref, diag_ref, full_ref):
+def factor_body(days, core_ref, mine_ref, theirs_ref, mine_late_ref, theirs_late_ref, inv_ref, diag_ref, full_ref):
     joined(core_ref, mine_ref, theirs_ref, full_ref)
     size = inv_ref.shape[0]
-    inverse, diag_row = eliminate(full_ref[:, days : days + size])
+    half = size // 2
+    lead = full_ref[:, days : days + half]
+    joined(core_ref, mine_late_ref, theirs_late_ref, full_ref)
+    trail = full_ref[:, days : days + size]
+    top = jnp.concatenate([lead, trail[:, :half].T], axis=1)
+    inverse, diag_row = eliminate(jnp.concatenate([top, trail], axis=0))
     inv_ref[...] = inverse
     diag_ref[...] = diag_row
 
 
-def last_gram_body(days_all, mine_ref, inv_ref, applied_ref, gram_ref):
-    applied = jnp.dot(inv_ref[...], mine_ref[...] / days_all, precision=HIGH, preferred_element_type=F32)
+def last_gram_body(days_all, lead_ref, trail_ref, inv_ref, applied_ref, gram_ref):
+    raw = jnp.concatenate([lead_ref[...], trail_ref[...]], axis=0) / days_all
+    applied = jnp.dot(inv_ref[...], raw, precision=HIGH, preferred_element_type=F32)
     applied_ref[...] = applied
-    gram = gram_of(applied)
+    gram = gram_of(applied, applied)
     half = gram_ref.shape[0]
     gram_ref[...] = jnp.concatenate([gram[:half], gram[half:]], axis=1)
 
@@ -255,6 +296,12 @@
 def swap(x, axis, mask):
     size = lax.axis_size(axis)
     return lax.ppermute(x, axis, [(s, s ^ mask) for s in range(size)])
+
+
+def cross(x, gr_mask, gc_mask):
+    gr, gc = lax.axis_size("gr"), lax.axis_size("gc")
+    pairs = [(g * gc + c, (g ^ gr_mask) * gc + (c ^ gc_mask)) for g in range(gr) for c in range(gc)]
+    return lax.ppermute(x, ("gr", "gc"), pairs)
 
 
 def tree(parts):
@@ -315,10 +362,8 @@
     pieces = [p if m == 0 else swap(p, "gr", m) for m, p in enumerate(pieces)]
 
     asset_half = ((factors, span // 2), F32)
-    day_half = ((half, packed_width), F32)
     full_assets = pltpu.VMEM((factors, span), F32)
     slab = pltpu.VMEM((factors, slab_days), F32)
-    full_days = pltpu.VMEM((factors, packed_width), F32)
 
     shared = [own, twin, *pairs]
     keep, send = call(
@@ -335,42 +380,52 @@
     mine_late = sum_days(keep, send)
     pieces = [mine, theirs, mine_late, swap(mine_late, "gc", 1)]
     block_list = [block, last]
-    inverse = None
+    quarter = ((half // 2, packed_width), F32)
+    rows = ((half, span), F32)
+    part_assets = pltpu.VMEM((half, span), F32)
+    part_days = pltpu.VMEM((half, packed_width), F32)
+    lane_half = ((half, span // 2), F32)
     diagonals = []
     for sweep in range(ITERS - 1):
         if sweep:
-            mine = sum_days(keep, send)
-            pieces = [mine, swap(mine, "gc", 1)]
-        arrays = pieces + block_list + ([] if inverse is None else [inverse])
-        keep, send = call(
-            functools.partial(
-                project_body, days_all, inverse is not None, len(pieces) // 2, len(block_list)
-            ),
-            [day_half] * 2, [par, core], arrays, dots, [full_assets, full_days],
-        )
-        mine, theirs = sum_assets(keep, send)
-        keep, send = call(
-            apply_body, [asset_half] * 2, [core, par], [mine, theirs, *block_list], dots,
-            [full_days, full_assets],
-        )
+            mine = sum_days(*sent[0])
+            keep, send, raw, applied = call(
+                functools.partial(project_lead_body, days_all), [quarter] * 2 + [rows] * 2, [par, core],
+                [mine, swap(mine, "gc", 1), *block_list, inverse], dots // 2, [part_assets, part_days],
+            )
+            lead = sum_assets(keep, send)
+            mine = sum_days(*sent[1])
+            keep, send = call(
+                functools.partial(project_trail_body, days_all), [quarter] * 2, [par, core],
+                [mine, swap(mine, "gc", 1), raw, applied, *block_list, inverse], dots // 2,
+                [part_assets, part_days],
+            )
+            trail = sum_assets(keep, send)
+        else:
+            parts = call(
+                functools.partial(project_both_body, days_all, len(pieces) // 2, len(block_list)),
+                [quarter] * 4, [par, core], pieces + block_list, dots, [full_assets, part_days],
+            )
+            lead = sum_assets(*parts[:2])
+            trail = sum_assets(*parts[2:])
+        sent = [
+            call(apply_body, [lane_half] * 2, [core, par], [*pair, *block_list], dots // 2, [part_days, part_assets])
+            for pair in (lead, trail)
+        ]
         inverse, diag_row = call(
             functools.partial(factor_body, slab_days),
-            [((factors, factors), F32), ((1, factors), F32)], [core], [mine, theirs],
-            dots, [full_days],
+            [((factors, factors), F32), ((1, factors), F32)], [core], [*lead, *trail], dots // 2, [part_days],
         )
         diagonals.append(diag_row)
-    mine = sum_days(keep, send)
+    lead = sum_days(*sent[0])
+    trail = sum_days(*sent[1])
     applied, gram = call(
         functools.partial(last_gram_body, days_all),
-        [asset_half, ((half, 2 * factors), F32)], [], [mine, inverse], dots,
+        [asset_half, ((half, 2 * factors), F32)], [], [lead, trail, inverse], dots,
     )
     theirs = swap(applied, "gc", 1)
-    gram = gram + swap(gram, "gr", 1)
-    mask = 2
-    while mask < blocks:
-        gram = gram + swap(gram, "gr", mask)
-        mask *= 2
-    gram = gram + swap(gram, "gc", 1)
+    gram = (gram + cross(gram, 1, 0)) + (cross(gram, 0, 1) + cross(gram, 1, 1))
+    gram = sum_chips(gram)
     loadings, strengths = call(
         functools.partial(last_body, math.sqrt(assets)),
         [((factors, span), F32), ((ITERS, factors), F32)], [par],

time: 146 us -> 142 us (0.973)
  waiting for transfers between devices: 79.7 us -> 53.9 us
  starting transfers between devices: 44.8 us -> 64.5 us
  Pallas kernels: 15.5 us -> 17.7 us
    ppermute x37 -> x51, waiting for transfers between devices: 79.7 us -> 52 us  [swap(): return lax.ppermute(x, axis, [(s, s ^ mask) for s in range(size)])]
    ppermute x37 -> x51, starting transfers between devices: 39.6 us -> 57.5 us  [swap(): return lax.ppermute(x, axis, [(s, s ^ mask) for s in range(size)])]
    pallas_call x11 -> x14, Pallas kernels: 13 us -> 15.2 us  [call(): pl.pallas_call(body, out_shape=[jax.ShapeDtypeStruct(shape, dtype) for sh...]
    ppermute x0 -> x3, waiting for transfers between devices: none -> 1.96 us  [cross(): return lax.ppermute(x, ('gr', 'gc'), pairs)]
    ppermute x0 -> x3, starting transfers between devices: none -> 1.87 us  [cross(): return lax.ppermute(x, ('gr', 'gc'), pairs)]
  transfers between devices with their start and end apart: 38 -> 55, of which waited for: 26 -> 27; matrix products, arithmetic and copies ran while one was open for 0% -> 0% of each run, Pallas kernels for 4% -> 7%
where the time goes in v1:
time: 142 us
  starting transfers between devices  64.5 us (45%)
  waiting for transfers between devices  53.9 us (38%)
  Pallas kernels  17.7 us (12%)
  local copies, waits for them, and re-layouts  4.5 us (3%)
    ppermute x51, starting transfers between devices, swap(): return lax.ppermute(x, axis, [(s, s ^ mask) for s in range(size)])  57.5 us
    ppermute x51, waiting for transfers between devices, swap(): return lax.ppermute(x, axis, [(s, s ^ mask) for s in range(size)])  52 us
    pallas_call x14, Pallas kernels, call(): pl.pallas_call(body, out_shape=[jax.ShapeDtypeStruct(shape, dtype) for sh...  15.2 us
    all_to_all x1, starting transfers between devices, local(): block = lax.all_to_all(dealt, 'gr', 0, 0).reshape(slab_days, cut)  5.21 us
    unnamed x12, local copies, waits for them, and re-layouts  4.5 us
  transfers between devices with their start and end apart: 55, of which 27 were waited for; matrix products, arithmetic and copies ran while one was open for 0% of the time, Pallas kernels for 7%

profile of v1, /device:TPU:0, one launch (start us, length us, event | category | flops | bytes accessed | tf_op | source)
XLA Modules:
  0.0 141.8 jit_solution(11210504419818959116)
XLA Ops:
  0.6 2.5 %shard_map.42 = bf16[8,128,512]{2,1,0:T(8,128)(2,1)} custom-call(bf16[128,8192]{1,0:T(8,128)(2,1)} %returns_ref.3), custom_call_target="tpu_custom_call" | custom-call | tf_op jit(solution)/shard_map/pallas_call | solution.py:68
  3.1 5.2 %all-to-all-start = ((bf16[8,128,512]{2,1,0:T(8,128)(2,1)}), bf16[8,128,512]{2,1,0:T(8,128)(2,1)S(1)}, u32[]{:S(2)}, u32[]{:S(2)}) async-start(bf16[8,128,512]{2,1,0:T(8,128)(2,1)} %shard_map.42), calls=%async_computation | async-start | bytes 2097152 | tf_op jit(solution)/shard_map/all_to_all | solution.py:353
  13.5 1.8 %collective-permute-start.1 = (f32[2,64,128]{2,1,0:T(8,128)S(1)}, f32[2,64,128]{2,1,0:T(8,128)S(1)}, u32[]{:S(2)}, u32[]{:S(2)}) collective-permute-start(f32[2,64,128]{2,1,0:T(8,128)S(1)} %pad_maximum_fusion), channel_id=1, source_target_pairs={{0,8},{4,12},{8,0},{12,4},{16,24},{20,28},{24,16},{28,20},{1,9},{5... | collective-permute-start | bytes 196616 | tf_op jit(solution)/shard_map/ppermute | solution.py:298
  17.1 7.8 %collective-permute-done.1.rest_0_ = f32[2,64,128]{2,1,0:T(8,128)S(1)} collective-permute-done((f32[2,64,128]{2,1,0:T(8,128)S(1)}, f32[2,64,128]{2,1,0:T(8,128)S(1)}, u32[]{:S(2)}, u32[]{:S(2)}) %collective-permute-start.1) | collective-permute-done | bytes 65568 | tf_op jit(solution)/shard_map/ppermute | solution.py:298
  26.3 7.7 %collective-permute-done.2.rest_1_ = f32[2,64,128]{2,1,0:T(8,128)S(1)} collective-permute-done((f32[2,64,128]{2,1,0:T(8,128)S(1)}, f32[2,64,128]{2,1,0:T(8,128)S(1)}, u32[]{:S(2)}, u32[]{:S(2)}) %collective-permute-start.2) | collective-permute-done | bytes 65568 | tf_op jit(solution)/shard_map/ppermute | solution.py:298
  38.1 3.2 %collective-permute-done.13.rest_10_ = bf16[128,512]{1,0:T(8,128)(2,1)S(1)} collective-permute-done((bf16[128,512]{1,0:T(8,128)(2,1)}, bf16[128,512]{1,0:T(8,128)(2,1)S(1)}, u32[]{:S(2)}, u32[]{:S(2)}) %collective-permute-start.13) | collective-permute-done | bytes 131104 | tf_op jit(solution)/shard_map/ppermute | solution.py:298
  41.3 2.2 %collective-permute-done.8.rest_5_ = bf16[128,512]{1,0:T(8,128)(2,1)S(1)} collective-permute-done((bf16[128,512]{1,0:T(8,128)(2,1)}, bf16[128,512]{1,0:T(8,128)(2,1)S(1)}, u32[]{:S(2)}, u32[]{:S(2)}) %collective-permute-start.8) | collective-permute-done | bytes 131104 | tf_op jit(solution)/shard_map/ppermute | solution.py:298
  43.5 2.4 %collective-permute-done.9.rest_6_ = bf16[128,512]{1,0:T(8,128)(2,1)S(1)} collective-permute-done((bf16[128,512]{1,0:T(8,128)(2,1)S(1)}, bf16[128,512]{1,0:T(8,128)(2,1)S(1)}, u32[]{:S(2)}, u32[]{:S(2)}) %collective-permute-start.9) | collective-permute-done | bytes 131104 | tf_op jit(solution)/shard_map/ppermute | solution.py:298
  51.2 2.0 %collective-permute-done.14 = f32[64,256]{1,0:T(8,128)S(1)} collective-permute-done((f32[64,256]{1,0:T(8,128)}, f32[64,256]{1,0:T(8,128)S(1)}, u32[]{:S(2)}, u32[]{:S(2)}) %collective-permute-start.14) | collective-permute-done | bytes 65568 | tf_op jit(solution)/shard_map/ppermute | solution.py:298
  53.2 2.7 %collective-permute-start.15 = (f32[64,256]{1,0:T(8,128)S(1)}, f32[64,256]{1,0:T(8,128)S(1)}, u32[]{:S(2)}, u32[]{:S(2)}) collective-permute-start(f32[64,256]{1,0:T(8,128)S(1)} %add.113), channel_id=1, source_target_pairs={{0,2},{1,3},{2,0},{3,1},{4,6},{5,7},{6,4},{7,5},{8,10},{9,11},{10,... | collective-permute-start | bytes 196616 | tf_op jit(solution)/shard_map/ppermute | solution.py:298
  55.9 2.1 %collective-permute-start.5 = (f32[64,256]{1,0:T(8,128)S(1)}, f32[64,256]{1,0:T(8,128)S(1)}, u32[]{:S(2)}, u32[]{:S(2)}) collective-permute-start(f32[64,256]{1,0:T(8,128)S(1)} %add.111), channel_id=1, source_target_pairs={{0,2},{1,3},{2,0},{3,1},{4,6},{5,7},{6,4},{7,5},{8,10},{9,11},{10,... | collective-permute-start | bytes 196616 | tf_op jit(solution)/shard_map/ppermute | solution.py:298
  58.7 2.4 %collective-permute-start.16 = (f32[64,256]{1,0:T(8,128)S(1)}, f32[64,256]{1,0:T(8,128)S(1)}, u32[]{:S(2)}, u32[]{:S(2)}) collective-permute-start(f32[64,256]{1,0:T(8,128)S(1)} %add.114.rest_2_), channel_id=1, source_target_pairs={{0,1},{1,0},{2,3},{3,2},{4,5},{5,4},{6,7},{7,6},{8,9},{9,8},{10,11... | collective-permute-start | bytes 196616 | tf_op jit(solution)/shard_map/ppermute | solution.py:298
  61.2 2.2 %collective-permute-start.6 = (f32[64,256]{1,0:T(8,128)S(1)}, f32[64,256]{1,0:T(8,128)S(1)}, u32[]{:S(2)}, u32[]{:S(2)}) collective-permute-start(f32[64,256]{1,0:T(8,128)S(1)} %add.112.rest_0_), channel_id=1, source_target_pairs={{0,1},{1,0},{2,3},{3,2},{4,5},{5,4},{6,7},{7,6},{8,9},{9,8},{10,11... | collective-permute-start | bytes 196616 | tf_op jit(solution)/shard_map/ppermute | solution.py:298
  63.4 2.2 %collective-permute-done.6.rest_1_ = f32[64,256]{1,0:T(8,128)S(1)} collective-permute-done((f32[64,256]{1,0:T(8,128)S(1)}, f32[64,256]{1,0:T(8,128)S(1)}, u32[]{:S(2)}, u32[]{:S(2)}) %collective-permute-start.6) | collective-permute-done | bytes 65568 | tf_op jit(solution)/shard_map/ppermute | solution.py:298
  69.5 1.6 %collective-permute-start.19 = (f32[16,1152]{1,0:T(8,128)S(1)}, f32[16,1152]{1,0:T(8,128)S(1)}, u32[]{:S(2)}, u32[]{:S(2)}) collective-permute-start(f32[16,1152]{1,0:T(8,128)S(1)} %add.115), channel_id=1, source_target_pairs={{0,16},{4,20},{8,24},{12,28},{16,0},{20,4},{24,8},{28,12},{1,17},{... | collective-permute-start | bytes 221192 | tf_op jit(solution)/shard_map/ppermute | solution.py:298
  73.1 1.6 %collective-permute-start.27 = (f32[16,1152]{1,0:T(8,128)S(1)}, f32[16,1152]{1,0:T(8,128)S(1)}, u32[]{:S(2)}, u32[]{:S(2)}) collective-permute-start(f32[16,1152]{1,0:T(8,128)S(1)} %add.121), channel_id=1, source_target_pairs={{0,16},{4,20},{8,24},{12,28},{16,0},{20,4},{24,8},{28,12},{1,17},{... | collective-permute-start | bytes 221192 | tf_op jit(solution)/shard_map/ppermute | solution.py:298
  77.9 2.1 %collective-permute-done.28 = f32[16,1152]{1,0:T(8,128)S(1)} collective-permute-done((f32[16,1152]{1,0:T(8,128)S(1)}, f32[16,1152]{1,0:T(8,128)S(1)}, u32[]{:S(2)}, u32[]{:S(2)}) %collective-permute-start.28) | collective-permute-done | bytes 73760 | tf_op jit(solution)/shard_map/ppermute | solution.py:298
  80.6 2.1 %collective-permute-start.22 = (f32[32,512]{1,0:T(8,128)S(1)}, f32[32,512]{1,0:T(8,128)S(1)}, u32[]{:S(2)}, u32[]{:S(2)}) collective-permute-start(f32[32,512]{1,0:T(8,128)S(1)} %get-tuple-element.59), channel_id=1, source_target_pairs={{0,1},{1,0},{2,3},{3,2},{4,5},{5,4},{6,7},{7,6},{8,9},{9,8},{10,11... | collective-permute-start | bytes 196616 | tf_op jit(solution)/shard_map/ppermute | solution.py:298
  85.4 3.9 %collective-permute-start.23 = (f32[32,512]{1,0:T(8,128)S(1)}, f32[32,512]{1,0:T(8,128)S(1)}, u32[]{:S(2)}, u32[]{:S(2)}) collective-permute-start(f32[32,512]{1,0:T(8,128)S(1)} %add.119), channel_id=1, source_target_pairs={{0,2},{1,3},{2,0},{3,1},{4,6},{5,7},{6,4},{7,5},{8,10},{9,11},{10,... | collective-permute-start | bytes 196616 | tf_op jit(solution)/shard_map/ppermute | solution.py:298
  91.7 2.2 %collective-permute-start.24 = (f32[32,512]{1,0:T(8,128)S(1)}, f32[32,512]{1,0:T(8,128)S(1)}, u32[]{:S(2)}, u32[]{:S(2)}) collective-permute-start(f32[32,512]{1,0:T(8,128)S(1)} %add.120.mine_ref), channel_id=1, source_target_pairs={{0,1},{1,0},{2,3},{3,2},{4,5},{5,4},{6,7},{7,6},{8,9},{9,8},{10,11... | collective-permute-start | bytes 196616 | tf_op jit(solution)/shard_map/ppermute | solution.py:298
  95.2 1.8 %shard_map.47 = (f32[64,64]{1,0:T(8,128)S(1)}, f32[1,64]{1,0:T(1,128)S(1)}) custom-call(s32[1]{0:T(128)} %bitcast.1.core_ref, f32[16,1152]{1,0:T(8,128)S(1)} %add_add_fusion.3.mine_ref, f32[16,1152]{1,0:T(8,128)S(1)} %collective-permute-done.21.theirs_ref, f32[16,1152]{1,0:T(8,128)S(1)} %add_add_fusion.2.mine_late_ref.mine_ref, ...), custom_call_target="tpu_custom_call" | custom-call | flops 201326592 | bytes 16640 | tf_op jit(solution)/shard_map/pallas_call | solution.py:31
  103.2 2.4 %collective-permute-start.43 = (f32[16,1152]{1,0:T(8,128)S(1)}, f32[16,1152]{1,0:T(8,128)S(1)}, u32[]{:S(2)}, u32[]{:S(2)}) collective-permute-start(f32[16,1152]{1,0:T(8,128)S(1)} %add.133), channel_id=1, source_target_pairs={{0,24},{4,28},{8,16},{12,20},{16,8},{20,12},{24,0},{28,4},{1,25},{... | collective-permute-start | bytes 221192 | tf_op jit(solution)/shard_map/ppermute | solution.py:298
  106.8 2.4 %collective-permute-start.33 = (f32[16,1152]{1,0:T(8,128)S(1)}, f32[16,1152]{1,0:T(8,128)S(1)}, u32[]{:S(2)}, u32[]{:S(2)}) collective-permute-start(f32[16,1152]{1,0:T(8,128)S(1)} %add.125), channel_id=1, source_target_pairs={{0,24},{4,28},{8,16},{12,20},{16,8},{20,12},{24,0},{28,4},{1,25},{... | collective-permute-start | bytes 221192 | tf_op jit(solution)/shard_map/ppermute | solution.py:298
  115.3 2.3 %collective-permute-done.45 = f32[32,512]{1,0:T(8,128)S(1)} collective-permute-done((f32[32,512]{1,0:T(8,128)S(1)}, f32[32,512]{1,0:T(8,128)S(1)}, u32[]{:S(2)}, u32[]{:S(2)}) %collective-permute-start.45) | collective-permute-done | bytes 65568 | tf_op jit(solution)/shard_map/ppermute | solution.py:298
  117.6 2.0 %collective-permute-start.46 = (f32[32,512]{1,0:T(8,128)S(1)}, f32[32,512]{1,0:T(8,128)S(1)}, u32[]{:S(2)}, u32[]{:S(2)}) collective-permute-start(f32[32,512]{1,0:T(8,128)S(1)} %add.137), channel_id=1, source_target_pairs={{0,2},{1,3},{2,0},{3,1},{4,6},{5,7},{6,4},{7,5},{8,10},{9,11},{10,... | collective-permute-start | bytes 196616 | tf_op jit(solution)/shard_map/ppermute | solution.py:298
  120.9 1.8 %shard_map.53 = (f32[64,64]{1,0:T(8,128)S(1)}, f32[1,64]{1,0:T(1,128)S(1)}) custom-call(s32[1]{0:T(128)} %bitcast.1.core_ref, f32[16,1152]{1,0:T(8,128)S(1)} %add_add_fusion.1.mine_ref, f32[16,1152]{1,0:T(8,128)S(1)} %collective-permute-done.34.theirs_ref, f32[16,1152]{1,0:T(8,128)S(1)} %add_add_fusion.mine_ref.mine_late_ref, ...), custom_call_target="tpu_custom_call" | custom-call | flops 201326592 | bytes 16640 | tf_op jit(solution)/shard_map/pallas_call | solution.py:31
  122.8 1.9 %collective-permute-done.46 = f32[32,512]{1,0:T(8,128)S(1)} collective-permute-done((f32[32,512]{1,0:T(8,128)S(1)}, f32[32,512]{1,0:T(8,128)S(1)}, u32[]{:S(2)}, u32[]{:S(2)}) %collective-permute-start.46) | collective-permute-done | bytes 65568 | tf_op jit(solution)/shard_map/ppermute | solution.py:298
  126.9 1.8 %collective-permute-start.50 = (f32[32,128]{1,0:T(8,128)S(1)}, f32[32,128]{1,0:T(8,128)S(1)}, u32[]{:S(2)}, u32[]{:S(2)}) collective-permute-start(f32[32,128]{1,0:T(8,128)S(1)} %get-tuple-element.77), channel_id=1, source_target_pairs={{0,5},{1,4},{2,7},{3,6},{4,1},{5,0},{6,3},{7,2},{8,13},{9,12},{10,... | collective-permute-start | bytes 49160 | tf_op jit(solution)/shard_map/ppermute | solution.py:304
  128.7 2.0 %collective-permute-done.49 = f32[32,128]{1,0:T(8,128)S(1)} collective-permute-done((f32[32,128]{1,0:T(8,128)S(1)}, f32[32,128]{1,0:T(8,128)S(1)}, u32[]{:S(2)}, u32[]{:S(2)}) %collective-permute-start.49) | collective-permute-done | bytes 16416 | tf_op jit(solution)/shard_map/ppermute | solution.py:304
  132.0 1.6 %collective-permute-start.52 = (f32[32,128]{1,0:T(8,128)S(1)}, f32[32,128]{1,0:T(8,128)S(1)}, u32[]{:S(2)}, u32[]{:S(2)}) collective-permute-start(f32[32,128]{1,0:T(8,128)S(1)} %add_add_fusion.5), channel_id=1, source_target_pairs={{0,16},{4,20},{8,24},{12,28},{16,0},{20,4},{24,8},{28,12},{1,17},{... | collective-permute-start | bytes 49160 | tf_op jit(solution)/shard_map/ppermute | solution.py:298
  135.7 2.5 %collective-permute-done.53 = f32[32,128]{1,0:T(8,128)S(1)} collective-permute-done((f32[32,128]{1,0:T(8,128)S(1)}, f32[32,128]{1,0:T(8,128)S(1)}, u32[]{:S(2)}, u32[]{:S(2)}) %collective-permute-start.53) | collective-permute-done | bytes 16416 | tf_op jit(solution)/shard_map/ppermute | solution.py:298
  139.1 2.7 %shard_map.55 = (f32[64,1024]{1,0:T(8,128)}, f32[3,64]{1,0:T(4,128)}) custom-call(s32[1]{0:T(128)} %bitcast.par_ref, f32[64,512]{1,0:T(8,128)S(1)} %get-tuple-element.76.mine_ref, f32[64,512]{1,0:T(8,128)S(1)} %collective-permute-done.47.theirs_ref, f32[32,128]{1,0:T(8,128)S(1)} %add_add_fusion.4.gram_ref, f32[1,64]{1,0:T(1,128)S(1)} %get-tuple-element.78.rest_0_, ...), custom_call_target="tpu_custom_call" | custom-call | flops 402653184 | bytes 262912 | tf_op jit(solution)/shard_map/pallas_call | solution.py:31
  (128 shorter events, 55.8 us)
Async XLA Ops:
  3.1 47.1 %all-to-all-start = ((bf16[8,128,512]{2,1,0:T(8,128)(2,1)}), bf16[8,128,512]{2,1,0:T(8,128)(2,1)S(1)}, u32[]{:S(2)}, u32[]{:S(2)}) async-start(bf16[8,128,512]{2,1,0:T(8,128)(2,1)} %shard_map.42), calls=%async_computation | async-start | bytes 2097152 | tf_op jit(solution)/shard_map/all_to_all | solution.py:353
  11.9 24.8 %collective-permute-start.10 = (bf16[128,512]{1,0:T(8,128)(2,1)S(1)}, bf16[128,512]{1,0:T(8,128)(2,1)S(1)}, u32[]{:S(2)}, u32[]{:S(2)}) collective-permute-start(bf16[128,512]{1,0:T(8,128)(2,1)S(1)} %get-tuple-element.49), channel_id=1, source_target_pairs={{0,16},{4,20},{8,24},{12,28},{16,0},{20,4},{24,8},{28,12},{1,17},{... | collective-permute-start | bytes 393224 | tf_op jit(solution)/shard_map/ppermute | solution.py:298
  13.5 23.7 %collective-permute-start.11 = (bf16[128,512]{1,0:T(8,128)(2,1)S(1)}, bf16[128,512]{1,0:T(8,128)(2,1)S(1)}, u32[]{:S(2)}, u32[]{:S(2)}) collective-permute-start(bf16[128,512]{1,0:T(8,128)(2,1)S(1)} %get-tuple-element.50), channel_id=1, source_target_pairs={{0,20},{4,16},{8,28},{12,24},{16,4},{20,0},{24,12},{28,8},{1,21},{... | collective-permute-start | bytes 393224 | tf_op jit(solution)/shard_map/ppermute | solution.py:298
  13.5 11.3 %collective-permute-start.1 = (f32[2,64,128]{2,1,0:T(8,128)S(1)}, f32[2,64,128]{2,1,0:T(8,128)S(1)}, u32[]{:S(2)}, u32[]{:S(2)}) collective-permute-start(f32[2,64,128]{2,1,0:T(8,128)S(1)} %pad_maximum_fusion), channel_id=1, source_target_pairs={{0,8},{4,12},{8,0},{12,4},{16,24},{20,28},{24,16},{28,20},{1,9},{5... | collective-permute-start | bytes 196616 | tf_op jit(solution)/shard_map/ppermute | solution.py:298
  15.3 18.7 %collective-permute-start.2 = (f32[2,64,128]{2,1,0:T(8,128)S(1)}, f32[2,64,128]{2,1,0:T(8,128)S(1)}, u32[]{:S(2)}, u32[]{:S(2)}) collective-permute-start(f32[2,64,128]{2,1,0:T(8,128)S(1)} %pad_maximum_fusion), channel_id=1, source_target_pairs={{0,16},{4,20},{8,24},{12,28},{16,0},{20,4},{24,8},{28,12},{1,17},{... | collective-permute-start | bytes 196616 | tf_op jit(solution)/shard_map/ppermute | solution.py:298
  16.8 18.8 %collective-permute-start.3 = (f32[2,64,128]{2,1,0:T(8,128)S(1)}, f32[2,64,128]{2,1,0:T(8,128)S(1)}, u32[]{:S(2)}, u32[]{:S(2)}) collective-permute-start(f32[2,64,128]{2,1,0:T(8,128)S(1)} %pad_maximum_fusion), channel_id=1, source_target_pairs={{0,24},{4,28},{8,16},{12,20},{16,8},{20,12},{24,0},{28,4},{1,25},{... | collective-permute-start | bytes 196616 | tf_op jit(solution)/shard_map/ppermute | solution.py:298
  24.8 13.2 %collective-permute-start.12 = (bf16[128,512]{1,0:T(8,128)(2,1)}, bf16[128,512]{1,0:T(8,128)(2,1)S(1)}, u32[]{:S(2)}, u32[]{:S(2)}) collective-permute-start(bf16[128,512]{1,0:T(8,128)(2,1)} %get-tuple-element.51), channel_id=1, source_target_pairs={{0,24},{4,28},{8,16},{12,20},{16,8},{20,12},{24,0},{28,4},{1,25},{... | collective-permute-start | bytes 393224 | tf_op jit(solution)/shard_map/ppermute | solution.py:298
  34.6 6.6 %collective-permute-start.13 = (bf16[128,512]{1,0:T(8,128)(2,1)}, bf16[128,512]{1,0:T(8,128)(2,1)S(1)}, u32[]{:S(2)}, u32[]{:S(2)}) collective-permute-start(bf16[128,512]{1,0:T(8,128)(2,1)} %get-tuple-element.52), channel_id=1, source_target_pairs={{0,28},{4,24},{8,20},{12,16},{16,12},{20,8},{24,4},{28,0},{1,29},{... | collective-permute-start | bytes 393224 | tf_op jit(solution)/shard_map/ppermute | solution.py:298
  36.2 5.1 %collective-permute-start.7 = (bf16[128,512]{1,0:T(8,128)(2,1)}, bf16[128,512]{1,0:T(8,128)(2,1)S(1)}, u32[]{:S(2)}, u32[]{:S(2)}) collective-permute-start(bf16[128,512]{1,0:T(8,128)(2,1)} %get-tuple-element.46), channel_id=1, source_target_pairs={{0,4},{4,0},{8,12},{12,8},{16,20},{20,16},{24,28},{28,24},{1,5},{5... | collective-permute-start | bytes 393224 | tf_op jit(solution)/shard_map/ppermute | solution.py:298
  36.7 6.8 %collective-permute-start.8 = (bf16[128,512]{1,0:T(8,128)(2,1)}, bf16[128,512]{1,0:T(8,128)(2,1)S(1)}, u32[]{:S(2)}, u32[]{:S(2)}) collective-permute-start(bf16[128,512]{1,0:T(8,128)(2,1)} %get-tuple-element.47), channel_id=1, source_target_pairs={{0,8},{4,12},{8,0},{12,4},{16,24},{20,28},{24,16},{28,20},{1,9},{5... | collective-permute-start | bytes 393224 | tf_op jit(solution)/shard_map/ppermute | solution.py:298
  37.2 8.7 %collective-permute-start.9 = (bf16[128,512]{1,0:T(8,128)(2,1)S(1)}, bf16[128,512]{1,0:T(8,128)(2,1)S(1)}, u32[]{:S(2)}, u32[]{:S(2)}) collective-permute-start(bf16[128,512]{1,0:T(8,128)(2,1)S(1)} %get-tuple-element.48), channel_id=1, source_target_pairs={{0,12},{4,8},{8,4},{12,0},{16,28},{20,24},{24,20},{28,16},{1,13},{... | collective-permute-start | bytes 393224 | tf_op jit(solution)/shard_map/ppermute | solution.py:298
  50.7 5.2 %collective-permute-start.4 = (f32[64,256]{1,0:T(8,128)S(1)}, f32[64,256]{1,0:T(8,128)S(1)}, u32[]{:S(2)}, u32[]{:S(2)}) collective-permute-start(f32[64,256]{1,0:T(8,128)S(1)} %get-tuple-element.44), channel_id=1, source_target_pairs={{0,1},{1,0},{2,3},{3,2},{4,5},{5,4},{6,7},{7,6},{8,9},{9,8},{10,11... | collective-permute-start | bytes 196616 | tf_op jit(solution)/shard_map/ppermute | solution.py:298
  53.2 5.6 %collective-permute-start.15 = (f32[64,256]{1,0:T(8,128)S(1)}, f32[64,256]{1,0:T(8,128)S(1)}, u32[]{:S(2)}, u32[]{:S(2)}) collective-permute-start(f32[64,256]{1,0:T(8,128)S(1)} %add.113), channel_id=1, source_target_pairs={{0,2},{1,3},{2,0},{3,1},{4,6},{5,7},{6,4},{7,5},{8,10},{9,11},{10,... | collective-permute-start | bytes 196616 | tf_op jit(solution)/shard_map/ppermute | solution.py:298
  55.9 5.4 %collective-permute-start.5 = (f32[64,256]{1,0:T(8,128)S(1)}, f32[64,256]{1,0:T(8,128)S(1)}, u32[]{:S(2)}, u32[]{:S(2)}) collective-permute-start(f32[64,256]{1,0:T(8,128)S(1)} %add.111), channel_id=1, source_target_pairs={{0,2},{1,3},{2,0},{3,1},{4,6},{5,7},{6,4},{7,5},{8,10},{9,11},{10,... | collective-permute-start | bytes 196616 | tf_op jit(solution)/shard_map/ppermute | solution.py:298
  68.1 6.7 %collective-permute-start.18 = (f32[16,1152]{1,0:T(8,128)S(1)}, f32[16,1152]{1,0:T(8,128)S(1)}, u32[]{:S(2)}, u32[]{:S(2)}) collective-permute-start(f32[16,1152]{1,0:T(8,128)S(1)} %add.115), channel_id=1, source_target_pairs={{0,8},{4,12},{8,0},{12,4},{16,24},{20,28},{24,16},{28,20},{1,9},{5... | collective-permute-start | bytes 221192 | tf_op jit(solution)/shard_map/ppermute | solution.py:298
  69.5 5.8 %collective-permute-start.19 = (f32[16,1152]{1,0:T(8,128)S(1)}, f32[16,1152]{1,0:T(8,128)S(1)}, u32[]{:S(2)}, u32[]{:S(2)}) collective-permute-start(f32[16,1152]{1,0:T(8,128)S(1)} %add.115), channel_id=1, source_target_pairs={{0,16},{4,20},{8,24},{12,28},{16,0},{20,4},{24,8},{28,12},{1,17},{... | collective-permute-start | bytes 221192 | tf_op jit(solution)/shard_map/ppermute | solution.py:298
  71.2 5.5 %collective-permute-start.20 = (f32[16,1152]{1,0:T(8,128)S(1)}, f32[16,1152]{1,0:T(8,128)S(1)}, u32[]{:S(2)}, u32[]{:S(2)}) collective-permute-start(f32[16,1152]{1,0:T(8,128)S(1)} %add.115), channel_id=1, source_target_pairs={{0,24},{4,28},{8,16},{12,20},{16,8},{20,12},{24,0},{28,4},{1,25},{... | collective-permute-start | bytes 221192 | tf_op jit(solution)/shard_map/ppermute | solution.py:298
  71.6 5.1 %collective-permute-start.26 = (f32[16,1152]{1,0:T(8,128)S(1)}, f32[16,1152]{1,0:T(8,128)S(1)}, u32[]{:S(2)}, u32[]{:S(2)}) collective-permute-start(f32[16,1152]{1,0:T(8,128)S(1)} %add.121), channel_id=1, source_target_pairs={{0,8},{4,12},{8,0},{12,4},{16,24},{20,28},{24,16},{28,20},{1,9},{5... | collective-permute-start | bytes 221192 | tf_op jit(solution)/shard_map/ppermute | solution.py:298
  74.7 5.3 %collective-permute-start.28 = (f32[16,1152]{1,0:T(8,128)S(1)}, f32[16,1152]{1,0:T(8,128)S(1)}, u32[]{:S(2)}, u32[]{:S(2)}) collective-permute-start(f32[16,1152]{1,0:T(8,128)S(1)} %add.121), channel_id=1, source_target_pairs={{0,24},{4,28},{8,16},{12,20},{16,8},{20,12},{24,0},{28,4},{1,25},{... | collective-permute-start | bytes 221192 | tf_op jit(solution)/shard_map/ppermute | solution.py:298
  83.2 6.1 %collective-permute-start.37 = (f32[32,512]{1,0:T(8,128)S(1)}, f32[32,512]{1,0:T(8,128)S(1)}, u32[]{:S(2)}, u32[]{:S(2)}) collective-permute-start(f32[32,512]{1,0:T(8,128)S(1)} %get-tuple-element.68), channel_id=1, source_target_pairs={{0,1},{1,0},{2,3},{3,2},{4,5},{5,4},{6,7},{7,6},{8,9},{9,8},{10,11... | collective-permute-start | bytes 196616 | tf_op jit(solution)/shard_map/ppermute | solution.py:298
  85.4 6.2 %collective-permute-start.23 = (f32[32,512]{1,0:T(8,128)S(1)}, f32[32,512]{1,0:T(8,128)S(1)}, u32[]{:S(2)}, u32[]{:S(2)}) collective-permute-start(f32[32,512]{1,0:T(8,128)S(1)} %add.119), channel_id=1, source_target_pairs={{0,2},{1,3},{2,0},{3,1},{4,6},{5,7},{6,4},{7,5},{8,10},{9,11},{10,... | collective-permute-start | bytes 196616 | tf_op jit(solution)/shard_map/ppermute | solution.py:298
  89.3 5.8 %collective-permute-start.38 = (f32[32,512]{1,0:T(8,128)S(1)}, f32[32,512]{1,0:T(8,128)S(1)}, u32[]{:S(2)}, u32[]{:S(2)}) collective-permute-start(f32[32,512]{1,0:T(8,128)S(1)} %add.131), channel_id=1, source_target_pairs={{0,2},{1,3},{2,0},{3,1},{4,6},{5,7},{6,4},{7,5},{8,10},{9,11},{10,... | collective-permute-start | bytes 196616 | tf_op jit(solution)/shard_map/ppermute | solution.py:298
  91.7 5.4 %collective-permute-start.24 = (f32[32,512]{1,0:T(8,128)S(1)}, f32[32,512]{1,0:T(8,128)S(1)}, u32[]{:S(2)}, u32[]{:S(2)}) collective-permute-start(f32[32,512]{1,0:T(8,128)S(1)} %add.120.mine_ref), channel_id=1, source_target_pairs={{0,1},{1,0},{2,3},{3,2},{4,5},{5,4},{6,7},{7,6},{8,9},{9,8},{10,11... | collective-permute-start | bytes 196616 | tf_op jit(solution)/shard_map/ppermute | solution.py:298
  102.3 6.8 %collective-permute-start.42 = (f32[16,1152]{1,0:T(8,128)S(1)}, f32[16,1152]{1,0:T(8,128)S(1)}, u32[]{:S(2)}, u32[]{:S(2)}) collective-permute-start(f32[16,1152]{1,0:T(8,128)S(1)} %add.133), channel_id=1, source_target_pairs={{0,16},{4,20},{8,24},{12,28},{16,0},{20,4},{24,8},{28,12},{1,17},{... | collective-permute-start | bytes 221192 | tf_op jit(solution)/shard_map/ppermute | solution.py:298
  103.2 6.0 %collective-permute-start.43 = (f32[16,1152]{1,0:T(8,128)S(1)}, f32[16,1152]{1,0:T(8,128)S(1)}, u32[]{:S(2)}, u32[]{:S(2)}) collective-permute-start(f32[16,1152]{1,0:T(8,128)S(1)} %add.133), channel_id=1, source_target_pairs={{0,24},{4,28},{8,16},{12,20},{16,8},{20,12},{24,0},{28,4},{1,25},{... | collective-permute-start | bytes 221192 | tf_op jit(solution)/shard_map/ppermute | solution.py:298
  106.8 5.3 %collective-permute-start.33 = (f32[16,1152]{1,0:T(8,128)S(1)}, f32[16,1152]{1,0:T(8,128)S(1)}, u32[]{:S(2)}, u32[]{:S(2)}) collective-permute-start(f32[16,1152]{1,0:T(8,128)S(1)} %add.125), channel_id=1, source_target_pairs={{0,24},{4,28},{8,16},{12,20},{16,8},{20,12},{24,0},{28,4},{1,25},{... | collective-permute-start | bytes 221192 | tf_op jit(solution)/shard_map/ppermute | solution.py:298
  112.6 5.0 %collective-permute-start.45 = (f32[32,512]{1,0:T(8,128)S(1)}, f32[32,512]{1,0:T(8,128)S(1)}, u32[]{:S(2)}, u32[]{:S(2)}) collective-permute-start(f32[32,512]{1,0:T(8,128)S(1)} %get-tuple-element.74), channel_id=1, source_target_pairs={{0,1},{1,0},{2,3},{3,2},{4,5},{5,4},{6,7},{7,6},{8,9},{9,8},{10,11... | collective-permute-start | bytes 196616 | tf_op jit(solution)/shard_map/ppermute | solution.py:298
  113.9 5.7 %collective-permute-start.35 = (f32[32,512]{1,0:T(8,128)S(1)}, f32[32,512]{1,0:T(8,128)S(1)}, u32[]{:S(2)}, u32[]{:S(2)}) collective-permute-start(f32[32,512]{1,0:T(8,128)S(1)} %get-tuple-element.66), channel_id=1, source_target_pairs={{0,1},{1,0},{2,3},{3,2},{4,5},{5,4},{6,7},{7,6},{8,9},{9,8},{10,11... | collective-permute-start | bytes 196616 | tf_op jit(solution)/shard_map/ppermute | solution.py:298
  117.6 7.1 %collective-permute-start.46 = (f32[32,512]{1,0:T(8,128)S(1)}, f32[32,512]{1,0:T(8,128)S(1)}, u32[]{:S(2)}, u32[]{:S(2)}) collective-permute-start(f32[32,512]{1,0:T(8,128)S(1)} %add.137), channel_id=1, source_target_pairs={{0,2},{1,3},{2,0},{3,1},{4,6},{5,7},{6,4},{7,5},{8,10},{9,11},{10,... | collective-permute-start | bytes 196616 | tf_op jit(solution)/shard_map/ppermute | solution.py:298
  119.6 6.5 %collective-permute-start.36 = (f32[32,512]{1,0:T(8,128)S(1)}, f32[32,512]{1,0:T(8,128)S(1)}, u32[]{:S(2)}, u32[]{:S(2)}) collective-permute-start(f32[32,512]{1,0:T(8,128)S(1)} %add.129), channel_id=1, source_target_pairs={{0,2},{1,3},{2,0},{3,1},{4,6},{5,7},{6,4},{7,5},{8,10},{9,11},{10,... | collective-permute-start | bytes 196616 | tf_op jit(solution)/shard_map/ppermute | solution.py:298
  130.6 5.0 %collective-permute-start.51 = (f32[32,128]{1,0:T(8,128)S(1)}, f32[32,128]{1,0:T(8,128)S(1)}, u32[]{:S(2)}, u32[]{:S(2)}) collective-permute-start(f32[32,128]{1,0:T(8,128)S(1)} %add_add_fusion.5), channel_id=1, source_target_pairs={{0,8},{4,12},{8,0},{12,4},{16,24},{20,28},{24,16},{28,20},{1,9},{5... | collective-permute-start | bytes 49160 | tf_op jit(solution)/shard_map/ppermute | solution.py:298
  134.2 5.0 %collective-permute-start.47 = (f32[64,512]{1,0:T(8,128)S(1)}, f32[64,512]{1,0:T(8,128)S(1)}, u32[]{:S(2)}, u32[]{:S(2)}) collective-permute-start(f32[64,512]{1,0:T(8,128)S(1)} %get-tuple-element.76.mine_ref), channel_id=1, source_target_pairs={{0,1},{1,0},{2,3},{3,2},{4,5},{5,4},{6,7},{7,6},{8,9},{9,8},{10,11... | collective-permute-start | bytes 393224 | tf_op jit(solution)/shard_map/ppermute | solution.py:298
  (29 other events, 97.0 us)

commit v2 on v1

--- a/solution.py
+++ b/solution.py
@@ -10,7 +10,7 @@
 
 ITERS = 3
 LANES = 128
-GROUP = 8
+GROUP = 16
 CUT = 4
 HIGH = lax.Precision.HIGHEST
 F32 = jnp.float32
@@ -51,41 +51,55 @@
     return tall[2 * rows :] + tall[rows : 2 * rows] + tall[:rows]
 
 
-def deal_body(returns_ref, out_ref, sems):
-    blocks, _, width = out_ref.shape
+def open_body(me_ref, returns_ref, seed_ref, out_ref, *rest):
+    *pieces, dealt_ref, wide_ref, table_ref, sems = rest
+    blocks, _, width = dealt_ref.shape
     span = returns_ref.shape[1] // blocks
     copies = [
-        pltpu.make_async_copy(returns_ref.at[:, b * span : b * span + width], out_ref.at[b], sems.at[b])
-        for b in range(blocks)
+        pltpu.make_async_copy(returns_ref, wide_ref, sems.at[0]),
+        pltpu.make_async_copy(seed_ref, table_ref, sems.at[1]),
     ]
+    for mask, piece in enumerate(pieces):
+        at = pl.multiple_of((me_ref[0] ^ mask) * span, LANES)
+        source = returns_ref.at[:, pl.ds(at, piece.shape[1])]
+        copies.append(pltpu.make_async_copy(source, piece, sems.at[2 + mask]))
     for copy in copies:
         copy.start()
-    for copy in copies:
+    for copy in copies[:2]:
         copy.wait()
-
-
-def deal(returns, blocks, width):
-    return pl.pallas_call(
-        deal_body,
-        out_shape=jax.ShapeDtypeStruct((blocks, returns.shape[0], width), returns.dtype),
-        in_specs=[pl.BlockSpec(memory_space=pl.ANY)],
-        out_specs=pl.BlockSpec(memory_space=pltpu.VMEM),
-        scratch_shapes=[pltpu.SemaphoreType.DMA((blocks,))],
-    )(returns)
-
-
-def project_first_body(span, me_ref, returns_ref, seed_ref, out_ref, *pieces):
     factors = out_ref.shape[0]
-    for mask, piece in enumerate(pieces):
-        width = piece.shape[1]
-        at = pl.multiple_of((me_ref[0] ^ mask) * span + span - width, LANES)
-        piece[...] = returns_ref[:, pl.ds(at, width)]
-    seed = seed_ref[...]
+    seed = table_ref[...]
     coarse = (seed >> 3) << 3
     fine = seed - coarse
     both = jnp.concatenate([coarse.astype(F32).astype(BF16), fine.astype(F32).astype(BF16)], axis=0)
-    tall = lax.dot_general(both, returns_ref[...], (((1,), (1,)), ((), ())), preferred_element_type=F32)
+    tall = lax.dot_general(both, wide_ref[...], (((1,), (1,)), ((), ())), preferred_element_type=F32)
     out_ref[...] = (tall[:factors] + tall[factors:]) / 1000.0
+    for b in range(blocks):
+        dealt_ref[b] = wide_ref[:, (b + 1) * span - width : (b + 1) * span]
+    for copy in copies[2:]:
+        copy.wait()
+
+
+def opening(me, returns, seed, blocks, width):
+    days, assets = returns.shape
+    rest = assets // blocks - width
+    factors = seed.shape[0]
+    outs = [((factors, days), F32)] + [((days, width), BF16)] * blocks + [((blocks, days, rest), BF16)]
+    return pl.pallas_call(
+        open_body,
+        out_shape=[jax.ShapeDtypeStruct(shape, dtype) for shape, dtype in outs],
+        in_specs=smem() + [pl.BlockSpec(memory_space=pltpu.HBM)] * 2,
+        out_specs=vmem(len(outs)),
+        scratch_shapes=[
+            pltpu.VMEM(returns.shape, BF16),
+            pltpu.VMEM(seed.shape, jnp.int32),
+            pltpu.SemaphoreType.DMA((2 + blocks,)),
+        ],
+        cost_estimate=pl.CostEstimate(
+            flops=4 * days * assets * factors, bytes_accessed=returns.size * 2, transcendentals=0
+        ),
+        compiler_params=pltpu.CompilerParams(vmem_limit_bytes=51 * 1024 * 1024),
+    )(me, returns, seed)
 
 
 def halves(par_ref, full_ref, keep_ref, send_ref):
@@ -325,8 +339,12 @@
     return mine
 
 
-def sum_assets(keep, send):
-    mine = sum_chips(keep + swap(send, "gr", 1))
+def sum_assets(keep, send, reverse):
+    mine = keep + swap(send, "gr", 1)
+    size = lax.axis_size("gr")
+    masks = [m for m in (1 << k for k in range(1, size)) if m < size]
+    for mask in masks[::-1] if reverse else masks:
+        mine = mine + swap(mine, "gr", mask)
     return mine, swap(mine, "gr", 1)
 
 
@@ -349,33 +367,28 @@
     rest = span - cut
     masks = tuple(range(2, blocks, 2))
 
-    dealt = deal(returns, blocks, cut)
-    block = lax.all_to_all(dealt, "gr", 0, 0).reshape(slab_days, cut)
-    own, *pieces = call(
-        functools.partial(project_first_body, span),
-        [((factors, days), F32)] + [((days, rest), BF16)] * blocks,
-        [me], [returns, start_seed.T], 4 * days * assets * factors,
-    )
+    own, *pieces, dealt = opening(me, returns, start_seed.T, blocks, cut)
     twin = swap(own, "gr", 1)
     both = jnp.stack([own, twin])
     pairs = [swap(both, "gr", m) for m in masks]
     pieces = [p if m == 0 else swap(p, "gr", m) for m, p in enumerate(pieces)]
+    last = lax.all_to_all(dealt, "gr", 0, 0).reshape(slab_days, rest)
 
     asset_half = ((factors, span // 2), F32)
     full_assets = pltpu.VMEM((factors, span), F32)
     slab = pltpu.VMEM((factors, slab_days), F32)
 
     shared = [own, twin, *pairs]
-    keep, send = call(
-        functools.partial(apply_first_body, masks, False), [((factors, cut // 2), F32)] * 2, [me, par],
-        shared + [block], dots, [slab, pltpu.VMEM((factors, cut), F32)],
+    block, keep, send = call(
+        functools.partial(apply_first_body, masks, True),
+        [((slab_days, cut), BF16)] + [((factors, cut // 2), F32)] * 2, [me, par],
+        shared + pieces, dots, [slab, pltpu.VMEM((factors, cut), F32)],
     )
     mine = sum_days(keep, send)
     theirs = swap(mine, "gc", 1)
-    last, keep, send = call(
-        functools.partial(apply_first_body, masks, True),
-        [((slab_days, rest), BF16)] + [((factors, rest // 2), F32)] * 2, [me, par],
-        shared + pieces, dots, [slab, pltpu.VMEM((factors, rest), F32)],
+    keep, send = call(
+        functools.partial(apply_first_body, masks, False), [((factors, rest // 2), F32)] * 2, [me, par],
+        shared + [last], dots, [slab, pltpu.VMEM((factors, rest), F32)],
     )
     mine_late = sum_days(keep, send)
     pieces = [mine, theirs, mine_late, swap(mine_late, "gc", 1)]
@@ -393,21 +406,21 @@
                 functools.partial(project_lead_body, days_all), [quarter] * 2 + [rows] * 2, [par, core],
                 [mine, swap(mine, "gc", 1), *block_list, inverse], dots // 2, [part_assets, part_days],
             )
-            lead = sum_assets(keep, send)
+            lead = sum_assets(keep, send, False)
             mine = sum_days(*sent[1])
             keep, send = call(
                 functools.partial(project_trail_body, days_all), [quarter] * 2, [par, core],
                 [mine, swap(mine, "gc", 1), raw, applied, *block_list, inverse], dots // 2,
                 [part_assets, part_days],
             )
-            trail = sum_assets(keep, send)
+            trail = sum_assets(keep, send, True)
         else:
             parts = call(
                 functools.partial(project_both_body, days_all, len(pieces) // 2, len(block_list)),
                 [quarter] * 4, [par, core], pieces + block_list, dots, [full_assets, part_days],
             )
-            lead = sum_assets(*parts[:2])
-            trail = sum_assets(*parts[2:])
+            lead = sum_assets(*parts[:2], False)
+            trail = sum_assets(*parts[2:], True)
         sent = [
             call(apply_body, [lane_half] * 2, [core, par], [*pair, *block_list], dots // 2, [part_days, part_assets])
             for pair in (lead, trail)

time: 142 us -> 134 us (0.944)
  local copies, waits for them, and re-layouts: 4.5 us -> 0 us
    unnamed x12 -> x0, local copies, waits for them, and re-layouts: 4.5 us -> none
    pallas_call x14 -> x13, Pallas kernels: 15.2 us -> 12.6 us  [call(): pl.pallas_call(body, out_shape=[jax.ShapeDtypeStruct(shape, dtype) for sh...]
    ppermute x51 -> x47, waiting for transfers between devices: 52 us -> 50.3 us  [swap(): return lax.ppermute(x, axis, [(s, s ^ mask) for s in range(size)])]
    pallas_call x1, Pallas kernels: 2.5 us -> 4.14 us  [opening(): pl.pallas_call(open_body, out_shape=[jax.ShapeDtypeStruct(shape, dtype) f...]
    ppermute x51 -> x47, starting transfers between devices: 57.5 us -> 56 us  [swap(): return lax.ppermute(x, axis, [(s, s ^ mask) for s in range(size)])]
  transfers between devices with their start and end apart: 55 -> 51, of which waited for: 27 -> 26; matrix products, arithmetic and copies ran while one was open for 0% -> 0% of each run, Pallas kernels for 7% -> 6%
where the time goes in v2:
time: 134 us
  starting transfers between devices  63.4 us (47%)
  waiting for transfers between devices  53 us (40%)
  Pallas kernels  16.7 us (12%)
    ppermute x47, starting transfers between devices, swap(): return lax.ppermute(x, axis, [(s, s ^ mask) for s in range(size)])  56 us
    ppermute x47, waiting for transfers between devices, swap(): return lax.ppermute(x, axis, [(s, s ^ mask) for s in range(size)])  50.3 us
    pallas_call x13, Pallas kernels, call(): pl.pallas_call(body, out_shape=[jax.ShapeDtypeStruct(shape, dtype) for sh...  12.6 us
    all_to_all x1, starting transfers between devices, local(): last = lax.all_to_all(dealt, 'gr', 0, 0).reshape(slab_days, rest)  5.22 us
    pallas_call x1, Pallas kernels, opening(): pl.pallas_call(open_body, out_shape=[jax.ShapeDtypeStruct(shape, dtype) f...  4.14 us
    ppermute x3, waiting for transfers between devices, cross(): return lax.ppermute(x, ('gr', 'gc'), pairs)  2.69 us
  transfers between devices with their start and end apart: 51, of which 26 were waited for; matrix products, arithmetic and copies ran while one was open for 0% of the time, Pallas kernels for 6%

profile of v2, /device:TPU:0, one launch (start us, length us, event | category | flops | bytes accessed | tf_op | source)
XLA Modules:
  0.0 134.3 jit_solution(6386523328774446147)
XLA Ops:
  0.6 4.1 %shard_map.41 = (f32[64,128]{1,0:T(8,128)S(1)}, bf16[128,512]{1,0:T(8,128)(2,1)S(1)}, bf16[128,512]{1,0:T(8,128)(2,1)S(1)}, bf16[128,512]{1,0:T(8,128)(2,1)S(1)}...) custom-call(s32[1]{0:T(128)} %bitcast.2.me_ref, ...), custom_call_target="tpu_custom_call" | custom-call | flops 268435456 | bytes 2097152 | tf_op jit(solution)/shard_map/pallas_call | solution.py:88
  4.8 5.2 %all-to-all-start = ((bf16[8,128,512]{2,1,0:T(8,128)(2,1)}), bf16[8,128,512]{2,1,0:T(8,128)(2,1)S(1)}, u32[]{:S(2)}, u32[]{:S(2)}) async-start(bf16[8,128,512]{2,1,0:T(8,128)(2,1)} %get-tuple-element.54), calls=%async_computation | async-start | bytes 2097152 | tf_op jit(solution)/shard_map/all_to_all | solution.py:375
  10.5 2.0 %collective-permute-start.5 = (bf16[128,512]{1,0:T(8,128)(2,1)S(1)}, bf16[128,512]{1,0:T(8,128)(2,1)S(1)}, u32[]{:S(2)}, u32[]{:S(2)}) collective-permute-start(bf16[128,512]{1,0:T(8,128)(2,1)S(1)} %get-tuple-element.46), channel_id=1, source_target_pairs={{0,8},{4,12},{8,0},{12,4},{16,24},{20,28},{24,16},{28,20},{1,9},{5... | collective-permute-start | bytes 393224 | tf_op jit(solution)/shard_map/ppermute | solution.py:312
  16.1 13.2 %collective-permute-done.1.rest_0_ = f32[2,64,128]{2,1,0:T(8,128)S(1)} collective-permute-done((f32[2,64,128]{2,1,0:T(8,128)S(1)}, f32[2,64,128]{2,1,0:T(8,128)S(1)}, u32[]{:S(2)}, u32[]{:S(2)}) %collective-permute-start.1) | collective-permute-done | bytes 65568 | tf_op jit(solution)/shard_map/ppermute | solution.py:312
  31.1 2.6 %collective-permute-start.9 = (bf16[128,512]{1,0:T(8,128)(2,1)S(1)}, bf16[128,512]{1,0:T(8,128)(2,1)S(1)}, u32[]{:S(2)}, u32[]{:S(2)}) collective-permute-start(bf16[128,512]{1,0:T(8,128)(2,1)S(1)} %get-tuple-element.50), channel_id=1, source_target_pairs={{0,24},{4,28},{8,16},{12,20},{16,8},{20,12},{24,0},{28,4},{1,25},{... | collective-permute-start | bytes 393224 | tf_op jit(solution)/shard_map/ppermute | solution.py:312
  34.2 7.0 %collective-permute-done.7.rest_7_ = bf16[128,512]{1,0:T(8,128)(2,1)S(1)} collective-permute-done((bf16[128,512]{1,0:T(8,128)(2,1)S(1)}, bf16[128,512]{1,0:T(8,128)(2,1)S(1)}, u32[]{:S(2)}, u32[]{:S(2)}) %collective-permute-start.7) | collective-permute-done | bytes 131104 | tf_op jit(solution)/shard_map/ppermute | solution.py:312
  41.3 1.7 %collective-permute-done.8.rest_8_ = bf16[128,512]{1,0:T(8,128)(2,1)S(1)} collective-permute-done((bf16[128,512]{1,0:T(8,128)(2,1)S(1)}, bf16[128,512]{1,0:T(8,128)(2,1)S(1)}, u32[]{:S(2)}, u32[]{:S(2)}) %collective-permute-start.8) | collective-permute-done | bytes 131104 | tf_op jit(solution)/shard_map/ppermute | solution.py:312
  43.4 1.6 %collective-permute-start.11 = (f32[64,256]{1,0:T(8,128)S(1)}, f32[64,256]{1,0:T(8,128)S(1)}, u32[]{:S(2)}, u32[]{:S(2)}) collective-permute-start(f32[64,256]{1,0:T(8,128)S(1)} %get-tuple-element.53), channel_id=1, source_target_pairs={{0,1},{1,0},{2,3},{3,2},{4,5},{5,4},{6,7},{7,6},{8,9},{9,8},{10,11... | collective-permute-start | bytes 196616 | tf_op jit(solution)/shard_map/ppermute | solution.py:312
  46.0 1.9 %collective-permute-done.11 = f32[64,256]{1,0:T(8,128)S(1)} collective-permute-done((f32[64,256]{1,0:T(8,128)S(1)}, f32[64,256]{1,0:T(8,128)S(1)}, u32[]{:S(2)}, u32[]{:S(2)}) %collective-permute-start.11) | collective-permute-done | bytes 65568 | tf_op jit(solution)/shard_map/ppermute | solution.py:312
  47.9 2.6 %collective-permute-start.12 = (f32[64,256]{1,0:T(8,128)S(1)}, f32[64,256]{1,0:T(8,128)S(1)}, u32[]{:S(2)}, u32[]{:S(2)}) collective-permute-start(f32[64,256]{1,0:T(8,128)S(1)} %add.99), channel_id=1, source_target_pairs={{0,2},{1,3},{2,0},{3,1},{4,6},{5,7},{6,4},{7,5},{8,10},{9,11},{10,... | collective-permute-start | bytes 196616 | tf_op jit(solution)/shard_map/ppermute | solution.py:312
  50.6 1.9 %collective-permute-start.15 = (f32[64,256]{1,0:T(8,128)S(1)}, f32[64,256]{1,0:T(8,128)S(1)}, u32[]{:S(2)}, u32[]{:S(2)}) collective-permute-start(f32[64,256]{1,0:T(8,128)S(1)} %add.101), channel_id=1, source_target_pairs={{0,2},{1,3},{2,0},{3,1},{4,6},{5,7},{6,4},{7,5},{8,10},{9,11},{10,... | collective-permute-start | bytes 196616 | tf_op jit(solution)/shard_map/ppermute | solution.py:312
  53.5 3.2 %collective-permute-start.13 = (f32[64,256]{1,0:T(8,128)S(1)}, f32[64,256]{1,0:T(8,128)S(1)}, u32[]{:S(2)}, u32[]{:S(2)}) collective-permute-start(f32[64,256]{1,0:T(8,128)S(1)} %add.100.rest_0_), channel_id=1, source_target_pairs={{0,1},{1,0},{2,3},{3,2},{4,5},{5,4},{6,7},{7,6},{8,9},{9,8},{10,11... | collective-permute-start | bytes 196616 | tf_op jit(solution)/shard_map/ppermute | solution.py:312
  56.7 2.0 %collective-permute-start.16 = (f32[64,256]{1,0:T(8,128)S(1)}, f32[64,256]{1,0:T(8,128)S(1)}, u32[]{:S(2)}, u32[]{:S(2)}) collective-permute-start(f32[64,256]{1,0:T(8,128)S(1)} %add.102.rest_2_), channel_id=1, source_target_pairs={{0,1},{1,0},{2,3},{3,2},{4,5},{5,4},{6,7},{7,6},{8,9},{9,8},{10,11... | collective-permute-start | bytes 196616 | tf_op jit(solution)/shard_map/ppermute | solution.py:312
  64.5 1.7 %collective-permute-start.25 = (f32[16,1152]{1,0:T(8,128)S(1)}, f32[16,1152]{1,0:T(8,128)S(1)}, u32[]{:S(2)}, u32[]{:S(2)}) collective-permute-start(f32[16,1152]{1,0:T(8,128)S(1)} %add.108), channel_id=1, source_target_pairs={{0,16},{4,20},{8,24},{12,28},{16,0},{20,4},{24,8},{28,12},{1,17},{... | collective-permute-start | bytes 221192 | tf_op jit(solution)/shard_map/ppermute | solution.py:312
  66.3 1.6 %collective-permute-done.18 = f32[16,1152]{1,0:T(8,128)S(1)} collective-permute-done((f32[16,1152]{1,0:T(8,128)S(1)}, f32[16,1152]{1,0:T(8,128)S(1)}, u32[]{:S(2)}, u32[]{:S(2)}) %collective-permute-start.18) | collective-permute-done | bytes 73760 | tf_op jit(solution)/shard_map/ppermute | solution.py:312
  70.7 1.6 %collective-permute-done.19 = f32[16,1152]{1,0:T(8,128)S(1)} collective-permute-done((f32[16,1152]{1,0:T(8,128)S(1)}, f32[16,1152]{1,0:T(8,128)S(1)}, u32[]{:S(2)}, u32[]{:S(2)}) %collective-permute-start.19) | collective-permute-done | bytes 73760 | tf_op jit(solution)/shard_map/ppermute | solution.py:312
  74.3 2.0 %collective-permute-start.21 = (f32[32,512]{1,0:T(8,128)S(1)}, f32[32,512]{1,0:T(8,128)S(1)}, u32[]{:S(2)}, u32[]{:S(2)}) collective-permute-start(f32[32,512]{1,0:T(8,128)S(1)} %get-tuple-element.61), channel_id=1, source_target_pairs={{0,1},{1,0},{2,3},{3,2},{4,5},{5,4},{6,7},{7,6},{8,9},{9,8},{10,11... | collective-permute-start | bytes 196616 | tf_op jit(solution)/shard_map/ppermute | solution.py:312
  79.1 2.9 %collective-permute-start.22 = (f32[32,512]{1,0:T(8,128)S(1)}, f32[32,512]{1,0:T(8,128)S(1)}, u32[]{:S(2)}, u32[]{:S(2)}) collective-permute-start(f32[32,512]{1,0:T(8,128)S(1)} %add.106), channel_id=1, source_target_pairs={{0,2},{1,3},{2,0},{3,1},{4,6},{5,7},{6,4},{7,5},{8,10},{9,11},{10,... | collective-permute-start | bytes 196616 | tf_op jit(solution)/shard_map/ppermute | solution.py:312
  83.5 1.8 %collective-permute-done.22 = f32[32,512]{1,0:T(8,128)S(1)} collective-permute-done((f32[32,512]{1,0:T(8,128)S(1)}, f32[32,512]{1,0:T(8,128)S(1)}, u32[]{:S(2)}, u32[]{:S(2)}) %collective-permute-start.22) | collective-permute-done | bytes 65568 | tf_op jit(solution)/shard_map/ppermute | solution.py:312
  85.4 2.4 %collective-permute-start.23 = (f32[32,512]{1,0:T(8,128)S(1)}, f32[32,512]{1,0:T(8,128)S(1)}, u32[]{:S(2)}, u32[]{:S(2)}) collective-permute-start(f32[32,512]{1,0:T(8,128)S(1)} %add.107.mine_ref), channel_id=1, source_target_pairs={{0,1},{1,0},{2,3},{3,2},{4,5},{5,4},{6,7},{7,6},{8,9},{9,8},{10,11... | collective-permute-start | bytes 196616 | tf_op jit(solution)/shard_map/ppermute | solution.py:312
  87.8 1.7 %collective-permute-start.36 = (f32[32,512]{1,0:T(8,128)S(1)}, f32[32,512]{1,0:T(8,128)S(1)}, u32[]{:S(2)}, u32[]{:S(2)}) collective-permute-start(f32[32,512]{1,0:T(8,128)S(1)} %add.117.mine_ref), channel_id=1, source_target_pairs={{0,1},{1,0},{2,3},{3,2},{4,5},{5,4},{6,7},{7,6},{8,9},{9,8},{10,11... | collective-permute-start | bytes 196616 | tf_op jit(solution)/shard_map/ppermute | solution.py:312
  89.5 1.6 %shard_map.46 = (f32[64,64]{1,0:T(8,128)S(1)}, f32[1,64]{1,0:T(1,128)S(1)}) custom-call(s32[1]{0:T(128)} %bitcast.1.core_ref, f32[16,1152]{1,0:T(8,128)S(1)} %add.105.mine_ref, f32[16,1152]{1,0:T(8,128)S(1)} %collective-permute-done.20.theirs_ref, f32[16,1152]{1,0:T(8,128)S(1)} %add.110.mine_late_ref.mine_ref, ...), custom_call_target="tpu_custom_call" | custom-call | flops 201326592 | bytes 16640 | tf_op jit(solution)/shard_map/pallas_call | solution.py:31
  96.3 2.2 %collective-permute-done.29 = f32[16,1152]{1,0:T(8,128)S(1)} collective-permute-done((f32[16,1152]{1,0:T(8,128)S(1)}, f32[16,1152]{1,0:T(8,128)S(1)}, u32[]{:S(2)}, u32[]{:S(2)}) %collective-permute-start.29) | collective-permute-done | bytes 73760 | tf_op jit(solution)/shard_map/ppermute | solution.py:312
  100.9 2.0 %collective-permute-done.30 = f32[16,1152]{1,0:T(8,128)S(1)} collective-permute-done((f32[16,1152]{1,0:T(8,128)S(1)}, f32[16,1152]{1,0:T(8,128)S(1)}, u32[]{:S(2)}, u32[]{:S(2)}) %collective-permute-start.30) | collective-permute-done | bytes 73760 | tf_op jit(solution)/shard_map/ppermute | solution.py:312
  107.5 2.1 %collective-permute-done.32 = f32[32,512]{1,0:T(8,128)S(1)} collective-permute-done((f32[32,512]{1,0:T(8,128)S(1)}, f32[32,512]{1,0:T(8,128)S(1)}, u32[]{:S(2)}, u32[]{:S(2)}) %collective-permute-start.32) | collective-permute-done | bytes 65568 | tf_op jit(solution)/shard_map/ppermute | solution.py:312
  109.6 2.7 %collective-permute-start.33 = (f32[32,512]{1,0:T(8,128)S(1)}, f32[32,512]{1,0:T(8,128)S(1)}, u32[]{:S(2)}, u32[]{:S(2)}) collective-permute-start(f32[32,512]{1,0:T(8,128)S(1)} %add.114), channel_id=1, source_target_pairs={{0,2},{1,3},{2,0},{3,1},{4,6},{5,7},{6,4},{7,5},{8,10},{9,11},{10,... | collective-permute-start | bytes 196616 | tf_op jit(solution)/shard_map/ppermute | solution.py:312
  112.3 1.9 %collective-permute-start.42 = (f32[32,512]{1,0:T(8,128)S(1)}, f32[32,512]{1,0:T(8,128)S(1)}, u32[]{:S(2)}, u32[]{:S(2)}) collective-permute-start(f32[32,512]{1,0:T(8,128)S(1)} %add.121), channel_id=1, source_target_pairs={{0,2},{1,3},{2,0},{3,1},{4,6},{5,7},{6,4},{7,5},{8,10},{9,11},{10,... | collective-permute-start | bytes 196616 | tf_op jit(solution)/shard_map/ppermute | solution.py:312
  115.8 1.8 %collective-permute-done.42 = f32[32,512]{1,0:T(8,128)S(1)} collective-permute-done((f32[32,512]{1,0:T(8,128)S(1)}, f32[32,512]{1,0:T(8,128)S(1)}, u32[]{:S(2)}, u32[]{:S(2)}) %collective-permute-start.42) | collective-permute-done | bytes 65568 | tf_op jit(solution)/shard_map/ppermute | solution.py:312
  118.3 1.7 %collective-permute-start.45 = (f32[32,128]{1,0:T(8,128)S(1)}, f32[32,128]{1,0:T(8,128)S(1)}, u32[]{:S(2)}, u32[]{:S(2)}) collective-permute-start(f32[32,128]{1,0:T(8,128)S(1)} %get-tuple-element.79), channel_id=1, source_target_pairs={{0,1},{1,0},{2,3},{3,2},{4,5},{5,4},{6,7},{7,6},{8,9},{9,8},{10,11... | collective-permute-start | bytes 49160 | tf_op jit(solution)/shard_map/ppermute | solution.py:318
  127.3 1.7 %collective-permute-done.49 = f32[32,128]{1,0:T(8,128)S(1)} collective-permute-done((f32[32,128]{1,0:T(8,128)S(1)}, f32[32,128]{1,0:T(8,128)S(1)}, u32[]{:S(2)}, u32[]{:S(2)}) %collective-permute-start.49) | collective-permute-done | bytes 16416 | tf_op jit(solution)/shard_map/ppermute | solution.py:312
  129.6 2.1 %collective-permute-done.43.theirs_ref = f32[64,512]{1,0:T(8,128)S(1)} collective-permute-done((f32[64,512]{1,0:T(8,128)S(1)}, f32[64,512]{1,0:T(8,128)S(1)}, u32[]{:S(2)}, u32[]{:S(2)}) %collective-permute-start.43) | collective-permute-done | bytes 131104 | tf_op jit(solution)/shard_map/ppermute | solution.py:312
  131.7 2.6 %shard_map.54 = (f32[64,1024]{1,0:T(8,128)}, f32[3,64]{1,0:T(4,128)}) custom-call(s32[1]{0:T(128)} %bitcast.par_ref, f32[64,512]{1,0:T(8,128)S(1)} %get-tuple-element.78.mine_ref, f32[64,512]{1,0:T(8,128)S(1)} %collective-permute-done.43.theirs_ref, f32[32,128]{1,0:T(8,128)S(1)} %add_add_fusion.gram_ref, f32[1,64]{1,0:T(1,128)S(1)} %get-tuple-element.80.rest_0_, ...), custom_call_target="tpu_custom_call" | custom-call | flops 402653184 | bytes 262912 | tf_op jit(solution)/shard_map/pallas_call | solution.py:31
  (111 shorter events, 46.1 us)
Async XLA Ops:
  4.8 40.3 %all-to-all-start = ((bf16[8,128,512]{2,1,0:T(8,128)(2,1)}), bf16[8,128,512]{2,1,0:T(8,128)(2,1)S(1)}, u32[]{:S(2)}, u32[]{:S(2)}) async-start(bf16[8,128,512]{2,1,0:T(8,128)(2,1)} %get-tuple-element.54), calls=%async_computation | async-start | bytes 2097152 | tf_op jit(solution)/shard_map/all_to_all | solution.py:375
  10.5 20.6 %collective-permute-start.4 = (bf16[128,512]{1,0:T(8,128)(2,1)S(1)}, bf16[128,512]{1,0:T(8,128)(2,1)S(1)}, u32[]{:S(2)}, u32[]{:S(2)}) collective-permute-start(bf16[128,512]{1,0:T(8,128)(2,1)S(1)} %get-tuple-element.45), channel_id=1, source_target_pairs={{0,4},{4,0},{8,12},{12,8},{16,20},{20,16},{24,28},{28,24},{1,5},{5... | collective-permute-start | bytes 393224 | tf_op jit(solution)/shard_map/ppermute | solution.py:312
  10.5 23.2 %collective-permute-start.5 = (bf16[128,512]{1,0:T(8,128)(2,1)S(1)}, bf16[128,512]{1,0:T(8,128)(2,1)S(1)}, u32[]{:S(2)}, u32[]{:S(2)}) collective-permute-start(bf16[128,512]{1,0:T(8,128)(2,1)S(1)} %get-tuple-element.46), channel_id=1, source_target_pairs={{0,8},{4,12},{8,0},{12,4},{16,24},{20,28},{24,16},{28,20},{1,9},{5... | collective-permute-start | bytes 393224 | tf_op jit(solution)/shard_map/ppermute | solution.py:312
  12.5 16.8 %collective-permute-start.1 = (f32[2,64,128]{2,1,0:T(8,128)S(1)}, f32[2,64,128]{2,1,0:T(8,128)S(1)}, u32[]{:S(2)}, u32[]{:S(2)}) collective-permute-start(f32[2,64,128]{2,1,0:T(8,128)S(1)} %pad_maximum_fusion), channel_id=1, source_target_pairs={{0,8},{4,12},{8,0},{12,4},{16,24},{20,28},{24,16},{28,20},{1,9},{5... | collective-permute-start | bytes 196616 | tf_op jit(solution)/shard_map/ppermute | solution.py:312
  13.3 16.0 %collective-permute-start.2 = (f32[2,64,128]{2,1,0:T(8,128)S(1)}, f32[2,64,128]{2,1,0:T(8,128)S(1)}, u32[]{:S(2)}, u32[]{:S(2)}) collective-permute-start(f32[2,64,128]{2,1,0:T(8,128)S(1)} %pad_maximum_fusion), channel_id=1, source_target_pairs={{0,16},{4,20},{8,24},{12,28},{16,0},{20,4},{24,8},{28,12},{1,17},{... | collective-permute-start | bytes 196616 | tf_op jit(solution)/shard_map/ppermute | solution.py:312
  14.7 16.3 %collective-permute-start.3 = (f32[2,64,128]{2,1,0:T(8,128)S(1)}, f32[2,64,128]{2,1,0:T(8,128)S(1)}, u32[]{:S(2)}, u32[]{:S(2)}) collective-permute-start(f32[2,64,128]{2,1,0:T(8,128)S(1)} %pad_maximum_fusion), channel_id=1, source_target_pairs={{0,24},{4,28},{8,16},{12,20},{16,8},{20,12},{24,0},{28,4},{1,25},{... | collective-permute-start | bytes 196616 | tf_op jit(solution)/shard_map/ppermute | solution.py:312
  29.3 4.9 %collective-permute-start.6 = (bf16[128,512]{1,0:T(8,128)(2,1)S(1)}, bf16[128,512]{1,0:T(8,128)(2,1)S(1)}, u32[]{:S(2)}, u32[]{:S(2)}) collective-permute-start(bf16[128,512]{1,0:T(8,128)(2,1)S(1)} %get-tuple-element.47), channel_id=1, source_target_pairs={{0,12},{4,8},{8,4},{12,0},{16,28},{20,24},{24,20},{28,16},{1,13},{... | collective-permute-start | bytes 393224 | tf_op jit(solution)/shard_map/ppermute | solution.py:312
  29.3 12.0 %collective-permute-start.7 = (bf16[128,512]{1,0:T(8,128)(2,1)S(1)}, bf16[128,512]{1,0:T(8,128)(2,1)S(1)}, u32[]{:S(2)}, u32[]{:S(2)}) collective-permute-start(bf16[128,512]{1,0:T(8,128)(2,1)S(1)} %get-tuple-element.48), channel_id=1, source_target_pairs={{0,16},{4,20},{8,24},{12,28},{16,0},{20,4},{24,8},{28,12},{1,17},{... | collective-permute-start | bytes 393224 | tf_op jit(solution)/shard_map/ppermute | solution.py:312
  31.0 11.9 %collective-permute-start.8 = (bf16[128,512]{1,0:T(8,128)(2,1)S(1)}, bf16[128,512]{1,0:T(8,128)(2,1)S(1)}, u32[]{:S(2)}, u32[]{:S(2)}) collective-permute-start(bf16[128,512]{1,0:T(8,128)(2,1)S(1)} %get-tuple-element.49), channel_id=1, source_target_pairs={{0,20},{4,16},{8,28},{12,24},{16,4},{20,0},{24,12},{28,8},{1,21},{... | collective-permute-start | bytes 393224 | tf_op jit(solution)/shard_map/ppermute | solution.py:312
  31.1 11.8 %collective-permute-start.9 = (bf16[128,512]{1,0:T(8,128)(2,1)S(1)}, bf16[128,512]{1,0:T(8,128)(2,1)S(1)}, u32[]{:S(2)}, u32[]{:S(2)}) collective-permute-start(bf16[128,512]{1,0:T(8,128)(2,1)S(1)} %get-tuple-element.50), channel_id=1, source_target_pairs={{0,24},{4,28},{8,16},{12,20},{16,8},{20,12},{24,0},{28,4},{1,25},{... | collective-permute-start | bytes 393224 | tf_op jit(solution)/shard_map/ppermute | solution.py:312
  33.7 9.2 %collective-permute-start.10 = (bf16[128,512]{1,0:T(8,128)(2,1)S(1)}, bf16[128,512]{1,0:T(8,128)(2,1)S(1)}, u32[]{:S(2)}, u32[]{:S(2)}) collective-permute-start(bf16[128,512]{1,0:T(8,128)(2,1)S(1)} %get-tuple-element.51), channel_id=1, source_target_pairs={{0,28},{4,24},{8,20},{12,16},{16,12},{20,8},{24,4},{28,0},{1,29},{... | collective-permute-start | bytes 393224 | tf_op jit(solution)/shard_map/ppermute | solution.py:312
  43.4 4.5 %collective-permute-start.11 = (f32[64,256]{1,0:T(8,128)S(1)}, f32[64,256]{1,0:T(8,128)S(1)}, u32[]{:S(2)}, u32[]{:S(2)}) collective-permute-start(f32[64,256]{1,0:T(8,128)S(1)} %get-tuple-element.53), channel_id=1, source_target_pairs={{0,1},{1,0},{2,3},{3,2},{4,5},{5,4},{6,7},{7,6},{8,9},{9,8},{10,11... | collective-permute-start | bytes 196616 | tf_op jit(solution)/shard_map/ppermute | solution.py:312
  45.5 5.1 %collective-permute-start.14 = (f32[64,256]{1,0:T(8,128)S(1)}, f32[64,256]{1,0:T(8,128)S(1)}, u32[]{:S(2)}, u32[]{:S(2)}) collective-permute-start(f32[64,256]{1,0:T(8,128)S(1)} %get-tuple-element.56), channel_id=1, source_target_pairs={{0,1},{1,0},{2,3},{3,2},{4,5},{5,4},{6,7},{7,6},{8,9},{9,8},{10,11... | collective-permute-start | bytes 196616 | tf_op jit(solution)/shard_map/ppermute | solution.py:312
  47.9 5.5 %collective-permute-start.12 = (f32[64,256]{1,0:T(8,128)S(1)}, f32[64,256]{1,0:T(8,128)S(1)}, u32[]{:S(2)}, u32[]{:S(2)}) collective-permute-start(f32[64,256]{1,0:T(8,128)S(1)} %add.99), channel_id=1, source_target_pairs={{0,2},{1,3},{2,0},{3,1},{4,6},{5,7},{6,4},{7,5},{8,10},{9,11},{10,... | collective-permute-start | bytes 196616 | tf_op jit(solution)/shard_map/ppermute | solution.py:312
  50.6 6.1 %collective-permute-start.15 = (f32[64,256]{1,0:T(8,128)S(1)}, f32[64,256]{1,0:T(8,128)S(1)}, u32[]{:S(2)}, u32[]{:S(2)}) collective-permute-start(f32[64,256]{1,0:T(8,128)S(1)} %add.101), channel_id=1, source_target_pairs={{0,2},{1,3},{2,0},{3,1},{4,6},{5,7},{6,4},{7,5},{8,10},{9,11},{10,... | collective-permute-start | bytes 196616 | tf_op jit(solution)/shard_map/ppermute | solution.py:312
  53.5 6.1 %collective-permute-start.13 = (f32[64,256]{1,0:T(8,128)S(1)}, f32[64,256]{1,0:T(8,128)S(1)}, u32[]{:S(2)}, u32[]{:S(2)}) collective-permute-start(f32[64,256]{1,0:T(8,128)S(1)} %add.100.rest_0_), channel_id=1, source_target_pairs={{0,1},{1,0},{2,3},{3,2},{4,5},{5,4},{6,7},{7,6},{8,9},{9,8},{10,11... | collective-permute-start | bytes 196616 | tf_op jit(solution)/shard_map/ppermute | solution.py:312
  64.5 4.8 %collective-permute-start.25 = (f32[16,1152]{1,0:T(8,128)S(1)}, f32[16,1152]{1,0:T(8,128)S(1)}, u32[]{:S(2)}, u32[]{:S(2)}) collective-permute-start(f32[16,1152]{1,0:T(8,128)S(1)} %add.108), channel_id=1, source_target_pairs={{0,16},{4,20},{8,24},{12,28},{16,0},{20,4},{24,8},{28,12},{1,17},{... | collective-permute-start | bytes 221192 | tf_op jit(solution)/shard_map/ppermute | solution.py:312
  67.9 4.4 %collective-permute-start.19 = (f32[16,1152]{1,0:T(8,128)S(1)}, f32[16,1152]{1,0:T(8,128)S(1)}, u32[]{:S(2)}, u32[]{:S(2)}) collective-permute-start(f32[16,1152]{1,0:T(8,128)S(1)} %add.104), channel_id=1, source_target_pairs={{0,16},{4,20},{8,24},{12,28},{16,0},{20,4},{24,8},{28,12},{1,17},{... | collective-permute-start | bytes 221192 | tf_op jit(solution)/shard_map/ppermute | solution.py:312
  74.3 4.7 %collective-permute-start.21 = (f32[32,512]{1,0:T(8,128)S(1)}, f32[32,512]{1,0:T(8,128)S(1)}, u32[]{:S(2)}, u32[]{:S(2)}) collective-permute-start(f32[32,512]{1,0:T(8,128)S(1)} %get-tuple-element.61), channel_id=1, source_target_pairs={{0,1},{1,0},{2,3},{3,2},{4,5},{5,4},{6,7},{7,6},{8,9},{9,8},{10,11... | collective-permute-start | bytes 196616 | tf_op jit(solution)/shard_map/ppermute | solution.py:312
  76.8 5.1 %collective-permute-start.34 = (f32[32,512]{1,0:T(8,128)S(1)}, f32[32,512]{1,0:T(8,128)S(1)}, u32[]{:S(2)}, u32[]{:S(2)}) collective-permute-start(f32[32,512]{1,0:T(8,128)S(1)} %get-tuple-element.70), channel_id=1, source_target_pairs={{0,1},{1,0},{2,3},{3,2},{4,5},{5,4},{6,7},{7,6},{8,9},{9,8},{10,11... | collective-permute-start | bytes 196616 | tf_op jit(solution)/shard_map/ppermute | solution.py:312
  79.1 6.3 %collective-permute-start.22 = (f32[32,512]{1,0:T(8,128)S(1)}, f32[32,512]{1,0:T(8,128)S(1)}, u32[]{:S(2)}, u32[]{:S(2)}) collective-permute-start(f32[32,512]{1,0:T(8,128)S(1)} %add.106), channel_id=1, source_target_pairs={{0,2},{1,3},{2,0},{3,1},{4,6},{5,7},{6,4},{7,5},{8,10},{9,11},{10,... | collective-permute-start | bytes 196616 | tf_op jit(solution)/shard_map/ppermute | solution.py:312
  81.9 5.9 %collective-permute-start.35 = (f32[32,512]{1,0:T(8,128)S(1)}, f32[32,512]{1,0:T(8,128)S(1)}, u32[]{:S(2)}, u32[]{:S(2)}) collective-permute-start(f32[32,512]{1,0:T(8,128)S(1)} %add.116), channel_id=1, source_target_pairs={{0,2},{1,3},{2,0},{3,1},{4,6},{5,7},{6,4},{7,5},{8,10},{9,11},{10,... | collective-permute-start | bytes 196616 | tf_op jit(solution)/shard_map/ppermute | solution.py:312
  85.4 5.8 %collective-permute-start.23 = (f32[32,512]{1,0:T(8,128)S(1)}, f32[32,512]{1,0:T(8,128)S(1)}, u32[]{:S(2)}, u32[]{:S(2)}) collective-permute-start(f32[32,512]{1,0:T(8,128)S(1)} %add.107.mine_ref), channel_id=1, source_target_pairs={{0,1},{1,0},{2,3},{3,2},{4,5},{5,4},{6,7},{7,6},{8,9},{9,8},{10,11... | collective-permute-start | bytes 196616 | tf_op jit(solution)/shard_map/ppermute | solution.py:312
  87.8 4.5 %collective-permute-start.36 = (f32[32,512]{1,0:T(8,128)S(1)}, f32[32,512]{1,0:T(8,128)S(1)}, u32[]{:S(2)}, u32[]{:S(2)}) collective-permute-start(f32[32,512]{1,0:T(8,128)S(1)} %add.117.mine_ref), channel_id=1, source_target_pairs={{0,1},{1,0},{2,3},{3,2},{4,5},{5,4},{6,7},{7,6},{8,9},{9,8},{10,11... | collective-permute-start | bytes 196616 | tf_op jit(solution)/shard_map/ppermute | solution.py:312
  95.1 4.7 %collective-permute-start.38 = (f32[16,1152]{1,0:T(8,128)S(1)}, f32[16,1152]{1,0:T(8,128)S(1)}, u32[]{:S(2)}, u32[]{:S(2)}) collective-permute-start(f32[16,1152]{1,0:T(8,128)S(1)} %add.118), channel_id=1, source_target_pairs={{0,16},{4,20},{8,24},{12,28},{16,0},{20,4},{24,8},{28,12},{1,17},{... | collective-permute-start | bytes 221192 | tf_op jit(solution)/shard_map/ppermute | solution.py:312
  98.5 4.4 %collective-permute-start.30 = (f32[16,1152]{1,0:T(8,128)S(1)}, f32[16,1152]{1,0:T(8,128)S(1)}, u32[]{:S(2)}, u32[]{:S(2)}) collective-permute-start(f32[16,1152]{1,0:T(8,128)S(1)} %add.112), channel_id=1, source_target_pairs={{0,16},{4,20},{8,24},{12,28},{16,0},{20,4},{24,8},{28,12},{1,17},{... | collective-permute-start | bytes 221192 | tf_op jit(solution)/shard_map/ppermute | solution.py:312
  104.8 4.8 %collective-permute-start.32 = (f32[32,512]{1,0:T(8,128)S(1)}, f32[32,512]{1,0:T(8,128)S(1)}, u32[]{:S(2)}, u32[]{:S(2)}) collective-permute-start(f32[32,512]{1,0:T(8,128)S(1)} %get-tuple-element.68), channel_id=1, source_target_pairs={{0,1},{1,0},{2,3},{3,2},{4,5},{5,4},{6,7},{7,6},{8,9},{9,8},{10,11... | collective-permute-start | bytes 196616 | tf_op jit(solution)/shard_map/ppermute | solution.py:312
  106.6 5.7 %collective-permute-start.41 = (f32[32,512]{1,0:T(8,128)S(1)}, f32[32,512]{1,0:T(8,128)S(1)}, u32[]{:S(2)}, u32[]{:S(2)}) collective-permute-start(f32[32,512]{1,0:T(8,128)S(1)} %get-tuple-element.76), channel_id=1, source_target_pairs={{0,1},{1,0},{2,3},{3,2},{4,5},{5,4},{6,7},{7,6},{8,9},{9,8},{10,11... | collective-permute-start | bytes 196616 | tf_op jit(solution)/shard_map/ppermute | solution.py:312
  109.6 6.2 %collective-permute-start.33 = (f32[32,512]{1,0:T(8,128)S(1)}, f32[32,512]{1,0:T(8,128)S(1)}, u32[]{:S(2)}, u32[]{:S(2)}) collective-permute-start(f32[32,512]{1,0:T(8,128)S(1)} %add.114), channel_id=1, source_target_pairs={{0,2},{1,3},{2,0},{3,1},{4,6},{5,7},{6,4},{7,5},{8,10},{9,11},{10,... | collective-permute-start | bytes 196616 | tf_op jit(solution)/shard_map/ppermute | solution.py:312
  112.3 5.4 %collective-permute-start.42 = (f32[32,512]{1,0:T(8,128)S(1)}, f32[32,512]{1,0:T(8,128)S(1)}, u32[]{:S(2)}, u32[]{:S(2)}) collective-permute-start(f32[32,512]{1,0:T(8,128)S(1)} %add.121), channel_id=1, source_target_pairs={{0,2},{1,3},{2,0},{3,1},{4,6},{5,7},{6,4},{7,5},{8,10},{9,11},{10,... | collective-permute-start | bytes 196616 | tf_op jit(solution)/shard_map/ppermute | solution.py:312
  124.4 4.6 %collective-permute-start.49 = (f32[32,128]{1,0:T(8,128)S(1)}, f32[32,128]{1,0:T(8,128)S(1)}, u32[]{:S(2)}, u32[]{:S(2)}) collective-permute-start(f32[32,128]{1,0:T(8,128)S(1)} %add_add_fusion.1), channel_id=1, source_target_pairs={{0,24},{4,28},{8,16},{12,20},{16,8},{20,12},{24,0},{28,4},{1,25},{... | collective-permute-start | bytes 49160 | tf_op jit(solution)/shard_map/ppermute | solution.py:312
  126.8 5.0 %collective-permute-start.43 = (f32[64,512]{1,0:T(8,128)S(1)}, f32[64,512]{1,0:T(8,128)S(1)}, u32[]{:S(2)}, u32[]{:S(2)}) collective-permute-start(f32[64,512]{1,0:T(8,128)S(1)} %get-tuple-element.78.mine_ref), channel_id=1, source_target_pairs={{0,1},{1,0},{2,3},{3,2},{4,5},{5,4},{6,7},{7,6},{8,9},{9,8},{10,11... | collective-permute-start | bytes 393224 | tf_op jit(solution)/shard_map/ppermute | solution.py:312
  (19 other events, 56.9 us)

commit v3 on v2

--- a/solution.py
+++ b/solution.py
@@ -65,8 +65,16 @@
         copies.append(pltpu.make_async_copy(source, piece, sems.at[2 + mask]))
     for copy in copies:
         copy.start()
-    for copy in copies[:2]:
-        copy.wait()
+    copies[0].wait()
+    deals = [
+        pltpu.make_async_copy(
+            wide_ref.at[:, (b + 1) * span - width : (b + 1) * span], dealt_ref.at[b], sems.at[2 + blocks + b]
+        )
+        for b in range(blocks)
+    ]
+    for deal in deals:
+        deal.start()
+    copies[1].wait()
     factors = out_ref.shape[0]
     seed = table_ref[...]
     coarse = (seed >> 3) << 3
@@ -74,9 +82,7 @@
     both = jnp.concatenate([coarse.astype(F32).astype(BF16), fine.astype(F32).astype(BF16)], axis=0)
     tall = lax.dot_general(both, wide_ref[...], (((1,), (1,)), ((), ())), preferred_element_type=F32)
     out_ref[...] = (tall[:factors] + tall[factors:]) / 1000.0
-    for b in range(blocks):
-        dealt_ref[b] = wide_ref[:, (b + 1) * span - width : (b + 1) * span]
-    for copy in copies[2:]:
+    for copy in copies[2:] + deals:
         copy.wait()
 
 
@@ -89,11 +95,11 @@
         open_body,
         out_shape=[jax.ShapeDtypeStruct(shape, dtype) for shape, dtype in outs],
         in_specs=smem() + [pl.BlockSpec(memory_space=pltpu.HBM)] * 2,
-        out_specs=vmem(len(outs)),
+        out_specs=vmem(len(outs) - 1) + [pl.BlockSpec(memory_space=pltpu.HBM)],
         scratch_shapes=[
             pltpu.VMEM(returns.shape, BF16),
             pltpu.VMEM(seed.shape, jnp.int32),
-            pltpu.SemaphoreType.DMA((2 + blocks,)),
+            pltpu.SemaphoreType.DMA((2 + 2 * blocks,)),
         ],
         cost_estimate=pl.CostEstimate(
             flops=4 * days * assets * factors, bytes_accessed=returns.size * 2, transcendentals=0
@@ -158,26 +164,22 @@
     return total
 
 
-def apply_first_body(masks, gathered, me_ref, par_ref, own_ref, twin_ref, *rest):
-    pairs = rest[: len(masks)]
-    rest = rest[len(masks) :]
+def apply_first_body(count, gathered, me_ref, par_ref, *rest):
+    slabs, rest = rest[:count], rest[count:]
     me = me_ref[0]
-    days = own_ref.shape[1]
+    days = slabs[0].shape[1]
+
+    def source(mask):
+        return pl.ds(pl.multiple_of((me ^ mask) * days, LANES), days)
+
     if gathered:
         *pieces, block_ref, keep_ref, send_ref, proj_ref, full_ref = rest
         for mask, piece in enumerate(pieces):
-            block_ref[pl.ds(pl.multiple_of((me ^ mask) * days, LANES), days), :] = piece[...]
+            block_ref[source(mask), :] = piece[...]
     else:
         block_ref, keep_ref, send_ref, proj_ref, full_ref = rest
-
-    def place(source, value):
-        proj_ref[:, pl.ds(pl.multiple_of(source * days, LANES), days)] = value
-
-    place(me, own_ref[...])
-    place(me ^ 1, twin_ref[...])
-    for mask, pair_ref in zip(masks, pairs):
-        place(me ^ mask, pair_ref[0])
-        place(me ^ mask ^ 1, pair_ref[1])
+    for mask, ref in enumerate(slabs):
+        proj_ref[:, source(mask)] = ref[...]
     back_project(proj_ref[...], [block_ref], full_ref)
     lane_halves(par_ref, full_ref, keep_ref, send_ref)
 
@@ -365,12 +367,12 @@
     unit = 2 * LANES
     cut = span * CUT // 8 // unit * unit
     rest = span - cut
-    masks = tuple(range(2, blocks, 2))
 
     own, *pieces, dealt = opening(me, returns, start_seed.T, blocks, cut)
-    twin = swap(own, "gr", 1)
-    both = jnp.stack([own, twin])
-    pairs = [swap(both, "gr", m) for m in masks]
+    even = tuple(range(0, blocks, 2))
+    near = [own if m == 0 else swap(own, "gr", m) for m in even]
+    far = [swap(x, "gr", 1) for x in near]
+    shared = [x for pair in zip(near, far) for x in pair]
     pieces = [p if m == 0 else swap(p, "gr", m) for m, p in enumerate(pieces)]
     last = lax.all_to_all(dealt, "gr", 0, 0).reshape(slab_days, rest)
 
@@ -378,16 +380,15 @@
     full_assets = pltpu.VMEM((factors, span), F32)
     slab = pltpu.VMEM((factors, slab_days), F32)
 
-    shared = [own, twin, *pairs]
     block, keep, send = call(
-        functools.partial(apply_first_body, masks, True),
+        functools.partial(apply_first_body, blocks, True),
         [((slab_days, cut), BF16)] + [((factors, cut // 2), F32)] * 2, [me, par],
         shared + pieces, dots, [slab, pltpu.VMEM((factors, cut), F32)],
     )
     mine = sum_days(keep, send)
     theirs = swap(mine, "gc", 1)
     keep, send = call(
-        functools.partial(apply_first_body, masks, False), [((factors, rest // 2), F32)] * 2, [me, par],
+        functools.partial(apply_first_body, blocks, False), [((factors, rest // 2), F32)] * 2, [me, par],
         shared + [last], dots, [slab, pltpu.VMEM((factors, rest), F32)],
     )
     mine_late = sum_days(keep, send)

time: 134 us -> 135 us (level)
  waiting for transfers between devices: 53 us -> 63.9 us
  starting transfers between devices: 63.4 us -> 53.7 us
    ppermute x47 -> x50, waiting for transfers between devices: 50.3 us -> 61.5 us  [swap(): return lax.ppermute(x, axis, [(s, s ^ mask) for s in range(size)])]
    ppermute x47 -> x50, starting transfers between devices: 56 us -> 46.3 us  [swap(): return lax.ppermute(x, axis, [(s, s ^ mask) for s in range(size)])]
  transfers between devices with their start and end apart: 51 -> 54, of which waited for: 26 -> 31; matrix products, arithmetic and copies ran while one was open for 0% -> 0% of each run, Pallas kernels for 6% -> 6%
where the time goes in v3:
time: 135 us; the launch traced here: 134 us
  waiting for transfers between devices  63.9 us (47%)
  starting transfers between devices  53.7 us (40%)
  Pallas kernels  15.7 us (12%)
    ppermute x50, waiting for transfers between devices, swap(): return lax.ppermute(x, axis, [(s, s ^ mask) for s in range(size)])  61.5 us
    ppermute x50, starting transfers between devices, swap(): return lax.ppermute(x, axis, [(s, s ^ mask) for s in range(size)])  46.3 us
    pallas_call x13, Pallas kernels, call(): pl.pallas_call(body, out_shape=[jax.ShapeDtypeStruct(shape, dtype) for sh...  12.6 us
    all_to_all x1, starting transfers between devices, local(): last = lax.all_to_all(dealt, 'gr', 0, 0).reshape(slab_days, rest)  5.2 us
    pallas_call x1, Pallas kernels, opening(): pl.pallas_call(open_body, out_shape=[jax.ShapeDtypeStruct(shape, dtype) f...  3.13 us
  transfers between devices with their start and end apart: 54, of which 31 were waited for; matrix products, arithmetic and copies ran while one was open for 0% of the time, Pallas kernels for 6%

profile of v3, /device:TPU:0, one launch (start us, length us, event | category | flops | bytes accessed | tf_op | source)
XLA Modules:
  0.0 134.5 jit_solution(4305638950797602521)
XLA Ops:
  0.6 3.1 %shard_map.41 = (f32[64,128]{1,0:T(8,128)S(1)}, bf16[128,512]{1,0:T(8,128)(2,1)S(1)}, bf16[128,512]{1,0:T(8,128)(2,1)S(1)}, bf16[128,512]{1,0:T(8,128)(2,1)S(1)}...) custom-call(s32[1]{0:T(128)} %bitcast.2.me_ref, ...), custom_call_target="tpu_custom_call" | custom-call | flops 268435456 | bytes 2097152 | tf_op jit(solution)/shard_map/pallas_call | solution.py:94
  3.8 5.2 %all-to-all-start = ((bf16[8,128,512]{2,1,0:T(8,128)(2,1)}), bf16[8,128,512]{2,1,0:T(8,128)(2,1)S(1)}, u32[]{:S(2)}, u32[]{:S(2)}) async-start(bf16[8,128,512]{2,1,0:T(8,128)(2,1)} %get-tuple-element.54), calls=%async_computation | async-start | bytes 2097152 | tf_op jit(solution)/shard_map/all_to_all | solution.py:377
  9.5 1.6 %collective-permute-start.8 = (bf16[128,512]{1,0:T(8,128)(2,1)S(1)}, bf16[128,512]{1,0:T(8,128)(2,1)S(1)}, u32[]{:S(2)}, u32[]{:S(2)}) collective-permute-start(bf16[128,512]{1,0:T(8,128)(2,1)S(1)} %get-tuple-element.46), channel_id=1, source_target_pairs={{0,8},{4,12},{8,0},{12,4},{16,24},{20,28},{24,16},{28,20},{1,9},{5... | collective-permute-start | bytes 393224 | tf_op jit(solution)/shard_map/ppermute | solution.py:314
  11.5 1.7 %collective-permute-start.3 = (f32[64,128]{1,0:T(8,128)S(1)}, f32[64,128]{1,0:T(8,128)S(1)}, u32[]{:S(2)}, u32[]{:S(2)}) collective-permute-start(f32[64,128]{1,0:T(8,128)S(1)} %get-tuple-element.43.rest_0_), channel_id=1, source_target_pairs={{0,16},{4,20},{8,24},{12,28},{16,0},{20,4},{24,8},{28,12},{1,17},{... | collective-permute-start | bytes 98312 | tf_op jit(solution)/shard_map/ppermute | solution.py:314
  14.7 12.6 %collective-permute-done.1.rest_2_ = f32[64,128]{1,0:T(8,128)S(1)} collective-permute-done((f32[64,128]{1,0:T(8,128)S(1)}, f32[64,128]{1,0:T(8,128)S(1)}, u32[]{:S(2)}, u32[]{:S(2)}) %collective-permute-start.1) | collective-permute-done | bytes 32800 | tf_op jit(solution)/shard_map/ppermute | solution.py:314
  30.7 2.3 %collective-permute-start.12 = (bf16[128,512]{1,0:T(8,128)(2,1)S(1)}, bf16[128,512]{1,0:T(8,128)(2,1)S(1)}, u32[]{:S(2)}, u32[]{:S(2)}) collective-permute-start(bf16[128,512]{1,0:T(8,128)(2,1)S(1)} %get-tuple-element.50), channel_id=1, source_target_pairs={{0,24},{4,28},{8,16},{12,20},{16,8},{20,12},{24,0},{28,4},{1,25},{... | collective-permute-start | bytes 393224 | tf_op jit(solution)/shard_map/ppermute | solution.py:314
  33.7 7.6 %collective-permute-done.10.rest_12_ = bf16[128,512]{1,0:T(8,128)(2,1)S(1)} collective-permute-done((bf16[128,512]{1,0:T(8,128)(2,1)S(1)}, bf16[128,512]{1,0:T(8,128)(2,1)S(1)}, u32[]{:S(2)}, u32[]{:S(2)}) %collective-permute-start.10) | collective-permute-done | bytes 131104 | tf_op jit(solution)/shard_map/ppermute | solution.py:314
  42.6 1.6 %collective-permute-start.14 = (f32[64,256]{1,0:T(8,128)S(1)}, f32[64,256]{1,0:T(8,128)S(1)}, u32[]{:S(2)}, u32[]{:S(2)}) collective-permute-start(f32[64,256]{1,0:T(8,128)S(1)} %get-tuple-element.53), channel_id=1, source_target_pairs={{0,1},{1,0},{2,3},{3,2},{4,5},{5,4},{6,7},{7,6},{8,9},{9,8},{10,11... | collective-permute-start | bytes 196616 | tf_op jit(solution)/shard_map/ppermute | solution.py:314
  45.2 2.3 %collective-permute-done.14 = f32[64,256]{1,0:T(8,128)S(1)} collective-permute-done((f32[64,256]{1,0:T(8,128)S(1)}, f32[64,256]{1,0:T(8,128)S(1)}, u32[]{:S(2)}, u32[]{:S(2)}) %collective-permute-start.14) | collective-permute-done | bytes 65568 | tf_op jit(solution)/shard_map/ppermute | solution.py:314
  47.5 2.7 %collective-permute-start.15 = (f32[64,256]{1,0:T(8,128)S(1)}, f32[64,256]{1,0:T(8,128)S(1)}, u32[]{:S(2)}, u32[]{:S(2)}) collective-permute-start(f32[64,256]{1,0:T(8,128)S(1)} %add.99), channel_id=1, source_target_pairs={{0,2},{1,3},{2,0},{3,1},{4,6},{5,7},{6,4},{7,5},{8,10},{9,11},{10,... | collective-permute-start | bytes 196616 | tf_op jit(solution)/shard_map/ppermute | solution.py:314
  50.2 1.7 %collective-permute-start.18 = (f32[64,256]{1,0:T(8,128)S(1)}, f32[64,256]{1,0:T(8,128)S(1)}, u32[]{:S(2)}, u32[]{:S(2)}) collective-permute-start(f32[64,256]{1,0:T(8,128)S(1)} %add.101), channel_id=1, source_target_pairs={{0,2},{1,3},{2,0},{3,1},{4,6},{5,7},{6,4},{7,5},{8,10},{9,11},{10,... | collective-permute-start | bytes 196616 | tf_op jit(solution)/shard_map/ppermute | solution.py:314
  51.9 2.3 %collective-permute-done.15 = f32[64,256]{1,0:T(8,128)S(1)} collective-permute-done((f32[64,256]{1,0:T(8,128)S(1)}, f32[64,256]{1,0:T(8,128)S(1)}, u32[]{:S(2)}, u32[]{:S(2)}) %collective-permute-start.15) | collective-permute-done | bytes 65568 | tf_op jit(solution)/shard_map/ppermute | solution.py:314
  54.2 2.1 %collective-permute-start.16 = (f32[64,256]{1,0:T(8,128)S(1)}, f32[64,256]{1,0:T(8,128)S(1)}, u32[]{:S(2)}, u32[]{:S(2)}) collective-permute-start(f32[64,256]{1,0:T(8,128)S(1)} %add.100.rest_0_), channel_id=1, source_target_pairs={{0,1},{1,0},{2,3},{3,2},{4,5},{5,4},{6,7},{7,6},{8,9},{9,8},{10,11... | collective-permute-start | bytes 196616 | tf_op jit(solution)/shard_map/ppermute | solution.py:314
  58.6 2.7 %collective-permute-done.19.rest_3_ = f32[64,256]{1,0:T(8,128)S(1)} collective-permute-done((f32[64,256]{1,0:T(8,128)S(1)}, f32[64,256]{1,0:T(8,128)S(1)}, u32[]{:S(2)}, u32[]{:S(2)}) %collective-permute-start.19) | collective-permute-done | bytes 65568 | tf_op jit(solution)/shard_map/ppermute | solution.py:314
  65.8 2.4 %collective-permute-done.21 = f32[16,1152]{1,0:T(8,128)S(1)} collective-permute-done((f32[16,1152]{1,0:T(8,128)S(1)}, f32[16,1152]{1,0:T(8,128)S(1)}, u32[]{:S(2)}, u32[]{:S(2)}) %collective-permute-start.21) | collective-permute-done | bytes 73760 | tf_op jit(solution)/shard_map/ppermute | solution.py:314
  70.4 2.2 %collective-permute-done.22 = f32[16,1152]{1,0:T(8,128)S(1)} collective-permute-done((f32[16,1152]{1,0:T(8,128)S(1)}, f32[16,1152]{1,0:T(8,128)S(1)}, u32[]{:S(2)}, u32[]{:S(2)}) %collective-permute-start.22) | collective-permute-done | bytes 73760 | tf_op jit(solution)/shard_map/ppermute | solution.py:314
  77.4 2.4 %collective-permute-done.24 = f32[32,512]{1,0:T(8,128)S(1)} collective-permute-done((f32[32,512]{1,0:T(8,128)S(1)}, f32[32,512]{1,0:T(8,128)S(1)}, u32[]{:S(2)}, u32[]{:S(2)}) %collective-permute-start.24) | collective-permute-done | bytes 65568 | tf_op jit(solution)/shard_map/ppermute | solution.py:314
  79.8 2.2 %collective-permute-start.25 = (f32[32,512]{1,0:T(8,128)S(1)}, f32[32,512]{1,0:T(8,128)S(1)}, u32[]{:S(2)}, u32[]{:S(2)}) collective-permute-start(f32[32,512]{1,0:T(8,128)S(1)} %add.106), channel_id=1, source_target_pairs={{0,2},{1,3},{2,0},{3,1},{4,6},{5,7},{6,4},{7,5},{8,10},{9,11},{10,... | collective-permute-start | bytes 196616 | tf_op jit(solution)/shard_map/ppermute | solution.py:314
  82.0 1.5 %collective-permute-start.38 = (f32[32,512]{1,0:T(8,128)S(1)}, f32[32,512]{1,0:T(8,128)S(1)}, u32[]{:S(2)}, u32[]{:S(2)}) collective-permute-start(f32[32,512]{1,0:T(8,128)S(1)} %add.116), channel_id=1, source_target_pairs={{0,2},{1,3},{2,0},{3,1},{4,6},{5,7},{6,4},{7,5},{8,10},{9,11},{10,... | collective-permute-start | bytes 196616 | tf_op jit(solution)/shard_map/ppermute | solution.py:314
  83.6 3.3 %collective-permute-done.25 = f32[32,512]{1,0:T(8,128)S(1)} collective-permute-done((f32[32,512]{1,0:T(8,128)S(1)}, f32[32,512]{1,0:T(8,128)S(1)}, u32[]{:S(2)}, u32[]{:S(2)}) %collective-permute-start.25) | collective-permute-done | bytes 65568 | tf_op jit(solution)/shard_map/ppermute | solution.py:314
  89.1 1.6 %shard_map.46 = (f32[64,64]{1,0:T(8,128)S(1)}, f32[1,64]{1,0:T(1,128)S(1)}) custom-call(s32[1]{0:T(128)} %bitcast.1.core_ref, f32[16,1152]{1,0:T(8,128)S(1)} %add.105.mine_ref, f32[16,1152]{1,0:T(8,128)S(1)} %collective-permute-done.23.theirs_ref, f32[16,1152]{1,0:T(8,128)S(1)} %add.110.mine_late_ref.mine_ref, ...), custom_call_target="tpu_custom_call" | custom-call | flops 201326592 | bytes 16640 | tf_op jit(solution)/shard_map/pallas_call | solution.py:31
  96.9 2.1 %collective-permute-done.32 = f32[16,1152]{1,0:T(8,128)S(1)} collective-permute-done((f32[16,1152]{1,0:T(8,128)S(1)}, f32[16,1152]{1,0:T(8,128)S(1)}, u32[]{:S(2)}, u32[]{:S(2)}) %collective-permute-start.32) | collective-permute-done | bytes 73760 | tf_op jit(solution)/shard_map/ppermute | solution.py:314
  101.2 2.2 %collective-permute-done.33 = f32[16,1152]{1,0:T(8,128)S(1)} collective-permute-done((f32[16,1152]{1,0:T(8,128)S(1)}, f32[16,1152]{1,0:T(8,128)S(1)}, u32[]{:S(2)}, u32[]{:S(2)}) %collective-permute-start.33) | collective-permute-done | bytes 73760 | tf_op jit(solution)/shard_map/ppermute | solution.py:314
  108.1 2.4 %collective-permute-done.35 = f32[32,512]{1,0:T(8,128)S(1)} collective-permute-done((f32[32,512]{1,0:T(8,128)S(1)}, f32[32,512]{1,0:T(8,128)S(1)}, u32[]{:S(2)}, u32[]{:S(2)}) %collective-permute-start.35) | collective-permute-done | bytes 65568 | tf_op jit(solution)/shard_map/ppermute | solution.py:314
  110.5 1.7 %collective-permute-start.36 = (f32[32,512]{1,0:T(8,128)S(1)}, f32[32,512]{1,0:T(8,128)S(1)}, u32[]{:S(2)}, u32[]{:S(2)}) collective-permute-start(f32[32,512]{1,0:T(8,128)S(1)} %add.114), channel_id=1, source_target_pairs={{0,2},{1,3},{2,0},{3,1},{4,6},{5,7},{6,4},{7,5},{8,10},{9,11},{10,... | collective-permute-start | bytes 196616 | tf_op jit(solution)/shard_map/ppermute | solution.py:314
  112.2 2.1 %collective-permute-start.45 = (f32[32,512]{1,0:T(8,128)S(1)}, f32[32,512]{1,0:T(8,128)S(1)}, u32[]{:S(2)}, u32[]{:S(2)}) collective-permute-start(f32[32,512]{1,0:T(8,128)S(1)} %add.121), channel_id=1, source_target_pairs={{0,2},{1,3},{2,0},{3,1},{4,6},{5,7},{6,4},{7,5},{8,10},{9,11},{10,... | collective-permute-start | bytes 196616 | tf_op jit(solution)/shard_map/ppermute | solution.py:314
  114.3 1.6 %shard_map.52 = (f32[64,64]{1,0:T(8,128)S(1)}, f32[1,64]{1,0:T(1,128)S(1)}) custom-call(s32[1]{0:T(128)} %bitcast.1.core_ref, f32[16,1152]{1,0:T(8,128)S(1)} %add.113.mine_ref, f32[16,1152]{1,0:T(8,128)S(1)} %collective-permute-done.34.theirs_ref, f32[16,1152]{1,0:T(8,128)S(1)} %add.120.mine_ref.mine_late_ref, ...), custom_call_target="tpu_custom_call" | custom-call | flops 201326592 | bytes 16640 | tf_op jit(solution)/shard_map/pallas_call | solution.py:31
  121.0 1.6 %collective-permute-done.48 = f32[32,128]{1,0:T(8,128)S(1)} collective-permute-done((f32[32,128]{1,0:T(8,128)S(1)}, f32[32,128]{1,0:T(8,128)S(1)}, u32[]{:S(2)}, u32[]{:S(2)}) %collective-permute-start.48) | collective-permute-done | bytes 16416 | tf_op jit(solution)/shard_map/ppermute | solution.py:320
  123.4 1.5 %collective-permute-start.51 = (f32[32,128]{1,0:T(8,128)S(1)}, f32[32,128]{1,0:T(8,128)S(1)}, u32[]{:S(2)}, u32[]{:S(2)}) collective-permute-start(f32[32,128]{1,0:T(8,128)S(1)} %add_add_fusion.1), channel_id=1, source_target_pairs={{0,16},{4,20},{8,24},{12,28},{16,0},{20,4},{24,8},{28,12},{1,17},{... | collective-permute-start | bytes 49160 | tf_op jit(solution)/shard_map/ppermute | solution.py:314
  127.8 1.7 %collective-permute-done.52 = f32[32,128]{1,0:T(8,128)S(1)} collective-permute-done((f32[32,128]{1,0:T(8,128)S(1)}, f32[32,128]{1,0:T(8,128)S(1)}, u32[]{:S(2)}, u32[]{:S(2)}) %collective-permute-start.52) | collective-permute-done | bytes 16416 | tf_op jit(solution)/shard_map/ppermute | solution.py:314
  129.9 2.0 %collective-permute-done.46.theirs_ref = f32[64,512]{1,0:T(8,128)S(1)} collective-permute-done((f32[64,512]{1,0:T(8,128)S(1)}, f32[64,512]{1,0:T(8,128)S(1)}, u32[]{:S(2)}, u32[]{:S(2)}) %collective-permute-start.46) | collective-permute-done | bytes 131104 | tf_op jit(solution)/shard_map/ppermute | solution.py:314
  131.9 2.6 %shard_map.54 = (f32[64,1024]{1,0:T(8,128)}, f32[3,64]{1,0:T(4,128)}) custom-call(s32[1]{0:T(128)} %bitcast.par_ref, f32[64,512]{1,0:T(8,128)S(1)} %get-tuple-element.78.mine_ref, f32[64,512]{1,0:T(8,128)S(1)} %collective-permute-done.46.theirs_ref, f32[32,128]{1,0:T(8,128)S(1)} %add_add_fusion.gram_ref, f32[1,64]{1,0:T(1,128)S(1)} %get-tuple-element.80.rest_0_, ...), custom_call_target="tpu_custom_call" | custom-call | flops 402653184 | bytes 262912 | tf_op jit(solution)/shard_map/pallas_call | solution.py:31
  (116 shorter events, 46.6 us)
Async XLA Ops:
  3.8 40.5 %all-to-all-start = ((bf16[8,128,512]{2,1,0:T(8,128)(2,1)}), bf16[8,128,512]{2,1,0:T(8,128)(2,1)S(1)}, u32[]{:S(2)}, u32[]{:S(2)}) async-start(bf16[8,128,512]{2,1,0:T(8,128)(2,1)} %get-tuple-element.54), calls=%async_computation | async-start | bytes 2097152 | tf_op jit(solution)/shard_map/all_to_all | solution.py:377
  9.0 21.7 %collective-permute-start.7 = (bf16[128,512]{1,0:T(8,128)(2,1)S(1)}, bf16[128,512]{1,0:T(8,128)(2,1)S(1)}, u32[]{:S(2)}, u32[]{:S(2)}) collective-permute-start(bf16[128,512]{1,0:T(8,128)(2,1)S(1)} %get-tuple-element.45), channel_id=1, source_target_pairs={{0,4},{4,0},{8,12},{12,8},{16,20},{20,16},{24,28},{28,24},{1,5},{5... | collective-permute-start | bytes 393224 | tf_op jit(solution)/shard_map/ppermute | solution.py:314
  9.5 23.4 %collective-permute-start.8 = (bf16[128,512]{1,0:T(8,128)(2,1)S(1)}, bf16[128,512]{1,0:T(8,128)(2,1)S(1)}, u32[]{:S(2)}, u32[]{:S(2)}) collective-permute-start(bf16[128,512]{1,0:T(8,128)(2,1)S(1)} %get-tuple-element.46), channel_id=1, source_target_pairs={{0,8},{4,12},{8,0},{12,4},{16,24},{20,28},{24,16},{28,20},{1,9},{5... | collective-permute-start | bytes 393224 | tf_op jit(solution)/shard_map/ppermute | solution.py:314
  11.2 16.1 %collective-permute-start.1 = (f32[64,128]{1,0:T(8,128)S(1)}, f32[64,128]{1,0:T(8,128)S(1)}, u32[]{:S(2)}, u32[]{:S(2)}) collective-permute-start(f32[64,128]{1,0:T(8,128)S(1)} %get-tuple-element.43.rest_0_), channel_id=1, source_target_pairs={{0,8},{4,12},{8,0},{12,4},{16,24},{20,28},{24,16},{28,20},{1,9},{5... | collective-permute-start | bytes 98312 | tf_op jit(solution)/shard_map/ppermute | solution.py:314
  11.5 15.8 %collective-permute-start.3 = (f32[64,128]{1,0:T(8,128)S(1)}, f32[64,128]{1,0:T(8,128)S(1)}, u32[]{:S(2)}, u32[]{:S(2)}) collective-permute-start(f32[64,128]{1,0:T(8,128)S(1)} %get-tuple-element.43.rest_0_), channel_id=1, source_target_pairs={{0,16},{4,20},{8,24},{12,28},{16,0},{20,4},{24,8},{28,12},{1,17},{... | collective-permute-start | bytes 98312 | tf_op jit(solution)/shard_map/ppermute | solution.py:314
  13.3 15.3 %collective-permute-start.5 = (f32[64,128]{1,0:T(8,128)S(1)}, f32[64,128]{1,0:T(8,128)S(1)}, u32[]{:S(2)}, u32[]{:S(2)}) collective-permute-start(f32[64,128]{1,0:T(8,128)S(1)} %get-tuple-element.43.rest_0_), channel_id=1, source_target_pairs={{0,24},{4,28},{8,16},{12,20},{16,8},{20,12},{24,0},{28,4},{1,25},{... | collective-permute-start | bytes 98312 | tf_op jit(solution)/shard_map/ppermute | solution.py:314
  28.6 5.1 %collective-permute-start.9 = (bf16[128,512]{1,0:T(8,128)(2,1)S(1)}, bf16[128,512]{1,0:T(8,128)(2,1)S(1)}, u32[]{:S(2)}, u32[]{:S(2)}) collective-permute-start(bf16[128,512]{1,0:T(8,128)(2,1)S(1)} %get-tuple-element.47), channel_id=1, source_target_pairs={{0,12},{4,8},{8,4},{12,0},{16,28},{20,24},{24,20},{28,16},{1,13},{... | collective-permute-start | bytes 393224 | tf_op jit(solution)/shard_map/ppermute | solution.py:314
  29.3 12.0 %collective-permute-start.10 = (bf16[128,512]{1,0:T(8,128)(2,1)S(1)}, bf16[128,512]{1,0:T(8,128)(2,1)S(1)}, u32[]{:S(2)}, u32[]{:S(2)}) collective-permute-start(bf16[128,512]{1,0:T(8,128)(2,1)S(1)} %get-tuple-element.48), channel_id=1, source_target_pairs={{0,16},{4,20},{8,24},{12,28},{16,0},{20,4},{24,8},{28,12},{1,17},{... | collective-permute-start | bytes 393224 | tf_op jit(solution)/shard_map/ppermute | solution.py:314
  30.4 11.8 %collective-permute-start.11 = (bf16[128,512]{1,0:T(8,128)(2,1)S(1)}, bf16[128,512]{1,0:T(8,128)(2,1)S(1)}, u32[]{:S(2)}, u32[]{:S(2)}) collective-permute-start(bf16[128,512]{1,0:T(8,128)(2,1)S(1)} %get-tuple-element.49), channel_id=1, source_target_pairs={{0,20},{4,16},{8,28},{12,24},{16,4},{20,0},{24,12},{28,8},{1,21},{... | collective-permute-start | bytes 393224 | tf_op jit(solution)/shard_map/ppermute | solution.py:314
  30.7 11.5 %collective-permute-start.12 = (bf16[128,512]{1,0:T(8,128)(2,1)S(1)}, bf16[128,512]{1,0:T(8,128)(2,1)S(1)}, u32[]{:S(2)}, u32[]{:S(2)}) collective-permute-start(bf16[128,512]{1,0:T(8,128)(2,1)S(1)} %get-tuple-element.50), channel_id=1, source_target_pairs={{0,24},{4,28},{8,16},{12,20},{16,8},{20,12},{24,0},{28,4},{1,25},{... | collective-permute-start | bytes 393224 | tf_op jit(solution)/shard_map/ppermute | solution.py:314
  32.9 9.2 %collective-permute-start.13 = (bf16[128,512]{1,0:T(8,128)(2,1)S(1)}, bf16[128,512]{1,0:T(8,128)(2,1)S(1)}, u32[]{:S(2)}, u32[]{:S(2)}) collective-permute-start(bf16[128,512]{1,0:T(8,128)(2,1)S(1)} %get-tuple-element.51), channel_id=1, source_target_pairs={{0,28},{4,24},{8,20},{12,16},{16,12},{20,8},{24,4},{28,0},{1,29},{... | collective-permute-start | bytes 393224 | tf_op jit(solution)/shard_map/ppermute | solution.py:314
  42.6 4.9 %collective-permute-start.14 = (f32[64,256]{1,0:T(8,128)S(1)}, f32[64,256]{1,0:T(8,128)S(1)}, u32[]{:S(2)}, u32[]{:S(2)}) collective-permute-start(f32[64,256]{1,0:T(8,128)S(1)} %get-tuple-element.53), channel_id=1, source_target_pairs={{0,1},{1,0},{2,3},{3,2},{4,5},{5,4},{6,7},{7,6},{8,9},{9,8},{10,11... | collective-permute-start | bytes 196616 | tf_op jit(solution)/shard_map/ppermute | solution.py:314
  44.7 5.5 %collective-permute-start.17 = (f32[64,256]{1,0:T(8,128)S(1)}, f32[64,256]{1,0:T(8,128)S(1)}, u32[]{:S(2)}, u32[]{:S(2)}) collective-permute-start(f32[64,256]{1,0:T(8,128)S(1)} %get-tuple-element.56), channel_id=1, source_target_pairs={{0,1},{1,0},{2,3},{3,2},{4,5},{5,4},{6,7},{7,6},{8,9},{9,8},{10,11... | collective-permute-start | bytes 196616 | tf_op jit(solution)/shard_map/ppermute | solution.py:314
  47.5 6.7 %collective-permute-start.15 = (f32[64,256]{1,0:T(8,128)S(1)}, f32[64,256]{1,0:T(8,128)S(1)}, u32[]{:S(2)}, u32[]{:S(2)}) collective-permute-start(f32[64,256]{1,0:T(8,128)S(1)} %add.99), channel_id=1, source_target_pairs={{0,2},{1,3},{2,0},{3,1},{4,6},{5,7},{6,4},{7,5},{8,10},{9,11},{10,... | collective-permute-start | bytes 196616 | tf_op jit(solution)/shard_map/ppermute | solution.py:314
  50.2 6.8 %collective-permute-start.18 = (f32[64,256]{1,0:T(8,128)S(1)}, f32[64,256]{1,0:T(8,128)S(1)}, u32[]{:S(2)}, u32[]{:S(2)}) collective-permute-start(f32[64,256]{1,0:T(8,128)S(1)} %add.101), channel_id=1, source_target_pairs={{0,2},{1,3},{2,0},{3,1},{4,6},{5,7},{6,4},{7,5},{8,10},{9,11},{10,... | collective-permute-start | bytes 196616 | tf_op jit(solution)/shard_map/ppermute | solution.py:314
  54.2 4.4 %collective-permute-start.16 = (f32[64,256]{1,0:T(8,128)S(1)}, f32[64,256]{1,0:T(8,128)S(1)}, u32[]{:S(2)}, u32[]{:S(2)}) collective-permute-start(f32[64,256]{1,0:T(8,128)S(1)} %add.100.rest_0_), channel_id=1, source_target_pairs={{0,1},{1,0},{2,3},{3,2},{4,5},{5,4},{6,7},{7,6},{8,9},{9,8},{10,11... | collective-permute-start | bytes 196616 | tf_op jit(solution)/shard_map/ppermute | solution.py:314
  63.8 4.4 %collective-permute-start.21 = (f32[16,1152]{1,0:T(8,128)S(1)}, f32[16,1152]{1,0:T(8,128)S(1)}, u32[]{:S(2)}, u32[]{:S(2)}) collective-permute-start(f32[16,1152]{1,0:T(8,128)S(1)} %add.103), channel_id=1, source_target_pairs={{0,8},{4,12},{8,0},{12,4},{16,24},{20,28},{24,16},{28,20},{1,9},{5... | collective-permute-start | bytes 221192 | tf_op jit(solution)/shard_map/ppermute | solution.py:314
  65.3 4.4 %collective-permute-start.28 = (f32[16,1152]{1,0:T(8,128)S(1)}, f32[16,1152]{1,0:T(8,128)S(1)}, u32[]{:S(2)}, u32[]{:S(2)}) collective-permute-start(f32[16,1152]{1,0:T(8,128)S(1)} %add.108), channel_id=1, source_target_pairs={{0,16},{4,20},{8,24},{12,28},{16,0},{20,4},{24,8},{28,12},{1,17},{... | collective-permute-start | bytes 221192 | tf_op jit(solution)/shard_map/ppermute | solution.py:314
  68.2 4.4 %collective-permute-start.22 = (f32[16,1152]{1,0:T(8,128)S(1)}, f32[16,1152]{1,0:T(8,128)S(1)}, u32[]{:S(2)}, u32[]{:S(2)}) collective-permute-start(f32[16,1152]{1,0:T(8,128)S(1)} %add.104), channel_id=1, source_target_pairs={{0,16},{4,20},{8,24},{12,28},{16,0},{20,4},{24,8},{28,12},{1,17},{... | collective-permute-start | bytes 221192 | tf_op jit(solution)/shard_map/ppermute | solution.py:314
  69.7 4.4 %collective-permute-start.29 = (f32[16,1152]{1,0:T(8,128)S(1)}, f32[16,1152]{1,0:T(8,128)S(1)}, u32[]{:S(2)}, u32[]{:S(2)}) collective-permute-start(f32[16,1152]{1,0:T(8,128)S(1)} %add.109), channel_id=1, source_target_pairs={{0,8},{4,12},{8,0},{12,4},{16,24},{20,28},{24,16},{28,20},{1,9},{5... | collective-permute-start | bytes 221192 | tf_op jit(solution)/shard_map/ppermute | solution.py:314
  74.8 5.0 %collective-permute-start.24 = (f32[32,512]{1,0:T(8,128)S(1)}, f32[32,512]{1,0:T(8,128)S(1)}, u32[]{:S(2)}, u32[]{:S(2)}) collective-permute-start(f32[32,512]{1,0:T(8,128)S(1)} %get-tuple-element.61), channel_id=1, source_target_pairs={{0,1},{1,0},{2,3},{3,2},{4,5},{5,4},{6,7},{7,6},{8,9},{9,8},{10,11... | collective-permute-start | bytes 196616 | tf_op jit(solution)/shard_map/ppermute | solution.py:314
  76.0 6.0 %collective-permute-start.37 = (f32[32,512]{1,0:T(8,128)S(1)}, f32[32,512]{1,0:T(8,128)S(1)}, u32[]{:S(2)}, u32[]{:S(2)}) collective-permute-start(f32[32,512]{1,0:T(8,128)S(1)} %get-tuple-element.70), channel_id=1, source_target_pairs={{0,1},{1,0},{2,3},{3,2},{4,5},{5,4},{6,7},{7,6},{8,9},{9,8},{10,11... | collective-permute-start | bytes 196616 | tf_op jit(solution)/shard_map/ppermute | solution.py:314
  79.8 7.1 %collective-permute-start.25 = (f32[32,512]{1,0:T(8,128)S(1)}, f32[32,512]{1,0:T(8,128)S(1)}, u32[]{:S(2)}, u32[]{:S(2)}) collective-permute-start(f32[32,512]{1,0:T(8,128)S(1)} %add.106), channel_id=1, source_target_pairs={{0,2},{1,3},{2,0},{3,1},{4,6},{5,7},{6,4},{7,5},{8,10},{9,11},{10,... | collective-permute-start | bytes 196616 | tf_op jit(solution)/shard_map/ppermute | solution.py:314
  82.0 6.5 %collective-permute-start.38 = (f32[32,512]{1,0:T(8,128)S(1)}, f32[32,512]{1,0:T(8,128)S(1)}, u32[]{:S(2)}, u32[]{:S(2)}) collective-permute-start(f32[32,512]{1,0:T(8,128)S(1)} %add.116), channel_id=1, source_target_pairs={{0,2},{1,3},{2,0},{3,1},{4,6},{5,7},{6,4},{7,5},{8,10},{9,11},{10,... | collective-permute-start | bytes 196616 | tf_op jit(solution)/shard_map/ppermute | solution.py:314
  86.9 4.8 %collective-permute-start.26 = (f32[32,512]{1,0:T(8,128)S(1)}, f32[32,512]{1,0:T(8,128)S(1)}, u32[]{:S(2)}, u32[]{:S(2)}) collective-permute-start(f32[32,512]{1,0:T(8,128)S(1)} %add.107.mine_ref), channel_id=1, source_target_pairs={{0,1},{1,0},{2,3},{3,2},{4,5},{5,4},{6,7},{7,6},{8,9},{9,8},{10,11... | collective-permute-start | bytes 196616 | tf_op jit(solution)/shard_map/ppermute | solution.py:314
  95.6 4.9 %collective-permute-start.41 = (f32[16,1152]{1,0:T(8,128)S(1)}, f32[16,1152]{1,0:T(8,128)S(1)}, u32[]{:S(2)}, u32[]{:S(2)}) collective-permute-start(f32[16,1152]{1,0:T(8,128)S(1)} %add.118), channel_id=1, source_target_pairs={{0,16},{4,20},{8,24},{12,28},{16,0},{20,4},{24,8},{28,12},{1,17},{... | collective-permute-start | bytes 221192 | tf_op jit(solution)/shard_map/ppermute | solution.py:314
  105.5 5.0 %collective-permute-start.35 = (f32[32,512]{1,0:T(8,128)S(1)}, f32[32,512]{1,0:T(8,128)S(1)}, u32[]{:S(2)}, u32[]{:S(2)}) collective-permute-start(f32[32,512]{1,0:T(8,128)S(1)} %get-tuple-element.68), channel_id=1, source_target_pairs={{0,1},{1,0},{2,3},{3,2},{4,5},{5,4},{6,7},{7,6},{8,9},{9,8},{10,11... | collective-permute-start | bytes 196616 | tf_op jit(solution)/shard_map/ppermute | solution.py:314
  106.7 5.5 %collective-permute-start.44 = (f32[32,512]{1,0:T(8,128)S(1)}, f32[32,512]{1,0:T(8,128)S(1)}, u32[]{:S(2)}, u32[]{:S(2)}) collective-permute-start(f32[32,512]{1,0:T(8,128)S(1)} %get-tuple-element.76), channel_id=1, source_target_pairs={{0,1},{1,0},{2,3},{3,2},{4,5},{5,4},{6,7},{7,6},{8,9},{9,8},{10,11... | collective-permute-start | bytes 196616 | tf_op jit(solution)/shard_map/ppermute | solution.py:314
  110.5 6.9 %collective-permute-start.36 = (f32[32,512]{1,0:T(8,128)S(1)}, f32[32,512]{1,0:T(8,128)S(1)}, u32[]{:S(2)}, u32[]{:S(2)}) collective-permute-start(f32[32,512]{1,0:T(8,128)S(1)} %add.114), channel_id=1, source_target_pairs={{0,2},{1,3},{2,0},{3,1},{4,6},{5,7},{6,4},{7,5},{8,10},{9,11},{10,... | collective-permute-start | bytes 196616 | tf_op jit(solution)/shard_map/ppermute | solution.py:314
  112.2 5.9 %collective-permute-start.45 = (f32[32,512]{1,0:T(8,128)S(1)}, f32[32,512]{1,0:T(8,128)S(1)}, u32[]{:S(2)}, u32[]{:S(2)}) collective-permute-start(f32[32,512]{1,0:T(8,128)S(1)} %add.121), channel_id=1, source_target_pairs={{0,2},{1,3},{2,0},{3,1},{4,6},{5,7},{6,4},{7,5},{8,10},{9,11},{10,... | collective-permute-start | bytes 196616 | tf_op jit(solution)/shard_map/ppermute | solution.py:314
  124.9 4.6 %collective-permute-start.52 = (f32[32,128]{1,0:T(8,128)S(1)}, f32[32,128]{1,0:T(8,128)S(1)}, u32[]{:S(2)}, u32[]{:S(2)}) collective-permute-start(f32[32,128]{1,0:T(8,128)S(1)} %add_add_fusion.1), channel_id=1, source_target_pairs={{0,24},{4,28},{8,16},{12,20},{16,8},{20,12},{24,0},{28,4},{1,25},{... | collective-permute-start | bytes 49160 | tf_op jit(solution)/shard_map/ppermute | solution.py:314
  126.9 5.0 %collective-permute-start.46 = (f32[64,512]{1,0:T(8,128)S(1)}, f32[64,512]{1,0:T(8,128)S(1)}, u32[]{:S(2)}, u32[]{:S(2)}) collective-permute-start(f32[64,512]{1,0:T(8,128)S(1)} %get-tuple-element.78.mine_ref), channel_id=1, source_target_pairs={{0,1},{1,0},{2,3},{3,2},{4,5},{5,4},{6,7},{7,6},{8,9},{9,8},{10,11... | collective-permute-start | bytes 393224 | tf_op jit(solution)/shard_map/ppermute | solution.py:314
  (22 other events, 60.4 us)

commit v4 on v3

--- a/solution.py
+++ b/solution.py
@@ -227,12 +227,9 @@
 
 
 def project_lead_body(days_all, par_ref, core_ref, mine_ref, theirs_ref, *rest):
-    *block_refs, inv_ref, keep_ref, send_ref, raw_ref, applied_ref, full_ref, out_ref = rest
+    *block_refs, keep_ref, send_ref, applied_ref, full_ref, out_ref = rest
     lane_joined(par_ref, mine_ref, theirs_ref, full_ref)
-    raw = full_ref[...] / days_all
-    half = full_ref.shape[0]
-    applied = jnp.dot(inv_ref[:half, :half], raw, precision=HIGH, preferred_element_type=F32)
-    raw_ref[...] = raw
+    applied = full_ref[...] / days_all
     applied_ref[...] = applied
     days = block_refs[0].shape[0]
     out_ref[:, :days] = forward_project(applied, block_refs)
@@ -240,17 +237,29 @@
     halves(core_ref, out_ref, keep_ref, send_ref)
 
 
-def project_trail_body(days_all, par_ref, core_ref, mine_ref, theirs_ref, raw_ref, lead_ref, *rest):
-    *block_refs, inv_ref, keep_ref, send_ref, full_ref, out_ref = rest
+def project_trail_body(days_all, par_ref, core_ref, mine_ref, theirs_ref, lead_ref, *rest):
+    *block_refs, keep_ref, send_ref, full_ref, out_ref = rest
     lane_joined(par_ref, mine_ref, theirs_ref, full_ref)
-    half = full_ref.shape[0]
-    raw = jnp.concatenate([raw_ref[...], full_ref[...] / days_all], axis=0)
-    applied = jnp.dot(inv_ref[half:, :], raw, precision=HIGH, preferred_element_type=F32)
+    applied = full_ref[...] / days_all
     days = block_refs[0].shape[0]
     out_ref[:, :days] = forward_project(applied, block_refs)
     both = jnp.concatenate([lead_ref[...], applied], axis=0)
     out_ref[:, days:] = widen(gram_of(applied, both), LANES)
     halves(core_ref, out_ref, keep_ref, send_ref)
+
+
+def apply_scaled_body(core_ref, par_ref, mine_ref, theirs_ref, mine_late_ref, theirs_late_ref, inv_ref, *rest):
+    *block_refs, keep_ref, send_ref, keep_late_ref, send_late_ref, proj_ref, full_ref = rest
+    half = keep_ref.shape[0]
+    days = block_refs[0].shape[0]
+    joined(core_ref, mine_ref, theirs_ref, proj_ref)
+    lead = proj_ref[:, :days]
+    joined(core_ref, mine_late_ref, theirs_late_ref, proj_ref)
+    both = jnp.concatenate([lead, proj_ref[:, :days]], axis=0)
+    scaled = jnp.dot(inv_ref[...], both, precision=HIGH, preferred_element_type=F32)
+    back_project(scaled, block_refs, full_ref)
+    lane_halves(par_ref, full_ref.at[:half], keep_ref, send_ref)
+    lane_halves(par_ref, full_ref.at[half:], keep_late_ref, send_late_ref)
 
 
 def eliminate(gram):
@@ -403,15 +412,15 @@
     for sweep in range(ITERS - 1):
         if sweep:
             mine = sum_days(*sent[0])
-            keep, send, raw, applied = call(
-                functools.partial(project_lead_body, days_all), [quarter] * 2 + [rows] * 2, [par, core],
-                [mine, swap(mine, "gc", 1), *block_list, inverse], dots // 2, [part_assets, part_days],
+            keep, send, applied = call(
+                functools.partial(project_lead_body, days_all), [quarter] * 2 + [rows], [par, core],
+                [mine, swap(mine, "gc", 1), *block_list], dots // 2, [part_assets, part_days],
             )
             lead = sum_assets(keep, send, False)
             mine = sum_days(*sent[1])
             keep, send = call(
                 functools.partial(project_trail_body, days_all), [quarter] * 2, [par, core],
-                [mine, swap(mine, "gc", 1), raw, applied, *block_list, inverse], dots // 2,
+                [mine, swap(mine, "gc", 1), applied, *block_list], dots // 2,
                 [part_assets, part_days],
             )
             trail = sum_assets(keep, send, True)
@@ -422,14 +431,21 @@
             )
             lead = sum_assets(*parts[:2], False)
             trail = sum_assets(*parts[2:], True)
-        sent = [
-            call(apply_body, [lane_half] * 2, [core, par], [*pair, *block_list], dots // 2, [part_days, part_assets])
-            for pair in (lead, trail)
-        ]
         inverse, diag_row = call(
             functools.partial(factor_body, slab_days),
             [((factors, factors), F32), ((1, factors), F32)], [core], [*lead, *trail], dots // 2, [part_days],
         )
+        if sweep == 0:
+            outs = call(
+                apply_scaled_body, [lane_half] * 4, [core, par], [*lead, *trail, inverse, *block_list], dots,
+                [part_days, full_assets],
+            )
+            sent = [outs[:2], outs[2:]]
+        else:
+            sent = [
+                call(apply_body, [lane_half] * 2, [core, par], [*pair, *block_list], dots // 2, [part_days, part_assets])
+                for pair in (lead, trail)
+            ]
         diagonals.append(diag_row)
     lead = sum_days(*sent[0])
     trail = sum_days(*sent[1])

time: 135 us -> 137 us (1.015)
  waiting for transfers between devices: 63.9 us -> 65.6 us
    ppermute x50, waiting for transfers between devices: 61.5 us -> 64 us  [swap(): return lax.ppermute(x, axis, [(s, s ^ mask) for s in range(size)])]
    pallas_call x13 -> x12, Pallas kernels: 12.6 us -> 12.2 us  [call(): pl.pallas_call(body, out_shape=[jax.ShapeDtypeStruct(shape, dtype) for sh...]
  transfers between devices with their start and end apart: 54 -> 54, of which waited for: 31 -> 30; matrix products, arithmetic and copies ran while one was open for 0% -> 0% of each run, Pallas kernels for 6% -> 4%
where the time goes in v4:
time: 137 us
  waiting for transfers between devices  65.6 us (48%)
  starting transfers between devices  55 us (40%)
  Pallas kernels  15.4 us (11%)
    ppermute x50, waiting for transfers between devices, swap(): return lax.ppermute(x, axis, [(s, s ^ mask) for s in range(size)])  64 us
    ppermute x50, starting transfers between devices, swap(): return lax.ppermute(x, axis, [(s, s ^ mask) for s in range(size)])  47.6 us
    pallas_call x12, Pallas kernels, call(): pl.pallas_call(body, out_shape=[jax.ShapeDtypeStruct(shape, dtype) for sh...  12.2 us
    all_to_all x1, starting transfers between devices, local(): last = lax.all_to_all(dealt, 'gr', 0, 0).reshape(slab_days, rest)  5.2 us
    pallas_call x1, Pallas kernels, opening(): pl.pallas_call(open_body, out_shape=[jax.ShapeDtypeStruct(shape, dtype) f...  3.13 us
  transfers between devices with their start and end apart: 54, of which 30 were waited for; matrix products, arithmetic and copies ran while one was open for 0% of the time, Pallas kernels for 4%

profile of v4, /device:TPU:0, one launch (start us, length us, event | category | flops | bytes accessed | tf_op | source)
XLA Modules:
  0.0 137.1 jit_solution(7530940691476472190)
XLA Ops:
  0.6 3.1 %shard_map.41 = (f32[64,128]{1,0:T(8,128)S(1)}, bf16[128,512]{1,0:T(8,128)(2,1)S(1)}, bf16[128,512]{1,0:T(8,128)(2,1)S(1)}, bf16[128,512]{1,0:T(8,128)(2,1)S(1)}...) custom-call(s32[1]{0:T(128)} %bitcast.2.me_ref, ...), custom_call_target="tpu_custom_call" | custom-call | flops 268435456 | bytes 2097152 | tf_op jit(solution)/shard_map/pallas_call | solution.py:94
  3.8 5.2 %all-to-all-start = ((bf16[8,128,512]{2,1,0:T(8,128)(2,1)}), bf16[8,128,512]{2,1,0:T(8,128)(2,1)S(1)}, u32[]{:S(2)}, u32[]{:S(2)}) async-start(bf16[8,128,512]{2,1,0:T(8,128)(2,1)} %get-tuple-element.53), calls=%async_computation | async-start | bytes 2097152 | tf_op jit(solution)/shard_map/all_to_all | solution.py:386
  9.5 1.6 %collective-permute-start.8 = (bf16[128,512]{1,0:T(8,128)(2,1)S(1)}, bf16[128,512]{1,0:T(8,128)(2,1)S(1)}, u32[]{:S(2)}, u32[]{:S(2)}) collective-permute-start(bf16[128,512]{1,0:T(8,128)(2,1)S(1)} %get-tuple-element.45), channel_id=1, source_target_pairs={{0,8},{4,12},{8,0},{12,4},{16,24},{20,28},{24,16},{28,20},{1,9},{5... | collective-permute-start | bytes 393224 | tf_op jit(solution)/shard_map/ppermute | solution.py:323
  11.5 1.7 %collective-permute-start.3 = (f32[64,128]{1,0:T(8,128)S(1)}, f32[64,128]{1,0:T(8,128)S(1)}, u32[]{:S(2)}, u32[]{:S(2)}) collective-permute-start(f32[64,128]{1,0:T(8,128)S(1)} %get-tuple-element.42.rest_0_), channel_id=1, source_target_pairs={{0,16},{4,20},{8,24},{12,28},{16,0},{20,4},{24,8},{28,12},{1,17},{... | collective-permute-start | bytes 98312 | tf_op jit(solution)/shard_map/ppermute | solution.py:323
  14.7 12.6 %collective-permute-done.1.rest_2_ = f32[64,128]{1,0:T(8,128)S(1)} collective-permute-done((f32[64,128]{1,0:T(8,128)S(1)}, f32[64,128]{1,0:T(8,128)S(1)}, u32[]{:S(2)}, u32[]{:S(2)}) %collective-permute-start.1) | collective-permute-done | bytes 32800 | tf_op jit(solution)/shard_map/ppermute | solution.py:323
  30.7 2.3 %collective-permute-start.12 = (bf16[128,512]{1,0:T(8,128)(2,1)S(1)}, bf16[128,512]{1,0:T(8,128)(2,1)S(1)}, u32[]{:S(2)}, u32[]{:S(2)}) collective-permute-start(bf16[128,512]{1,0:T(8,128)(2,1)S(1)} %get-tuple-element.49), channel_id=1, source_target_pairs={{0,24},{4,28},{8,16},{12,20},{16,8},{20,12},{24,0},{28,4},{1,25},{... | collective-permute-start | bytes 393224 | tf_op jit(solution)/shard_map/ppermute | solution.py:323
  33.7 7.6 %collective-permute-done.10.rest_12_ = bf16[128,512]{1,0:T(8,128)(2,1)S(1)} collective-permute-done((bf16[128,512]{1,0:T(8,128)(2,1)S(1)}, bf16[128,512]{1,0:T(8,128)(2,1)S(1)}, u32[]{:S(2)}, u32[]{:S(2)}) %collective-permute-start.10) | collective-permute-done | bytes 131104 | tf_op jit(solution)/shard_map/ppermute | solution.py:323
  42.6 1.6 %collective-permute-start.14 = (f32[64,256]{1,0:T(8,128)S(1)}, f32[64,256]{1,0:T(8,128)S(1)}, u32[]{:S(2)}, u32[]{:S(2)}) collective-permute-start(f32[64,256]{1,0:T(8,128)S(1)} %get-tuple-element.52), channel_id=1, source_target_pairs={{0,1},{1,0},{2,3},{3,2},{4,5},{5,4},{6,7},{7,6},{8,9},{9,8},{10,11... | collective-permute-start | bytes 196616 | tf_op jit(solution)/shard_map/ppermute | solution.py:323
  45.2 2.3 %collective-permute-done.14 = f32[64,256]{1,0:T(8,128)S(1)} collective-permute-done((f32[64,256]{1,0:T(8,128)S(1)}, f32[64,256]{1,0:T(8,128)S(1)}, u32[]{:S(2)}, u32[]{:S(2)}) %collective-permute-start.14) | collective-permute-done | bytes 65568 | tf_op jit(solution)/shard_map/ppermute | solution.py:323
  47.5 2.7 %collective-permute-start.15 = (f32[64,256]{1,0:T(8,128)S(1)}, f32[64,256]{1,0:T(8,128)S(1)}, u32[]{:S(2)}, u32[]{:S(2)}) collective-permute-start(f32[64,256]{1,0:T(8,128)S(1)} %add.99), channel_id=1, source_target_pairs={{0,2},{1,3},{2,0},{3,1},{4,6},{5,7},{6,4},{7,5},{8,10},{9,11},{10,... | collective-permute-start | bytes 196616 | tf_op jit(solution)/shard_map/ppermute | solution.py:323
  50.2 1.7 %collective-permute-start.18 = (f32[64,256]{1,0:T(8,128)S(1)}, f32[64,256]{1,0:T(8,128)S(1)}, u32[]{:S(2)}, u32[]{:S(2)}) collective-permute-start(f32[64,256]{1,0:T(8,128)S(1)} %add.101), channel_id=1, source_target_pairs={{0,2},{1,3},{2,0},{3,1},{4,6},{5,7},{6,4},{7,5},{8,10},{9,11},{10,... | collective-permute-start | bytes 196616 | tf_op jit(solution)/shard_map/ppermute | solution.py:323
  51.9 2.3 %collective-permute-done.15 = f32[64,256]{1,0:T(8,128)S(1)} collective-permute-done((f32[64,256]{1,0:T(8,128)S(1)}, f32[64,256]{1,0:T(8,128)S(1)}, u32[]{:S(2)}, u32[]{:S(2)}) %collective-permute-start.15) | collective-permute-done | bytes 65568 | tf_op jit(solution)/shard_map/ppermute | solution.py:323
  54.2 2.1 %collective-permute-start.16 = (f32[64,256]{1,0:T(8,128)S(1)}, f32[64,256]{1,0:T(8,128)S(1)}, u32[]{:S(2)}, u32[]{:S(2)}) collective-permute-start(f32[64,256]{1,0:T(8,128)S(1)} %add.100.rest_0_), channel_id=1, source_target_pairs={{0,1},{1,0},{2,3},{3,2},{4,5},{5,4},{6,7},{7,6},{8,9},{9,8},{10,11... | collective-permute-start | bytes 196616 | tf_op jit(solution)/shard_map/ppermute | solution.py:323
  58.6 2.7 %collective-permute-done.19.rest_3_ = f32[64,256]{1,0:T(8,128)S(1)} collective-permute-done((f32[64,256]{1,0:T(8,128)S(1)}, f32[64,256]{1,0:T(8,128)S(1)}, u32[]{:S(2)}, u32[]{:S(2)}) %collective-permute-start.19) | collective-permute-done | bytes 65568 | tf_op jit(solution)/shard_map/ppermute | solution.py:323
  65.8 2.4 %collective-permute-done.21 = f32[16,1152]{1,0:T(8,128)S(1)} collective-permute-done((f32[16,1152]{1,0:T(8,128)S(1)}, f32[16,1152]{1,0:T(8,128)S(1)}, u32[]{:S(2)}, u32[]{:S(2)}) %collective-permute-start.21) | collective-permute-done | bytes 73760 | tf_op jit(solution)/shard_map/ppermute | solution.py:323
  70.4 2.2 %collective-permute-done.22 = f32[16,1152]{1,0:T(8,128)S(1)} collective-permute-done((f32[16,1152]{1,0:T(8,128)S(1)}, f32[16,1152]{1,0:T(8,128)S(1)}, u32[]{:S(2)}, u32[]{:S(2)}) %collective-permute-start.22) | collective-permute-done | bytes 73760 | tf_op jit(solution)/shard_map/ppermute | solution.py:323
  75.5 1.6 %shard_map.45 = (f32[64,64]{1,0:T(8,128)S(1)}, f32[1,64]{1,0:T(1,128)S(1)}) custom-call(s32[1]{0:T(128)} %bitcast.1.core_ref, f32[16,1152]{1,0:T(8,128)S(1)} %add.105.mine_ref, f32[16,1152]{1,0:T(8,128)S(1)} %collective-permute-done.23.theirs_ref, f32[16,1152]{1,0:T(8,128)S(1)} %add.108.mine_late_ref, f32[16,1152]{1,0:T(8,128)S(1)} %collective-permute-done.27.theirs_late_ref), custom_call_target="tpu_custom_call" | custom-call | flops 201326592 | bytes 16640 | tf_op jit(solution)/shard_map/pallas_call | solution.py:31
  80.1 2.8 %collective-permute-done.28 = f32[32,512]{1,0:T(8,128)S(1)} collective-permute-done((f32[32,512]{1,0:T(8,128)S(1)}, f32[32,512]{1,0:T(8,128)S(1)}, u32[]{:S(2)}, u32[]{:S(2)}) %collective-permute-start.28) | collective-permute-done | bytes 65568 | tf_op jit(solution)/shard_map/ppermute | solution.py:323
  82.9 2.7 %collective-permute-start.29 = (f32[32,512]{1,0:T(8,128)S(1)}, f32[32,512]{1,0:T(8,128)S(1)}, u32[]{:S(2)}, u32[]{:S(2)}) collective-permute-start(f32[32,512]{1,0:T(8,128)S(1)} %add.109), channel_id=1, source_target_pairs={{0,2},{1,3},{2,0},{3,1},{4,6},{5,7},{6,4},{7,5},{8,10},{9,11},{10,... | collective-permute-start | bytes 196616 | tf_op jit(solution)/shard_map/ppermute | solution.py:323
  86.7 3.5 %collective-permute-done.29 = f32[32,512]{1,0:T(8,128)S(1)} collective-permute-done((f32[32,512]{1,0:T(8,128)S(1)}, f32[32,512]{1,0:T(8,128)S(1)}, u32[]{:S(2)}, u32[]{:S(2)}) %collective-permute-start.29) | collective-permute-done | bytes 65568 | tf_op jit(solution)/shard_map/ppermute | solution.py:323
  92.4 2.1 %collective-permute-done.30.theirs_ref = f32[32,512]{1,0:T(8,128)S(1)} collective-permute-done((f32[32,512]{1,0:T(8,128)S(1)}, f32[32,512]{1,0:T(8,128)S(1)}, u32[]{:S(2)}, u32[]{:S(2)}) %collective-permute-start.30) | collective-permute-done | bytes 65568 | tf_op jit(solution)/shard_map/ppermute | solution.py:323
  99.7 2.0 %collective-permute-done.32 = f32[16,1152]{1,0:T(8,128)S(1)} collective-permute-done((f32[16,1152]{1,0:T(8,128)S(1)}, f32[16,1152]{1,0:T(8,128)S(1)}, u32[]{:S(2)}, u32[]{:S(2)}) %collective-permute-start.32) | collective-permute-done | bytes 73760 | tf_op jit(solution)/shard_map/ppermute | solution.py:323
  104.2 1.9 %collective-permute-done.33 = f32[16,1152]{1,0:T(8,128)S(1)} collective-permute-done((f32[16,1152]{1,0:T(8,128)S(1)}, f32[16,1152]{1,0:T(8,128)S(1)}, u32[]{:S(2)}, u32[]{:S(2)}) %collective-permute-start.33) | collective-permute-done | bytes 73760 | tf_op jit(solution)/shard_map/ppermute | solution.py:323
  110.9 2.4 %collective-permute-done.35 = f32[32,512]{1,0:T(8,128)S(1)} collective-permute-done((f32[32,512]{1,0:T(8,128)S(1)}, f32[32,512]{1,0:T(8,128)S(1)}, u32[]{:S(2)}, u32[]{:S(2)}) %collective-permute-start.35) | collective-permute-done | bytes 65568 | tf_op jit(solution)/shard_map/ppermute | solution.py:323
  113.3 1.6 %collective-permute-start.36 = (f32[32,512]{1,0:T(8,128)S(1)}, f32[32,512]{1,0:T(8,128)S(1)}, u32[]{:S(2)}, u32[]{:S(2)}) collective-permute-start(f32[32,512]{1,0:T(8,128)S(1)} %add.114), channel_id=1, source_target_pairs={{0,2},{1,3},{2,0},{3,1},{4,6},{5,7},{6,4},{7,5},{8,10},{9,11},{10,... | collective-permute-start | bytes 196616 | tf_op jit(solution)/shard_map/ppermute | solution.py:323
  114.9 1.7 %collective-permute-start.45 = (f32[32,512]{1,0:T(8,128)S(1)}, f32[32,512]{1,0:T(8,128)S(1)}, u32[]{:S(2)}, u32[]{:S(2)}) collective-permute-start(f32[32,512]{1,0:T(8,128)S(1)} %add.121), channel_id=1, source_target_pairs={{0,2},{1,3},{2,0},{3,1},{4,6},{5,7},{6,4},{7,5},{8,10},{9,11},{10,... | collective-permute-start | bytes 196616 | tf_op jit(solution)/shard_map/ppermute | solution.py:323
  116.6 1.6 %shard_map.51 = (f32[64,64]{1,0:T(8,128)S(1)}, f32[1,64]{1,0:T(1,128)S(1)}) custom-call(s32[1]{0:T(128)} %bitcast.1.core_ref, f32[16,1152]{1,0:T(8,128)S(1)} %add.113.mine_ref, f32[16,1152]{1,0:T(8,128)S(1)} %collective-permute-done.34.theirs_ref, f32[16,1152]{1,0:T(8,128)S(1)} %add.120.mine_ref.mine_late_ref, ...), custom_call_target="tpu_custom_call" | custom-call | flops 201326592 | bytes 16640 | tf_op jit(solution)/shard_map/pallas_call | solution.py:31
  118.2 2.0 %collective-permute-done.36 = f32[32,512]{1,0:T(8,128)S(1)} collective-permute-done((f32[32,512]{1,0:T(8,128)S(1)}, f32[32,512]{1,0:T(8,128)S(1)}, u32[]{:S(2)}, u32[]{:S(2)}) %collective-permute-start.36) | collective-permute-done | bytes 65568 | tf_op jit(solution)/shard_map/ppermute | solution.py:323
  122.6 1.8 %collective-permute-start.47 = (f32[32,128]{1,0:T(8,128)S(1)}, f32[32,128]{1,0:T(8,128)S(1)}, u32[]{:S(2)}, u32[]{:S(2)}) collective-permute-start(f32[32,128]{1,0:T(8,128)S(1)} %get-tuple-element.77), channel_id=1, source_target_pairs={{0,4},{1,5},{2,6},{3,7},{4,0},{5,1},{6,2},{7,3},{8,12},{9,13},{10,... | collective-permute-start | bytes 49160 | tf_op jit(solution)/shard_map/ppermute | solution.py:329
  124.4 1.6 %collective-permute-done.48 = f32[32,128]{1,0:T(8,128)S(1)} collective-permute-done((f32[32,128]{1,0:T(8,128)S(1)}, f32[32,128]{1,0:T(8,128)S(1)}, u32[]{:S(2)}, u32[]{:S(2)}) %collective-permute-start.48) | collective-permute-done | bytes 16416 | tf_op jit(solution)/shard_map/ppermute | solution.py:329
  132.4 2.2 %collective-permute-done.46.theirs_ref = f32[64,512]{1,0:T(8,128)S(1)} collective-permute-done((f32[64,512]{1,0:T(8,128)S(1)}, f32[64,512]{1,0:T(8,128)S(1)}, u32[]{:S(2)}, u32[]{:S(2)}) %collective-permute-start.46) | collective-permute-done | bytes 131104 | tf_op jit(solution)/shard_map/ppermute | solution.py:323
  134.6 2.6 %shard_map.53 = (f32[64,1024]{1,0:T(8,128)}, f32[3,64]{1,0:T(4,128)}) custom-call(s32[1]{0:T(128)} %bitcast.par_ref, f32[64,512]{1,0:T(8,128)S(1)} %get-tuple-element.76.mine_ref, f32[64,512]{1,0:T(8,128)S(1)} %collective-permute-done.46.theirs_ref, f32[32,128]{1,0:T(8,128)S(1)} %add_add_fusion.gram_ref, f32[1,64]{1,0:T(1,128)S(1)} %get-tuple-element.78.rest_0_, ...), custom_call_target="tpu_custom_call" | custom-call | flops 402653184 | bytes 262912 | tf_op jit(solution)/shard_map/pallas_call | solution.py:31
  (115 shorter events, 47.9 us)
Async XLA Ops:
  3.8 40.5 %all-to-all-start = ((bf16[8,128,512]{2,1,0:T(8,128)(2,1)}), bf16[8,128,512]{2,1,0:T(8,128)(2,1)S(1)}, u32[]{:S(2)}, u32[]{:S(2)}) async-start(bf16[8,128,512]{2,1,0:T(8,128)(2,1)} %get-tuple-element.53), calls=%async_computation | async-start | bytes 2097152 | tf_op jit(solution)/shard_map/all_to_all | solution.py:386
  9.0 21.7 %collective-permute-start.7 = (bf16[128,512]{1,0:T(8,128)(2,1)S(1)}, bf16[128,512]{1,0:T(8,128)(2,1)S(1)}, u32[]{:S(2)}, u32[]{:S(2)}) collective-permute-start(bf16[128,512]{1,0:T(8,128)(2,1)S(1)} %get-tuple-element.44), channel_id=1, source_target_pairs={{0,4},{4,0},{8,12},{12,8},{16,20},{20,16},{24,28},{28,24},{1,5},{5... | collective-permute-start | bytes 393224 | tf_op jit(solution)/shard_map/ppermute | solution.py:323
  9.5 23.4 %collective-permute-start.8 = (bf16[128,512]{1,0:T(8,128)(2,1)S(1)}, bf16[128,512]{1,0:T(8,128)(2,1)S(1)}, u32[]{:S(2)}, u32[]{:S(2)}) collective-permute-start(bf16[128,512]{1,0:T(8,128)(2,1)S(1)} %get-tuple-element.45), channel_id=1, source_target_pairs={{0,8},{4,12},{8,0},{12,4},{16,24},{20,28},{24,16},{28,20},{1,9},{5... | collective-permute-start | bytes 393224 | tf_op jit(solution)/shard_map/ppermute | solution.py:323
  11.2 16.1 %collective-permute-start.1 = (f32[64,128]{1,0:T(8,128)S(1)}, f32[64,128]{1,0:T(8,128)S(1)}, u32[]{:S(2)}, u32[]{:S(2)}) collective-permute-start(f32[64,128]{1,0:T(8,128)S(1)} %get-tuple-element.42.rest_0_), channel_id=1, source_target_pairs={{0,8},{4,12},{8,0},{12,4},{16,24},{20,28},{24,16},{28,20},{1,9},{5... | collective-permute-start | bytes 98312 | tf_op jit(solution)/shard_map/ppermute | solution.py:323
  11.5 15.8 %collective-permute-start.3 = (f32[64,128]{1,0:T(8,128)S(1)}, f32[64,128]{1,0:T(8,128)S(1)}, u32[]{:S(2)}, u32[]{:S(2)}) collective-permute-start(f32[64,128]{1,0:T(8,128)S(1)} %get-tuple-element.42.rest_0_), channel_id=1, source_target_pairs={{0,16},{4,20},{8,24},{12,28},{16,0},{20,4},{24,8},{28,12},{1,17},{... | collective-permute-start | bytes 98312 | tf_op jit(solution)/shard_map/ppermute | solution.py:323
  13.3 15.3 %collective-permute-start.5 = (f32[64,128]{1,0:T(8,128)S(1)}, f32[64,128]{1,0:T(8,128)S(1)}, u32[]{:S(2)}, u32[]{:S(2)}) collective-permute-start(f32[64,128]{1,0:T(8,128)S(1)} %get-tuple-element.42.rest_0_), channel_id=1, source_target_pairs={{0,24},{4,28},{8,16},{12,20},{16,8},{20,12},{24,0},{28,4},{1,25},{... | collective-permute-start | bytes 98312 | tf_op jit(solution)/shard_map/ppermute | solution.py:323
  28.6 5.1 %collective-permute-start.9 = (bf16[128,512]{1,0:T(8,128)(2,1)S(1)}, bf16[128,512]{1,0:T(8,128)(2,1)S(1)}, u32[]{:S(2)}, u32[]{:S(2)}) collective-permute-start(bf16[128,512]{1,0:T(8,128)(2,1)S(1)} %get-tuple-element.46), channel_id=1, source_target_pairs={{0,12},{4,8},{8,4},{12,0},{16,28},{20,24},{24,20},{28,16},{1,13},{... | collective-permute-start | bytes 393224 | tf_op jit(solution)/shard_map/ppermute | solution.py:323
  29.3 12.0 %collective-permute-start.10 = (bf16[128,512]{1,0:T(8,128)(2,1)S(1)}, bf16[128,512]{1,0:T(8,128)(2,1)S(1)}, u32[]{:S(2)}, u32[]{:S(2)}) collective-permute-start(bf16[128,512]{1,0:T(8,128)(2,1)S(1)} %get-tuple-element.47), channel_id=1, source_target_pairs={{0,16},{4,20},{8,24},{12,28},{16,0},{20,4},{24,8},{28,12},{1,17},{... | collective-permute-start | bytes 393224 | tf_op jit(solution)/shard_map/ppermute | solution.py:323
  30.4 11.8 %collective-permute-start.11 = (bf16[128,512]{1,0:T(8,128)(2,1)S(1)}, bf16[128,512]{1,0:T(8,128)(2,1)S(1)}, u32[]{:S(2)}, u32[]{:S(2)}) collective-permute-start(bf16[128,512]{1,0:T(8,128)(2,1)S(1)} %get-tuple-element.48), channel_id=1, source_target_pairs={{0,20},{4,16},{8,28},{12,24},{16,4},{20,0},{24,12},{28,8},{1,21},{... | collective-permute-start | bytes 393224 | tf_op jit(solution)/shard_map/ppermute | solution.py:323
  30.7 11.5 %collective-permute-start.12 = (bf16[128,512]{1,0:T(8,128)(2,1)S(1)}, bf16[128,512]{1,0:T(8,128)(2,1)S(1)}, u32[]{:S(2)}, u32[]{:S(2)}) collective-permute-start(bf16[128,512]{1,0:T(8,128)(2,1)S(1)} %get-tuple-element.49), channel_id=1, source_target_pairs={{0,24},{4,28},{8,16},{12,20},{16,8},{20,12},{24,0},{28,4},{1,25},{... | collective-permute-start | bytes 393224 | tf_op jit(solution)/shard_map/ppermute | solution.py:323
  32.9 9.2 %collective-permute-start.13 = (bf16[128,512]{1,0:T(8,128)(2,1)S(1)}, bf16[128,512]{1,0:T(8,128)(2,1)S(1)}, u32[]{:S(2)}, u32[]{:S(2)}) collective-permute-start(bf16[128,512]{1,0:T(8,128)(2,1)S(1)} %get-tuple-element.50), channel_id=1, source_target_pairs={{0,28},{4,24},{8,20},{12,16},{16,12},{20,8},{24,4},{28,0},{1,29},{... | collective-permute-start | bytes 393224 | tf_op jit(solution)/shard_map/ppermute | solution.py:323
  42.6 4.9 %collective-permute-start.14 = (f32[64,256]{1,0:T(8,128)S(1)}, f32[64,256]{1,0:T(8,128)S(1)}, u32[]{:S(2)}, u32[]{:S(2)}) collective-permute-start(f32[64,256]{1,0:T(8,128)S(1)} %get-tuple-element.52), channel_id=1, source_target_pairs={{0,1},{1,0},{2,3},{3,2},{4,5},{5,4},{6,7},{7,6},{8,9},{9,8},{10,11... | collective-permute-start | bytes 196616 | tf_op jit(solution)/shard_map/ppermute | solution.py:323
  44.7 5.5 %collective-permute-start.17 = (f32[64,256]{1,0:T(8,128)S(1)}, f32[64,256]{1,0:T(8,128)S(1)}, u32[]{:S(2)}, u32[]{:S(2)}) collective-permute-start(f32[64,256]{1,0:T(8,128)S(1)} %get-tuple-element.55), channel_id=1, source_target_pairs={{0,1},{1,0},{2,3},{3,2},{4,5},{5,4},{6,7},{7,6},{8,9},{9,8},{10,11... | collective-permute-start | bytes 196616 | tf_op jit(solution)/shard_map/ppermute | solution.py:323
  47.5 6.7 %collective-permute-start.15 = (f32[64,256]{1,0:T(8,128)S(1)}, f32[64,256]{1,0:T(8,128)S(1)}, u32[]{:S(2)}, u32[]{:S(2)}) collective-permute-start(f32[64,256]{1,0:T(8,128)S(1)} %add.99), channel_id=1, source_target_pairs={{0,2},{1,3},{2,0},{3,1},{4,6},{5,7},{6,4},{7,5},{8,10},{9,11},{10,... | collective-permute-start | bytes 196616 | tf_op jit(solution)/shard_map/ppermute | solution.py:323
  50.2 6.8 %collective-permute-start.18 = (f32[64,256]{1,0:T(8,128)S(1)}, f32[64,256]{1,0:T(8,128)S(1)}, u32[]{:S(2)}, u32[]{:S(2)}) collective-permute-start(f32[64,256]{1,0:T(8,128)S(1)} %add.101), channel_id=1, source_target_pairs={{0,2},{1,3},{2,0},{3,1},{4,6},{5,7},{6,4},{7,5},{8,10},{9,11},{10,... | collective-permute-start | bytes 196616 | tf_op jit(solution)/shard_map/ppermute | solution.py:323
  54.2 4.4 %collective-permute-start.16 = (f32[64,256]{1,0:T(8,128)S(1)}, f32[64,256]{1,0:T(8,128)S(1)}, u32[]{:S(2)}, u32[]{:S(2)}) collective-permute-start(f32[64,256]{1,0:T(8,128)S(1)} %add.100.rest_0_), channel_id=1, source_target_pairs={{0,1},{1,0},{2,3},{3,2},{4,5},{5,4},{6,7},{7,6},{8,9},{9,8},{10,11... | collective-permute-start | bytes 196616 | tf_op jit(solution)/shard_map/ppermute | solution.py:323
  63.8 4.4 %collective-permute-start.21 = (f32[16,1152]{1,0:T(8,128)S(1)}, f32[16,1152]{1,0:T(8,128)S(1)}, u32[]{:S(2)}, u32[]{:S(2)}) collective-permute-start(f32[16,1152]{1,0:T(8,128)S(1)} %add.103), channel_id=1, source_target_pairs={{0,8},{4,12},{8,0},{12,4},{16,24},{20,28},{24,16},{28,20},{1,9},{5... | collective-permute-start | bytes 221192 | tf_op jit(solution)/shard_map/ppermute | solution.py:323
  65.3 4.4 %collective-permute-start.25 = (f32[16,1152]{1,0:T(8,128)S(1)}, f32[16,1152]{1,0:T(8,128)S(1)}, u32[]{:S(2)}, u32[]{:S(2)}) collective-permute-start(f32[16,1152]{1,0:T(8,128)S(1)} %add.106), channel_id=1, source_target_pairs={{0,16},{4,20},{8,24},{12,28},{16,0},{20,4},{24,8},{28,12},{1,17},{... | collective-permute-start | bytes 221192 | tf_op jit(solution)/shard_map/ppermute | solution.py:323
  68.2 4.4 %collective-permute-start.22 = (f32[16,1152]{1,0:T(8,128)S(1)}, f32[16,1152]{1,0:T(8,128)S(1)}, u32[]{:S(2)}, u32[]{:S(2)}) collective-permute-start(f32[16,1152]{1,0:T(8,128)S(1)} %add.104), channel_id=1, source_target_pairs={{0,16},{4,20},{8,24},{12,28},{16,0},{20,4},{24,8},{28,12},{1,17},{... | collective-permute-start | bytes 221192 | tf_op jit(solution)/shard_map/ppermute | solution.py:323
  78.0 4.9 %collective-permute-start.28 = (f32[32,512]{1,0:T(8,128)S(1)}, f32[32,512]{1,0:T(8,128)S(1)}, u32[]{:S(2)}, u32[]{:S(2)}) collective-permute-start(f32[32,512]{1,0:T(8,128)S(1)} %get-tuple-element.63), channel_id=1, source_target_pairs={{0,1},{1,0},{2,3},{3,2},{4,5},{5,4},{6,7},{7,6},{8,9},{9,8},{10,11... | collective-permute-start | bytes 196616 | tf_op jit(solution)/shard_map/ppermute | solution.py:323
  78.5 7.1 %collective-permute-start.37 = (f32[32,512]{1,0:T(8,128)S(1)}, f32[32,512]{1,0:T(8,128)S(1)}, u32[]{:S(2)}, u32[]{:S(2)}) collective-permute-start(f32[32,512]{1,0:T(8,128)S(1)} %get-tuple-element.69), channel_id=1, source_target_pairs={{0,1},{1,0},{2,3},{3,2},{4,5},{5,4},{6,7},{7,6},{8,9},{9,8},{10,11... | collective-permute-start | bytes 196616 | tf_op jit(solution)/shard_map/ppermute | solution.py:323
  82.9 7.2 %collective-permute-start.29 = (f32[32,512]{1,0:T(8,128)S(1)}, f32[32,512]{1,0:T(8,128)S(1)}, u32[]{:S(2)}, u32[]{:S(2)}) collective-permute-start(f32[32,512]{1,0:T(8,128)S(1)} %add.109), channel_id=1, source_target_pairs={{0,2},{1,3},{2,0},{3,1},{4,6},{5,7},{6,4},{7,5},{8,10},{9,11},{10,... | collective-permute-start | bytes 196616 | tf_op jit(solution)/shard_map/ppermute | solution.py:323
  85.6 5.3 %collective-permute-start.38 = (f32[32,512]{1,0:T(8,128)S(1)}, f32[32,512]{1,0:T(8,128)S(1)}, u32[]{:S(2)}, u32[]{:S(2)}) collective-permute-start(f32[32,512]{1,0:T(8,128)S(1)} %add.116), channel_id=1, source_target_pairs={{0,2},{1,3},{2,0},{3,1},{4,6},{5,7},{6,4},{7,5},{8,10},{9,11},{10,... | collective-permute-start | bytes 196616 | tf_op jit(solution)/shard_map/ppermute | solution.py:323
  90.9 4.7 %collective-permute-start.39 = (f32[32,512]{1,0:T(8,128)S(1)}, f32[32,512]{1,0:T(8,128)S(1)}, u32[]{:S(2)}, u32[]{:S(2)}) collective-permute-start(f32[32,512]{1,0:T(8,128)S(1)} %add.117.mine_ref), channel_id=1, source_target_pairs={{0,1},{1,0},{2,3},{3,2},{4,5},{5,4},{6,7},{7,6},{8,9},{9,8},{10,11... | collective-permute-start | bytes 196616 | tf_op jit(solution)/shard_map/ppermute | solution.py:323
  98.5 4.7 %collective-permute-start.41 = (f32[16,1152]{1,0:T(8,128)S(1)}, f32[16,1152]{1,0:T(8,128)S(1)}, u32[]{:S(2)}, u32[]{:S(2)}) collective-permute-start(f32[16,1152]{1,0:T(8,128)S(1)} %add.118), channel_id=1, source_target_pairs={{0,16},{4,20},{8,24},{12,28},{16,0},{20,4},{24,8},{28,12},{1,17},{... | collective-permute-start | bytes 221192 | tf_op jit(solution)/shard_map/ppermute | solution.py:323
  108.2 5.0 %collective-permute-start.35 = (f32[32,512]{1,0:T(8,128)S(1)}, f32[32,512]{1,0:T(8,128)S(1)}, u32[]{:S(2)}, u32[]{:S(2)}) collective-permute-start(f32[32,512]{1,0:T(8,128)S(1)} %get-tuple-element.67), channel_id=1, source_target_pairs={{0,1},{1,0},{2,3},{3,2},{4,5},{5,4},{6,7},{7,6},{8,9},{9,8},{10,11... | collective-permute-start | bytes 196616 | tf_op jit(solution)/shard_map/ppermute | solution.py:323
  109.5 5.4 %collective-permute-start.44 = (f32[32,512]{1,0:T(8,128)S(1)}, f32[32,512]{1,0:T(8,128)S(1)}, u32[]{:S(2)}, u32[]{:S(2)}) collective-permute-start(f32[32,512]{1,0:T(8,128)S(1)} %get-tuple-element.74), channel_id=1, source_target_pairs={{0,1},{1,0},{2,3},{3,2},{4,5},{5,4},{6,7},{7,6},{8,9},{9,8},{10,11... | collective-permute-start | bytes 196616 | tf_op jit(solution)/shard_map/ppermute | solution.py:323
  113.3 6.9 %collective-permute-start.36 = (f32[32,512]{1,0:T(8,128)S(1)}, f32[32,512]{1,0:T(8,128)S(1)}, u32[]{:S(2)}, u32[]{:S(2)}) collective-permute-start(f32[32,512]{1,0:T(8,128)S(1)} %add.114), channel_id=1, source_target_pairs={{0,2},{1,3},{2,0},{3,1},{4,6},{5,7},{6,4},{7,5},{8,10},{9,11},{10,... | collective-permute-start | bytes 196616 | tf_op jit(solution)/shard_map/ppermute | solution.py:323
  114.9 6.7 %collective-permute-start.45 = (f32[32,512]{1,0:T(8,128)S(1)}, f32[32,512]{1,0:T(8,128)S(1)}, u32[]{:S(2)}, u32[]{:S(2)}) collective-permute-start(f32[32,512]{1,0:T(8,128)S(1)} %add.121), channel_id=1, source_target_pairs={{0,2},{1,3},{2,0},{3,1},{4,6},{5,7},{6,4},{7,5},{8,10},{9,11},{10,... | collective-permute-start | bytes 196616 | tf_op jit(solution)/shard_map/ppermute | solution.py:323
  126.0 5.0 %collective-permute-start.51 = (f32[32,128]{1,0:T(8,128)S(1)}, f32[32,128]{1,0:T(8,128)S(1)}, u32[]{:S(2)}, u32[]{:S(2)}) collective-permute-start(f32[32,128]{1,0:T(8,128)S(1)} %add_add_fusion.1), channel_id=1, source_target_pairs={{0,16},{4,20},{8,24},{12,28},{16,0},{20,4},{24,8},{28,12},{1,17},{... | collective-permute-start | bytes 49160 | tf_op jit(solution)/shard_map/ppermute | solution.py:323
  127.2 4.6 %collective-permute-start.52 = (f32[32,128]{1,0:T(8,128)S(1)}, f32[32,128]{1,0:T(8,128)S(1)}, u32[]{:S(2)}, u32[]{:S(2)}) collective-permute-start(f32[32,128]{1,0:T(8,128)S(1)} %add_add_fusion.1), channel_id=1, source_target_pairs={{0,24},{4,28},{8,16},{12,20},{16,8},{20,12},{24,0},{28,4},{1,25},{... | collective-permute-start | bytes 49160 | tf_op jit(solution)/shard_map/ppermute | solution.py:323
  129.6 5.0 %collective-permute-start.46 = (f32[64,512]{1,0:T(8,128)S(1)}, f32[64,512]{1,0:T(8,128)S(1)}, u32[]{:S(2)}, u32[]{:S(2)}) collective-permute-start(f32[64,512]{1,0:T(8,128)S(1)} %get-tuple-element.76.mine_ref), channel_id=1, source_target_pairs={{0,1},{1,0},{2,3},{3,2},{4,5},{5,4},{6,7},{7,6},{8,9},{9,8},{10,11... | collective-permute-start | bytes 393224 | tf_op jit(solution)/shard_map/ppermute | solution.py:323
  (22 other events, 61.4 us)
